TPU v7x, 64 devices: a 2x2x8 block of a 4x4x8 slice. The times are simulated.
64 devices in a mesh: dp: 4 (over x, y), cp: 16 (over z, core).
Axes of the slice: x: 2, y: 2, z: 8, core: 2. Of those that a mesh axis runs over, the one named last changes fastest.
The devices are a block of a 4x4x8 slice.
Arguments:
- q_raw: bfloat16 [16384, 64, 128], P(('dp', 'cp')), parts along dimension 0
- k_raw: bfloat16 [16384, 4, 128], P(('dp', 'cp')), parts along dimension 0
- v_proj: bfloat16 [16384, 4, 128], P(('dp', 'cp')), parts along dimension 0
- out_fwd: bfloat16 [16384, 64, 128], P(('dp', 'cp')), parts along dimension 0
- lse_fwd: float32 [16384, 64], P(('dp', 'cp')), parts along dimension 0
- d_out: bfloat16 [16384, 64, 128], P(('dp', 'cp')), parts along dimension 0
- q_norm: float32 [128], replicated
- k_norm: float32 [128], replicated
Outputs:
- output 1: bfloat16 [16384, 64, 128], P(('dp', 'cp')), parts along dimension 0
- output 2: bfloat16 [16384, 4, 128], P(('dp', 'cp')), parts along dimension 0
- output 3: bfloat16 [16384, 4, 128], P(('dp', 'cp')), parts along dimension 0
- output 4: float32 [512], P('dp'), parts along dimension 0
- output 5: float32 [512], P('dp'), parts along dimension 0
There are 4 independent parts. A program takes and returns all parts, laid end to end along the dimension named above; an argument that names none is the same for every part.
All inputs are finite; a program needn't handle non-finite values.
Results may differ from a plain program's by a relative error of at most 0.00281665.
Values are sent between devices in bfloat16 or wider.
A program may use at most 768 MiB of HBM per device.

v0:
```python
import jax
import jax.numpy as jnp
from jax import lax
from jax.sharding import PartitionSpec as P

HEAD_DIM = 128
ROPE_THETA = 1000000.0
NORM_EPS = 1e-6


def rope_tables(positions):
    inv_freq = ROPE_THETA ** (-jnp.arange(0, HEAD_DIM, 2).astype(jnp.float32) / HEAD_DIM)
    angles = positions.astype(jnp.float32)[:, None] * inv_freq[None, :]
    angles = jnp.concatenate([angles, angles], axis=-1)
    return jnp.cos(angles)[:, None, :], jnp.sin(angles)[:, None, :]


def norm_rope(raw_in, weight, cos_t, sin_t):
    mean_sq = jnp.mean(raw_in * raw_in, axis=-1, keepdims=True)
    normed = raw_in * lax.rsqrt(mean_sq + NORM_EPS) * weight
    half_dim = raw_in.shape[-1] // 2
    rotated = jnp.concatenate([-normed[..., half_dim:], normed[..., :half_dim]], axis=-1)
    return normed * cos_t + rotated * sin_t


def pair_grads(q_blk, do_blk, lse_blk, delta_blk, k_blk, v_blk, visible):
    sm_scale = HEAD_DIM ** -0.5
    logits = jnp.einsum('qngd,knd->qngk', q_blk, k_blk, preferred_element_type=jnp.float32) * sm_scale - lse_blk[..., None]
    if visible is not None:
        logits = jnp.where(visible[:, None, None, :], logits, -jnp.inf)
    attn_prob = jnp.exp(logits)
    attn_dprob = jnp.einsum('qngd,knd->qngk', do_blk, v_blk, preferred_element_type=jnp.float32)
    score_grad = (attn_prob * (attn_dprob - delta_blk[..., None])).astype(jnp.bfloat16)
    prob_bf = attn_prob.astype(jnp.bfloat16)
    dq_part = sm_scale * jnp.einsum('qngk,knd->qngd', score_grad, k_blk, preferred_element_type=jnp.float32)
    dk_part = sm_scale * jnp.einsum('qngk,qngd->knd', score_grad, q_blk, preferred_element_type=jnp.float32)
    dv_part = jnp.einsum('qngk,qngd->knd', prob_bf, do_blk, preferred_element_type=jnp.float32)
    return dq_part, dk_part, dv_part


def own_grads(q_b, do_b, lse_b, delta_sum, k_blk, v_blk):
    chunk_len = k_blk.shape[0] // 2
    tri_mask = jnp.arange(chunk_len)[:, None] >= jnp.arange(chunk_len)[None, :]
    dq_first, dk_first, dv_first = pair_grads(q_b[:chunk_len], do_b[:chunk_len], lse_b[:chunk_len], delta_sum[:chunk_len], k_blk[:chunk_len], v_blk[:chunk_len], tri_mask)
    dq_cross, dk_cross, dv_cross = pair_grads(q_b[chunk_len:], do_b[chunk_len:], lse_b[chunk_len:], delta_sum[chunk_len:], k_blk[:chunk_len], v_blk[:chunk_len], None)
    dq_second, dk_second, dv_second = pair_grads(q_b[chunk_len:], do_b[chunk_len:], lse_b[chunk_len:], delta_sum[chunk_len:], k_blk[chunk_len:], v_blk[chunk_len:], tri_mask)
    dq_own = jnp.concatenate([dq_first, dq_cross + dq_second])
    dk_own = jnp.concatenate([dk_first + dk_cross, dk_second])
    dv_own = jnp.concatenate([dv_first + dv_cross, dv_second])
    return dq_own, dk_own, dv_own


def early_source(q_b, do_b, lse_b, delta_sum, k_blk, v_blk, dq_acc, dk_acc, dv_acc):
    chunk_len = k_blk.shape[0] // 2
    dq_part, dk_part, dv_part = pair_grads(q_b, do_b, lse_b, delta_sum, k_blk[:chunk_len], v_blk[:chunk_len], None)
    return (dq_acc + dq_part,
            jnp.concatenate([dk_acc[:chunk_len] + dk_part, dk_acc[chunk_len:]]),
            jnp.concatenate([dv_acc[:chunk_len] + dv_part, dv_acc[chunk_len:]]))


def late_source(q_b, do_b, lse_b, delta_sum, k_blk, v_blk, dq_acc, dk_acc, dv_acc):
    chunk_len = k_blk.shape[0] // 2
    dq_part, dk_part, dv_part = pair_grads(q_b[chunk_len:], do_b[chunk_len:], lse_b[chunk_len:], delta_sum[chunk_len:], k_blk, v_blk, None)
    return (jnp.concatenate([dq_acc[:chunk_len], dq_acc[chunk_len:] + dq_part]),
            dk_acc + dk_part,
            dv_acc + dv_part)


def solution(mesh):
    cp_size = mesh.shape['cp']
    shift_pairs = [(source, (source + 1) % cp_size) for source in range(cp_size)]

    def local_grads(q_raw, k_raw, v_proj, out_fwd, lse_fwd, d_out, q_norm, k_norm):
        dev_rank = lax.axis_index('cp')
        local_rows, num_heads = q_raw.shape[0], q_raw.shape[1]
        chunk_len = local_rows // 2
        kv_heads = k_raw.shape[1]
        per_kv = num_heads // kv_heads
        offsets = jnp.arange(chunk_len)
        positions = jnp.concatenate([dev_rank * chunk_len + offsets, (2 * cp_size - 1 - dev_rank) * chunk_len + offsets])
        cos_t, sin_t = rope_tables(positions)
        prepare = lambda raw_in, weight: norm_rope(raw_in, weight, cos_t, sin_t)
        q_full, pull_q = jax.vjp(prepare, q_raw.astype(jnp.float32), q_norm)
        k_full, pull_k = jax.vjp(prepare, k_raw.astype(jnp.float32), k_norm)
        q_b = q_full.astype(jnp.bfloat16).reshape(local_rows, kv_heads, per_kv, HEAD_DIM)
        k_b = k_full.astype(jnp.bfloat16)
        do_b = d_out.reshape(local_rows, kv_heads, per_kv, HEAD_DIM)
        lse_b = lse_fwd.reshape(local_rows, kv_heads, per_kv)
        delta_sum = jnp.einsum('thd,thd->th', d_out, out_fwd, preferred_element_type=jnp.float32).reshape(local_rows, kv_heads, per_kv)
        dq_acc, dk_acc, dv_acc = own_grads(q_b, do_b, lse_b, delta_sum, k_b, v_proj)

        def visit_source(step_idx, loop_state):
            k_cur, v_cur, dq_cur, dk_cur, dv_cur = loop_state
            k_cur = lax.ppermute(k_cur, 'cp', shift_pairs)
            v_cur = lax.ppermute(v_cur, 'cp', shift_pairs)
            dk_cur = lax.ppermute(dk_cur, 'cp', shift_pairs)
            dv_cur = lax.ppermute(dv_cur, 'cp', shift_pairs)
            source = (dev_rank - step_idx) % cp_size
            dq_cur, dk_cur, dv_cur = lax.cond(source < dev_rank, early_source, late_source, q_b, do_b, lse_b, delta_sum, k_cur, v_cur, dq_cur, dk_cur, dv_cur)
            return k_cur, v_cur, dq_cur, dk_cur, dv_cur

        loop_state = lax.fori_loop(1, cp_size, visit_source, (k_b, v_proj, dq_acc, dk_acc, dv_acc))
        dq_acc, dk_cur, dv_cur = loop_state[2], loop_state[3], loop_state[4]
        dk_home = lax.ppermute(dk_cur, 'cp', shift_pairs)
        dv_home = lax.ppermute(dv_cur, 'cp', shift_pairs)
        dq_raw, dq_weight = pull_q(dq_acc.reshape(local_rows, num_heads, HEAD_DIM))
        dk_raw, dk_weight = pull_k(dk_home)
        return (dq_raw.astype(jnp.bfloat16), dk_raw.astype(jnp.bfloat16), dv_home.astype(jnp.bfloat16),
                lax.psum(dq_weight, 'cp'), lax.psum(dk_weight, 'cp'))

    row_spec = P(('dp', 'cp'))
    in_specs = (row_spec, row_spec, row_spec, row_spec, row_spec, row_spec, P(), P())
    out_specs = (row_spec, row_spec, row_spec, P('dp'), P('dp'))
    return jax.shard_map(local_grads, mesh=mesh, in_specs=in_specs, out_specs=out_specs, check_vma=False)
```

profile of v0, /device:TPU:21, one launch (start us, length us, event | category | flops | bytes accessed | tf_op | source)
XLA Modules:
  0.0 910.2 jit_solution(2773865926632010765)
XLA Ops:
  0.7 7.0 copy.28
  24.9 8.8 fusion.72
  61.6 10.8 %convolution_bitcast_fusion.2 = f32[4,128,128]{1,2,0:T(8,128)S(1)} fusion(bf16[128,4,16,128]{0,3,2,1:T(8,128)(2,1)S(1)} %fusion.81, bf16[128,4,16,128]{3,0,2,1:T(8,128)(2,1)S(1)} %bitcast.288), kind=kOutput, calls=%fused_computation.117 | convolution fusion | flops 268435456 | bytes 4456448 | tf_op jit(solution)/shard_map/qngk,qngd->knd/dot_general | solution.py:36
  102.6 8.8 copy.30
  113.0 710.6 %while.23 = (s32[]{:T(128)}, bf16[256,4,128]{2,0,1:T(8,128)(2,1)}, bf16[256,4,128]{2,0,1:T(8,128)(2,1)}, f32[256,4,16,128]{3,0,2,1:T(8,128)}, f32[256,4,128]{2,0...) while((s32[]{:T(128)}, bf16[256,4,128]{2,0,1:T(8,128)(2,1)}, ...), condition=%wide.region_5.6_spmd, body=%wide.region_2.5_spmd.sunk | while | flops 2705784832 | bytes 200868848 | solution.py:102
  118.9 12.2 %collective-permute-done.1 = bf16[256,4,128]{2,0,1:T(8,128)(2,1)S(1)} collective-permute-done((bf16[256,4,128]{2,0,1:T(8,128)(2,1)}, bf16[256,4,128]{2,0,1:T(8,128)(2,1)S(1)}, u32[]{:S(2)}, u32[]{:S(2)}) %collective-permute-start.1) | collective-permute-done | bytes 262176 | tf_op jit(solution)/shard_map/while/body/eval_jaxpr/ppermute | solution.py:95
  134.7 28.0 %conditional.2 = (f32[256,4,16,128]{3,0,2,1:T(8,128)}, f32[256,4,128]{2,0,1:T(8,128)}, f32[256,4,128]{2,0,1:T(8,128)}) conditional(s32[]{:T(128)} %convert_element_type.166, (f32[256,4,16,128]{3,0,2,1:T(8,128)}, bf16[256,4,16,128]{3,0,2,1:T(8,128)(2,1)}, bf16[256,4,128]{2,0,1:T(8,128)(2,1)S(1)}, f32[256,4,16]{0,2,1:T(8,128)}, ...), branch_computations={%region_3.3_spmd, %region_4.4_spmd} | conditional | flops 2705784832 | bytes 193528224 | solution.py:99
  143.2 6.9 fusion.41
  167.4 12.3 %collective-permute-done.1 = bf16[256,4,128]{2,0,1:T(8,128)(2,1)S(1)} collective-permute-done((bf16[256,4,128]{2,0,1:T(8,128)(2,1)}, bf16[256,4,128]{2,0,1:T(8,128)(2,1)S(1)}, u32[]{:S(2)}, u32[]{:S(2)}) %collective-permute-start.1) | collective-permute-done | bytes 262176 | tf_op jit(solution)/shard_map/while/body/eval_jaxpr/ppermute | solution.py:95
  183.2 25.6 %conditional.2 = (f32[256,4,16,128]{3,0,2,1:T(8,128)}, f32[256,4,128]{2,0,1:T(8,128)}, f32[256,4,128]{2,0,1:T(8,128)}) conditional(s32[]{:T(128)} %convert_element_type.166, (f32[256,4,16,128]{3,0,2,1:T(8,128)}, bf16[256,4,16,128]{3,0,2,1:T(8,128)(2,1)}, bf16[256,4,128]{2,0,1:T(8,128)(2,1)S(1)}, f32[256,4,16]{0,2,1:T(8,128)}, ...), branch_computations={%region_3.3_spmd, %region_4.4_spmd} | conditional | flops 2705784832 | bytes 193528224 | solution.py:99
  202.5 6.3 pad_maximum_fusion
  215.9 12.3 %collective-permute-done.1 = bf16[256,4,128]{2,0,1:T(8,128)(2,1)S(1)} collective-permute-done((bf16[256,4,128]{2,0,1:T(8,128)(2,1)}, bf16[256,4,128]{2,0,1:T(8,128)(2,1)S(1)}, u32[]{:S(2)}, u32[]{:S(2)}) %collective-permute-start.1) | collective-permute-done | bytes 262176 | tf_op jit(solution)/shard_map/while/body/eval_jaxpr/ppermute | solution.py:95
  231.7 25.6 %conditional.2 = (f32[256,4,16,128]{3,0,2,1:T(8,128)}, f32[256,4,128]{2,0,1:T(8,128)}, f32[256,4,128]{2,0,1:T(8,128)}) conditional(s32[]{:T(128)} %convert_element_type.166, (f32[256,4,16,128]{3,0,2,1:T(8,128)}, bf16[256,4,16,128]{3,0,2,1:T(8,128)(2,1)}, bf16[256,4,128]{2,0,1:T(8,128)(2,1)S(1)}, f32[256,4,16]{0,2,1:T(8,128)}, ...), branch_computations={%region_3.3_spmd, %region_4.4_spmd} | conditional | flops 2705784832 | bytes 193528224 | solution.py:99
  251.1 6.3 pad_maximum_fusion
  264.4 10.0 %collective-permute-done.1 = bf16[256,4,128]{2,0,1:T(8,128)(2,1)S(1)} collective-permute-done((bf16[256,4,128]{2,0,1:T(8,128)(2,1)}, bf16[256,4,128]{2,0,1:T(8,128)(2,1)S(1)}, u32[]{:S(2)}, u32[]{:S(2)}) %collective-permute-start.1) | collective-permute-done | bytes 262176 | tf_op jit(solution)/shard_map/while/body/eval_jaxpr/ppermute | solution.py:95
  277.9 25.6 %conditional.2 = (f32[256,4,16,128]{3,0,2,1:T(8,128)}, f32[256,4,128]{2,0,1:T(8,128)}, f32[256,4,128]{2,0,1:T(8,128)}) conditional(s32[]{:T(128)} %convert_element_type.166, (f32[256,4,16,128]{3,0,2,1:T(8,128)}, bf16[256,4,16,128]{3,0,2,1:T(8,128)(2,1)}, bf16[256,4,128]{2,0,1:T(8,128)(2,1)S(1)}, f32[256,4,16]{0,2,1:T(8,128)}, ...), branch_computations={%region_3.3_spmd, %region_4.4_spmd} | conditional | flops 2705784832 | bytes 193528224 | solution.py:99
  297.3 6.3 pad_maximum_fusion
  312.9 7.6 collective-permute-done.1
  324.1 25.6 %conditional.2 = (f32[256,4,16,128]{3,0,2,1:T(8,128)}, f32[256,4,128]{2,0,1:T(8,128)}, f32[256,4,128]{2,0,1:T(8,128)}) conditional(s32[]{:T(128)} %convert_element_type.166, (f32[256,4,16,128]{3,0,2,1:T(8,128)}, bf16[256,4,16,128]{3,0,2,1:T(8,128)(2,1)}, bf16[256,4,128]{2,0,1:T(8,128)(2,1)S(1)}, f32[256,4,16]{0,2,1:T(8,128)}, ...), branch_computations={%region_3.3_spmd, %region_4.4_spmd} | conditional | flops 2705784832 | bytes 193528224 | solution.py:99
  343.4 6.3 pad_maximum_fusion
  361.2 5.6 collective-permute-done.1
  370.3 25.6 %conditional.2 = (f32[256,4,16,128]{3,0,2,1:T(8,128)}, f32[256,4,128]{2,0,1:T(8,128)}, f32[256,4,128]{2,0,1:T(8,128)}) conditional(s32[]{:T(128)} %convert_element_type.166, (f32[256,4,16,128]{3,0,2,1:T(8,128)}, bf16[256,4,16,128]{3,0,2,1:T(8,128)(2,1)}, bf16[256,4,128]{2,0,1:T(8,128)(2,1)S(1)}, f32[256,4,16]{0,2,1:T(8,128)}, ...), branch_computations={%region_3.3_spmd, %region_4.4_spmd} | conditional | flops 2705784832 | bytes 193528224 | solution.py:99
  389.6 6.3 pad_maximum_fusion
  407.6 5.4 collective-permute-done.1
  416.5 25.6 %conditional.2 = (f32[256,4,16,128]{3,0,2,1:T(8,128)}, f32[256,4,128]{2,0,1:T(8,128)}, f32[256,4,128]{2,0,1:T(8,128)}) conditional(s32[]{:T(128)} %convert_element_type.166, (f32[256,4,16,128]{3,0,2,1:T(8,128)}, bf16[256,4,16,128]{3,0,2,1:T(8,128)(2,1)}, bf16[256,4,128]{2,0,1:T(8,128)(2,1)S(1)}, f32[256,4,16]{0,2,1:T(8,128)}, ...), branch_computations={%region_3.3_spmd, %region_4.4_spmd} | conditional | flops 2705784832 | bytes 193528224 | solution.py:99
  435.8 6.3 pad_maximum_fusion
  451.5 5.8 collective-permute-start
  462.6 25.6 %conditional.2 = (f32[256,4,16,128]{3,0,2,1:T(8,128)}, f32[256,4,128]{2,0,1:T(8,128)}, f32[256,4,128]{2,0,1:T(8,128)}) conditional(s32[]{:T(128)} %convert_element_type.166, (f32[256,4,16,128]{3,0,2,1:T(8,128)}, bf16[256,4,16,128]{3,0,2,1:T(8,128)(2,1)}, bf16[256,4,128]{2,0,1:T(8,128)(2,1)S(1)}, f32[256,4,16]{0,2,1:T(8,128)}, ...), branch_computations={%region_3.3_spmd, %region_4.4_spmd} | conditional | flops 2705784832 | bytes 193528224 | solution.py:99
  482.0 6.3 pad_maximum_fusion
  490.8 7.8 collective-permute-start.2
  501.1 5.9 collective-permute-start
  511.0 25.6 %conditional.2 = (f32[256,4,16,128]{3,0,2,1:T(8,128)}, f32[256,4,128]{2,0,1:T(8,128)}, f32[256,4,128]{2,0,1:T(8,128)}) conditional(s32[]{:T(128)} %convert_element_type.166, (f32[256,4,16,128]{3,0,2,1:T(8,128)}, bf16[256,4,16,128]{3,0,2,1:T(8,128)(2,1)}, bf16[256,4,128]{2,0,1:T(8,128)(2,1)S(1)}, f32[256,4,16]{0,2,1:T(8,128)}, ...), branch_computations={%region_3.3_spmd, %region_4.4_spmd} | conditional | flops 2705784832 | bytes 193528224 | solution.py:99
  530.4 6.3 pad_maximum_fusion
  539.2 6.8 collective-permute-start.2
  549.9 4.9 collective-permute-start
  558.9 25.6 %conditional.2 = (f32[256,4,16,128]{3,0,2,1:T(8,128)}, f32[256,4,128]{2,0,1:T(8,128)}, f32[256,4,128]{2,0,1:T(8,128)}) conditional(s32[]{:T(128)} %convert_element_type.166, (f32[256,4,16,128]{3,0,2,1:T(8,128)}, bf16[256,4,16,128]{3,0,2,1:T(8,128)(2,1)}, bf16[256,4,128]{2,0,1:T(8,128)(2,1)S(1)}, f32[256,4,16]{0,2,1:T(8,128)}, ...), branch_computations={%region_3.3_spmd, %region_4.4_spmd} | conditional | flops 2705784832 | bytes 193528224 | solution.py:99
  578.2 6.3 pad_maximum_fusion
  587.0 8.7 collective-permute-start.2
  598.2 5.9 collective-permute-start
  608.2 25.6 %conditional.2 = (f32[256,4,16,128]{3,0,2,1:T(8,128)}, f32[256,4,128]{2,0,1:T(8,128)}, f32[256,4,128]{2,0,1:T(8,128)}) conditional(s32[]{:T(128)} %convert_element_type.166, (f32[256,4,16,128]{3,0,2,1:T(8,128)}, bf16[256,4,16,128]{3,0,2,1:T(8,128)(2,1)}, bf16[256,4,128]{2,0,1:T(8,128)(2,1)S(1)}, f32[256,4,16]{0,2,1:T(8,128)}, ...), branch_computations={%region_3.3_spmd, %region_4.4_spmd} | conditional | flops 2705784832 | bytes 193528224 | solution.py:99
  627.5 6.3 pad_maximum_fusion
  636.3 6.8 collective-permute-start.2
  645.6 5.9 collective-permute-start
  655.6 25.6 %conditional.2 = (f32[256,4,16,128]{3,0,2,1:T(8,128)}, f32[256,4,128]{2,0,1:T(8,128)}, f32[256,4,128]{2,0,1:T(8,128)}) conditional(s32[]{:T(128)} %convert_element_type.166, (f32[256,4,16,128]{3,0,2,1:T(8,128)}, bf16[256,4,16,128]{3,0,2,1:T(8,128)(2,1)}, bf16[256,4,128]{2,0,1:T(8,128)(2,1)S(1)}, f32[256,4,16]{0,2,1:T(8,128)}, ...), branch_computations={%region_3.3_spmd, %region_4.4_spmd} | conditional | flops 2705784832 | bytes 193528224 | solution.py:99
  674.9 6.3 pad_maximum_fusion
  683.7 6.8 collective-permute-start.2
  693.0 5.9 collective-permute-start
  703.0 25.6 %conditional.2 = (f32[256,4,16,128]{3,0,2,1:T(8,128)}, f32[256,4,128]{2,0,1:T(8,128)}, f32[256,4,128]{2,0,1:T(8,128)}) conditional(s32[]{:T(128)} %convert_element_type.166, (f32[256,4,16,128]{3,0,2,1:T(8,128)}, bf16[256,4,16,128]{3,0,2,1:T(8,128)(2,1)}, bf16[256,4,128]{2,0,1:T(8,128)(2,1)S(1)}, f32[256,4,16]{0,2,1:T(8,128)}, ...), branch_computations={%region_3.3_spmd, %region_4.4_spmd} | conditional | flops 2705784832 | bytes 193528224 | solution.py:99
  722.3 6.3 pad_maximum_fusion
  731.1 6.8 collective-permute-start.2
  740.4 5.9 collective-permute-start
  750.4 25.6 %conditional.2 = (f32[256,4,16,128]{3,0,2,1:T(8,128)}, f32[256,4,128]{2,0,1:T(8,128)}, f32[256,4,128]{2,0,1:T(8,128)}) conditional(s32[]{:T(128)} %convert_element_type.166, (f32[256,4,16,128]{3,0,2,1:T(8,128)}, bf16[256,4,16,128]{3,0,2,1:T(8,128)(2,1)}, bf16[256,4,128]{2,0,1:T(8,128)(2,1)S(1)}, f32[256,4,16]{0,2,1:T(8,128)}, ...), branch_computations={%region_3.3_spmd, %region_4.4_spmd} | conditional | flops 2705784832 | bytes 193528224 | solution.py:99
  769.7 6.3 pad_maximum_fusion
  778.5 6.8 collective-permute-start.2
  787.8 5.9 collective-permute-start
  797.8 25.6 %conditional.2 = (f32[256,4,16,128]{3,0,2,1:T(8,128)}, f32[256,4,128]{2,0,1:T(8,128)}, f32[256,4,128]{2,0,1:T(8,128)}) conditional(s32[]{:T(128)} %convert_element_type.166, (f32[256,4,16,128]{3,0,2,1:T(8,128)}, bf16[256,4,16,128]{3,0,2,1:T(8,128)(2,1)}, bf16[256,4,128]{2,0,1:T(8,128)(2,1)S(1)}, f32[256,4,16]{0,2,1:T(8,128)}, ...), branch_computations={%region_3.3_spmd, %region_4.4_spmd} | conditional | flops 2705784832 | bytes 193528224 | solution.py:99
  817.1 6.3 pad_maximum_fusion
  827.5 6.8 collective-permute-start.4
  834.3 8.3 copy.32
  844.6 7.3 fusion.147
  851.9 7.9 fusion.74
  859.8 5.9 fusion.67
  865.8 5.8 fusion.68
  873.8 35.6 %all-reduce.4 = (f32[128]{0:T(128)}, f32[128]{0:T(128)}) all-reduce(f32[128]{0:T(128)S(1)} %get-tuple-element.409, f32[128]{0:T(128)S(1)} %get-tuple-element.411), channel_id=1, replica_groups=mesh['dp'=4,'cp'=16] {'cp'}, use_global_device_ids=true, to_apply=%region_9.10 | all-reduce | flops 256 | bytes 2048 | tf_op jit(solution)/shard_map/psum | solution.py:109
  (527 shorter events, 537.9 us)
Async XLA Ops:
  11.0 26.7 %copy-start.40 = (f32[256,4]{0,1:T(4,128)}, f32[256,4]{0,1:T(4,128)S(1)}, u32[]{:S(2)}) copy-start(f32[256,4]{0,1:T(4,128)S(1)} %fusion.141) | copy-start | bytes 12292
  16.4 21.3 %copy-start.32 = (f32[256,128]{1,0:T(8,128)}, f32[256,128]{1,0:T(8,128)S(1)}, u32[]{:S(2)}) copy-start(f32[256,128]{1,0:T(8,128)S(1)} %get-tuple-element.456) | copy-start | bytes 393220
  113.4 21.3 %collective-permute-start.3 = (f32[256,4,128]{2,0,1:T(8,128)}, f32[256,4,128]{2,0,1:T(8,128)S(1)}, u32[]{:S(2)}, u32[]{:S(2)}) collective-permute-start(f32[256,4,128]{2,0,1:T(8,128)} %get-tuple-element.577), channel_id=1, source_target_pairs={{0,1},{1,2},{2,3},{3,4},{4,5},{5,6},{6,7},{7,8},{8,9},{9,10},{10,1... | collective-permute-start | bytes 1572872 | tf_op jit(solution)/shard_map/while/body/eval_jaxpr/ppermute | solution.py:97
  116.6 18.0 %collective-permute-start.2 = (f32[256,4,128]{2,0,1:T(8,128)}, f32[256,4,128]{2,0,1:T(8,128)S(1)}, u32[]{:S(2)}, u32[]{:S(2)}) collective-permute-start(f32[256,4,128]{2,0,1:T(8,128)} %get-tuple-element.576), channel_id=1, source_target_pairs={{0,1},{1,2},{2,3},{3,4},{4,5},{5,6},{6,7},{7,8},{8,9},{9,10},{10,1... | collective-permute-start | bytes 1572872 | tf_op jit(solution)/shard_map/while/body/eval_jaxpr/ppermute | solution.py:96
  116.7 14.5 %collective-permute-start.1 = (bf16[256,4,128]{2,0,1:T(8,128)(2,1)}, bf16[256,4,128]{2,0,1:T(8,128)(2,1)S(1)}, u32[]{:S(2)}, u32[]{:S(2)}) collective-permute-start(bf16[256,4,128]{2,0,1:T(8,128)(2,1)} %get-tuple-element.574), channel_id=1, source_target_pairs={{0,1},{1,2},{2,3},{3,4},{4,5},{5,6},{6,7},{7,8},{8,9},{9,10},{10,1... | collective-permute-start | bytes 786440 | tf_op jit(solution)/shard_map/while/body/eval_jaxpr/ppermute | solution.py:95
  118.8 15.1 %collective-permute-start = (bf16[256,4,128]{2,0,1:T(8,128)(2,1)}, bf16[256,4,128]{2,0,1:T(8,128)(2,1)S(1)}, u32[]{:S(2)}, u32[]{:S(2)}) collective-permute-start(bf16[256,4,128]{2,0,1:T(8,128)(2,1)} %get-tuple-element.573), channel_id=1, source_target_pairs={{0,1},{1,2},{2,3},{3,4},{4,5},{5,6},{6,7},{7,8},{8,9},{9,10},{10,1... | collective-permute-start | bytes 786440 | tf_op jit(solution)/shard_map/while/body/eval_jaxpr/ppermute | solution.py:94
  162.6 20.5 %collective-permute-start.3 = (f32[256,4,128]{2,0,1:T(8,128)}, f32[256,4,128]{2,0,1:T(8,128)S(1)}, u32[]{:S(2)}, u32[]{:S(2)}) collective-permute-start(f32[256,4,128]{2,0,1:T(8,128)} %get-tuple-element.577), channel_id=1, source_target_pairs={{0,1},{1,2},{2,3},{3,4},{4,5},{5,6},{6,7},{7,8},{8,9},{9,10},{10,1... | collective-permute-start | bytes 1572872 | tf_op jit(solution)/shard_map/while/body/eval_jaxpr/ppermute | solution.py:97
  165.1 18.0 %collective-permute-start.2 = (f32[256,4,128]{2,0,1:T(8,128)}, f32[256,4,128]{2,0,1:T(8,128)S(1)}, u32[]{:S(2)}, u32[]{:S(2)}) collective-permute-start(f32[256,4,128]{2,0,1:T(8,128)} %get-tuple-element.576), channel_id=1, source_target_pairs={{0,1},{1,2},{2,3},{3,4},{4,5},{5,6},{6,7},{7,8},{8,9},{9,10},{10,1... | collective-permute-start | bytes 1572872 | tf_op jit(solution)/shard_map/while/body/eval_jaxpr/ppermute | solution.py:96
  165.2 14.5 %collective-permute-start.1 = (bf16[256,4,128]{2,0,1:T(8,128)(2,1)}, bf16[256,4,128]{2,0,1:T(8,128)(2,1)S(1)}, u32[]{:S(2)}, u32[]{:S(2)}) collective-permute-start(bf16[256,4,128]{2,0,1:T(8,128)(2,1)} %get-tuple-element.574), channel_id=1, source_target_pairs={{0,1},{1,2},{2,3},{3,4},{4,5},{5,6},{6,7},{7,8},{8,9},{9,10},{10,1... | collective-permute-start | bytes 786440 | tf_op jit(solution)/shard_map/while/body/eval_jaxpr/ppermute | solution.py:95
  167.4 15.1 %collective-permute-start = (bf16[256,4,128]{2,0,1:T(8,128)(2,1)}, bf16[256,4,128]{2,0,1:T(8,128)(2,1)S(1)}, u32[]{:S(2)}, u32[]{:S(2)}) collective-permute-start(bf16[256,4,128]{2,0,1:T(8,128)(2,1)} %get-tuple-element.573), channel_id=1, source_target_pairs={{0,1},{1,2},{2,3},{3,4},{4,5},{5,6},{6,7},{7,8},{8,9},{9,10},{10,1... | collective-permute-start | bytes 786440 | tf_op jit(solution)/shard_map/while/body/eval_jaxpr/ppermute | solution.py:94
  208.8 22.9 %collective-permute-start.3 = (f32[256,4,128]{2,0,1:T(8,128)}, f32[256,4,128]{2,0,1:T(8,128)S(1)}, u32[]{:S(2)}, u32[]{:S(2)}) collective-permute-start(f32[256,4,128]{2,0,1:T(8,128)} %get-tuple-element.577), channel_id=1, source_target_pairs={{0,1},{1,2},{2,3},{3,4},{4,5},{5,6},{6,7},{7,8},{8,9},{9,10},{10,1... | collective-permute-start | bytes 1572872 | tf_op jit(solution)/shard_map/while/body/eval_jaxpr/ppermute | solution.py:97
  213.7 18.0 %collective-permute-start.2 = (f32[256,4,128]{2,0,1:T(8,128)}, f32[256,4,128]{2,0,1:T(8,128)S(1)}, u32[]{:S(2)}, u32[]{:S(2)}) collective-permute-start(f32[256,4,128]{2,0,1:T(8,128)} %get-tuple-element.576), channel_id=1, source_target_pairs={{0,1},{1,2},{2,3},{3,4},{4,5},{5,6},{6,7},{7,8},{8,9},{9,10},{10,1... | collective-permute-start | bytes 1572872 | tf_op jit(solution)/shard_map/while/body/eval_jaxpr/ppermute | solution.py:96
  213.7 14.5 %collective-permute-start.1 = (bf16[256,4,128]{2,0,1:T(8,128)(2,1)}, bf16[256,4,128]{2,0,1:T(8,128)(2,1)S(1)}, u32[]{:S(2)}, u32[]{:S(2)}) collective-permute-start(bf16[256,4,128]{2,0,1:T(8,128)(2,1)} %get-tuple-element.574), channel_id=1, source_target_pairs={{0,1},{1,2},{2,3},{3,4},{4,5},{5,6},{6,7},{7,8},{8,9},{9,10},{10,1... | collective-permute-start | bytes 786440 | tf_op jit(solution)/shard_map/while/body/eval_jaxpr/ppermute | solution.py:95
  215.9 15.1 %collective-permute-start = (bf16[256,4,128]{2,0,1:T(8,128)(2,1)}, bf16[256,4,128]{2,0,1:T(8,128)(2,1)S(1)}, u32[]{:S(2)}, u32[]{:S(2)}) collective-permute-start(bf16[256,4,128]{2,0,1:T(8,128)(2,1)} %get-tuple-element.573), channel_id=1, source_target_pairs={{0,1},{1,2},{2,3},{3,4},{4,5},{5,6},{6,7},{7,8},{8,9},{9,10},{10,1... | collective-permute-start | bytes 786440 | tf_op jit(solution)/shard_map/while/body/eval_jaxpr/ppermute | solution.py:94
  257.3 20.6 %collective-permute-start.3 = (f32[256,4,128]{2,0,1:T(8,128)}, f32[256,4,128]{2,0,1:T(8,128)S(1)}, u32[]{:S(2)}, u32[]{:S(2)}) collective-permute-start(f32[256,4,128]{2,0,1:T(8,128)} %get-tuple-element.577), channel_id=1, source_target_pairs={{0,1},{1,2},{2,3},{3,4},{4,5},{5,6},{6,7},{7,8},{8,9},{9,10},{10,1... | collective-permute-start | bytes 1572872 | tf_op jit(solution)/shard_map/while/body/eval_jaxpr/ppermute | solution.py:97
  259.8 18.0 %collective-permute-start.2 = (f32[256,4,128]{2,0,1:T(8,128)}, f32[256,4,128]{2,0,1:T(8,128)S(1)}, u32[]{:S(2)}, u32[]{:S(2)}) collective-permute-start(f32[256,4,128]{2,0,1:T(8,128)} %get-tuple-element.576), channel_id=1, source_target_pairs={{0,1},{1,2},{2,3},{3,4},{4,5},{5,6},{6,7},{7,8},{8,9},{9,10},{10,1... | collective-permute-start | bytes 1572872 | tf_op jit(solution)/shard_map/while/body/eval_jaxpr/ppermute | solution.py:96
  261.9 12.5 %collective-permute-start.1 = (bf16[256,4,128]{2,0,1:T(8,128)(2,1)}, bf16[256,4,128]{2,0,1:T(8,128)(2,1)S(1)}, u32[]{:S(2)}, u32[]{:S(2)}) collective-permute-start(bf16[256,4,128]{2,0,1:T(8,128)(2,1)} %get-tuple-element.574), channel_id=1, source_target_pairs={{0,1},{1,2},{2,3},{3,4},{4,5},{5,6},{6,7},{7,8},{8,9},{9,10},{10,1... | collective-permute-start | bytes 786440 | tf_op jit(solution)/shard_map/while/body/eval_jaxpr/ppermute | solution.py:95
  264.4 12.8 %collective-permute-start = (bf16[256,4,128]{2,0,1:T(8,128)(2,1)}, bf16[256,4,128]{2,0,1:T(8,128)(2,1)S(1)}, u32[]{:S(2)}, u32[]{:S(2)}) collective-permute-start(bf16[256,4,128]{2,0,1:T(8,128)(2,1)} %get-tuple-element.573), channel_id=1, source_target_pairs={{0,1},{1,2},{2,3},{3,4},{4,5},{5,6},{6,7},{7,8},{8,9},{9,10},{10,1... | collective-permute-start | bytes 786440 | tf_op jit(solution)/shard_map/while/body/eval_jaxpr/ppermute | solution.py:94
  303.5 20.5 %collective-permute-start.3 = (f32[256,4,128]{2,0,1:T(8,128)}, f32[256,4,128]{2,0,1:T(8,128)S(1)}, u32[]{:S(2)}, u32[]{:S(2)}) collective-permute-start(f32[256,4,128]{2,0,1:T(8,128)} %get-tuple-element.577), channel_id=1, source_target_pairs={{0,1},{1,2},{2,3},{3,4},{4,5},{5,6},{6,7},{7,8},{8,9},{9,10},{10,1... | collective-permute-start | bytes 1572872 | tf_op jit(solution)/shard_map/while/body/eval_jaxpr/ppermute | solution.py:97
  306.0 18.0 %collective-permute-start.2 = (f32[256,4,128]{2,0,1:T(8,128)}, f32[256,4,128]{2,0,1:T(8,128)S(1)}, u32[]{:S(2)}, u32[]{:S(2)}) collective-permute-start(f32[256,4,128]{2,0,1:T(8,128)} %get-tuple-element.576), channel_id=1, source_target_pairs={{0,1},{1,2},{2,3},{3,4},{4,5},{5,6},{6,7},{7,8},{8,9},{9,10},{10,1... | collective-permute-start | bytes 1572872 | tf_op jit(solution)/shard_map/while/body/eval_jaxpr/ppermute | solution.py:96
  308.1 12.5 %collective-permute-start.1 = (bf16[256,4,128]{2,0,1:T(8,128)(2,1)}, bf16[256,4,128]{2,0,1:T(8,128)(2,1)S(1)}, u32[]{:S(2)}, u32[]{:S(2)}) collective-permute-start(bf16[256,4,128]{2,0,1:T(8,128)(2,1)} %get-tuple-element.574), channel_id=1, source_target_pairs={{0,1},{1,2},{2,3},{3,4},{4,5},{5,6},{6,7},{7,8},{8,9},{9,10},{10,1... | collective-permute-start | bytes 786440 | tf_op jit(solution)/shard_map/while/body/eval_jaxpr/ppermute | solution.py:95
  312.9 10.5 %collective-permute-start = (bf16[256,4,128]{2,0,1:T(8,128)(2,1)}, bf16[256,4,128]{2,0,1:T(8,128)(2,1)S(1)}, u32[]{:S(2)}, u32[]{:S(2)}) collective-permute-start(bf16[256,4,128]{2,0,1:T(8,128)(2,1)} %get-tuple-element.573), channel_id=1, source_target_pairs={{0,1},{1,2},{2,3},{3,4},{4,5},{5,6},{6,7},{7,8},{8,9},{9,10},{10,1... | collective-permute-start | bytes 786440 | tf_op jit(solution)/shard_map/while/body/eval_jaxpr/ppermute | solution.py:94
  349.7 20.6 %collective-permute-start.3 = (f32[256,4,128]{2,0,1:T(8,128)}, f32[256,4,128]{2,0,1:T(8,128)S(1)}, u32[]{:S(2)}, u32[]{:S(2)}) collective-permute-start(f32[256,4,128]{2,0,1:T(8,128)} %get-tuple-element.577), channel_id=1, source_target_pairs={{0,1},{1,2},{2,3},{3,4},{4,5},{5,6},{6,7},{7,8},{8,9},{9,10},{10,1... | collective-permute-start | bytes 1572872 | tf_op jit(solution)/shard_map/while/body/eval_jaxpr/ppermute | solution.py:97
  352.2 18.0 %collective-permute-start.2 = (f32[256,4,128]{2,0,1:T(8,128)}, f32[256,4,128]{2,0,1:T(8,128)S(1)}, u32[]{:S(2)}, u32[]{:S(2)}) collective-permute-start(f32[256,4,128]{2,0,1:T(8,128)} %get-tuple-element.576), channel_id=1, source_target_pairs={{0,1},{1,2},{2,3},{3,4},{4,5},{5,6},{6,7},{7,8},{8,9},{9,10},{10,1... | collective-permute-start | bytes 1572872 | tf_op jit(solution)/shard_map/while/body/eval_jaxpr/ppermute | solution.py:96
  356.6 10.1 %collective-permute-start.1 = (bf16[256,4,128]{2,0,1:T(8,128)(2,1)}, bf16[256,4,128]{2,0,1:T(8,128)(2,1)S(1)}, u32[]{:S(2)}, u32[]{:S(2)}) collective-permute-start(bf16[256,4,128]{2,0,1:T(8,128)(2,1)} %get-tuple-element.574), channel_id=1, source_target_pairs={{0,1},{1,2},{2,3},{3,4},{4,5},{5,6},{6,7},{7,8},{8,9},{9,10},{10,1... | collective-permute-start | bytes 786440 | tf_op jit(solution)/shard_map/while/body/eval_jaxpr/ppermute | solution.py:95
  359.1 10.5 %collective-permute-start = (bf16[256,4,128]{2,0,1:T(8,128)(2,1)}, bf16[256,4,128]{2,0,1:T(8,128)(2,1)S(1)}, u32[]{:S(2)}, u32[]{:S(2)}) collective-permute-start(bf16[256,4,128]{2,0,1:T(8,128)(2,1)} %get-tuple-element.573), channel_id=1, source_target_pairs={{0,1},{1,2},{2,3},{3,4},{4,5},{5,6},{6,7},{7,8},{8,9},{9,10},{10,1... | collective-permute-start | bytes 786440 | tf_op jit(solution)/shard_map/while/body/eval_jaxpr/ppermute | solution.py:94
  395.9 20.5 %collective-permute-start.3 = (f32[256,4,128]{2,0,1:T(8,128)}, f32[256,4,128]{2,0,1:T(8,128)S(1)}, u32[]{:S(2)}, u32[]{:S(2)}) collective-permute-start(f32[256,4,128]{2,0,1:T(8,128)} %get-tuple-element.577), channel_id=1, source_target_pairs={{0,1},{1,2},{2,3},{3,4},{4,5},{5,6},{6,7},{7,8},{8,9},{9,10},{10,1... | collective-permute-start | bytes 1572872 | tf_op jit(solution)/shard_map/while/body/eval_jaxpr/ppermute | solution.py:97
  398.4 18.0 %collective-permute-start.2 = (f32[256,4,128]{2,0,1:T(8,128)}, f32[256,4,128]{2,0,1:T(8,128)S(1)}, u32[]{:S(2)}, u32[]{:S(2)}) collective-permute-start(f32[256,4,128]{2,0,1:T(8,128)} %get-tuple-element.576), channel_id=1, source_target_pairs={{0,1},{1,2},{2,3},{3,4},{4,5},{5,6},{6,7},{7,8},{8,9},{9,10},{10,1... | collective-permute-start | bytes 1572872 | tf_op jit(solution)/shard_map/while/body/eval_jaxpr/ppermute | solution.py:96
  402.8 10.1 %collective-permute-start.1 = (bf16[256,4,128]{2,0,1:T(8,128)(2,1)}, bf16[256,4,128]{2,0,1:T(8,128)(2,1)S(1)}, u32[]{:S(2)}, u32[]{:S(2)}) collective-permute-start(bf16[256,4,128]{2,0,1:T(8,128)(2,1)} %get-tuple-element.574), channel_id=1, source_target_pairs={{0,1},{1,2},{2,3},{3,4},{4,5},{5,6},{6,7},{7,8},{8,9},{9,10},{10,1... | collective-permute-start | bytes 786440 | tf_op jit(solution)/shard_map/while/body/eval_jaxpr/ppermute | solution.py:95
  405.3 10.5 %collective-permute-start = (bf16[256,4,128]{2,0,1:T(8,128)(2,1)}, bf16[256,4,128]{2,0,1:T(8,128)(2,1)S(1)}, u32[]{:S(2)}, u32[]{:S(2)}) collective-permute-start(bf16[256,4,128]{2,0,1:T(8,128)(2,1)} %get-tuple-element.573), channel_id=1, source_target_pairs={{0,1},{1,2},{2,3},{3,4},{4,5},{5,6},{6,7},{7,8},{8,9},{9,10},{10,1... | collective-permute-start | bytes 786440 | tf_op jit(solution)/shard_map/while/body/eval_jaxpr/ppermute | solution.py:94
  442.1 20.6 %collective-permute-start.3 = (f32[256,4,128]{2,0,1:T(8,128)}, f32[256,4,128]{2,0,1:T(8,128)S(1)}, u32[]{:S(2)}, u32[]{:S(2)}) collective-permute-start(f32[256,4,128]{2,0,1:T(8,128)} %get-tuple-element.577), channel_id=1, source_target_pairs={{0,1},{1,2},{2,3},{3,4},{4,5},{5,6},{6,7},{7,8},{8,9},{9,10},{10,1... | collective-permute-start | bytes 1572872 | tf_op jit(solution)/shard_map/while/body/eval_jaxpr/ppermute | solution.py:97
  444.6 18.0 %collective-permute-start.2 = (f32[256,4,128]{2,0,1:T(8,128)}, f32[256,4,128]{2,0,1:T(8,128)S(1)}, u32[]{:S(2)}, u32[]{:S(2)}) collective-permute-start(f32[256,4,128]{2,0,1:T(8,128)} %get-tuple-element.576), channel_id=1, source_target_pairs={{0,1},{1,2},{2,3},{3,4},{4,5},{5,6},{6,7},{7,8},{8,9},{9,10},{10,1... | collective-permute-start | bytes 1572872 | tf_op jit(solution)/shard_map/while/body/eval_jaxpr/ppermute | solution.py:96
  449.0 10.1 %collective-permute-start.1 = (bf16[256,4,128]{2,0,1:T(8,128)(2,1)}, bf16[256,4,128]{2,0,1:T(8,128)(2,1)S(1)}, u32[]{:S(2)}, u32[]{:S(2)}) collective-permute-start(bf16[256,4,128]{2,0,1:T(8,128)(2,1)} %get-tuple-element.574), channel_id=1, source_target_pairs={{0,1},{1,2},{2,3},{3,4},{4,5},{5,6},{6,7},{7,8},{8,9},{9,10},{10,1... | collective-permute-start | bytes 786440 | tf_op jit(solution)/shard_map/while/body/eval_jaxpr/ppermute | solution.py:95
  451.5 10.5 %collective-permute-start = (bf16[256,4,128]{2,0,1:T(8,128)(2,1)}, bf16[256,4,128]{2,0,1:T(8,128)(2,1)S(1)}, u32[]{:S(2)}, u32[]{:S(2)}) collective-permute-start(bf16[256,4,128]{2,0,1:T(8,128)(2,1)} %get-tuple-element.573), channel_id=1, source_target_pairs={{0,1},{1,2},{2,3},{3,4},{4,5},{5,6},{6,7},{7,8},{8,9},{9,10},{10,1... | collective-permute-start | bytes 786440 | tf_op jit(solution)/shard_map/while/body/eval_jaxpr/ppermute | solution.py:94
  488.3 22.7 %collective-permute-start.3 = (f32[256,4,128]{2,0,1:T(8,128)}, f32[256,4,128]{2,0,1:T(8,128)S(1)}, u32[]{:S(2)}, u32[]{:S(2)}) collective-permute-start(f32[256,4,128]{2,0,1:T(8,128)} %get-tuple-element.577), channel_id=1, source_target_pairs={{0,1},{1,2},{2,3},{3,4},{4,5},{5,6},{6,7},{7,8},{8,9},{9,10},{10,1... | collective-permute-start | bytes 1572872 | tf_op jit(solution)/shard_map/while/body/eval_jaxpr/ppermute | solution.py:97
  490.8 20.2 %collective-permute-start.2 = (f32[256,4,128]{2,0,1:T(8,128)}, f32[256,4,128]{2,0,1:T(8,128)S(1)}, u32[]{:S(2)}, u32[]{:S(2)}) collective-permute-start(f32[256,4,128]{2,0,1:T(8,128)} %get-tuple-element.576), channel_id=1, source_target_pairs={{0,1},{1,2},{2,3},{3,4},{4,5},{5,6},{6,7},{7,8},{8,9},{9,10},{10,1... | collective-permute-start | bytes 1572872 | tf_op jit(solution)/shard_map/while/body/eval_jaxpr/ppermute | solution.py:96
  498.6 8.9 collective-permute-start.1
  501.1 9.2 %collective-permute-start = (bf16[256,4,128]{2,0,1:T(8,128)(2,1)}, bf16[256,4,128]{2,0,1:T(8,128)(2,1)S(1)}, u32[]{:S(2)}, u32[]{:S(2)}) collective-permute-start(bf16[256,4,128]{2,0,1:T(8,128)(2,1)} %get-tuple-element.573), channel_id=1, source_target_pairs={{0,1},{1,2},{2,3},{3,4},{4,5},{5,6},{6,7},{7,8},{8,9},{9,10},{10,1... | collective-permute-start | bytes 786440 | tf_op jit(solution)/shard_map/while/body/eval_jaxpr/ppermute | solution.py:94
  536.7 22.2 %collective-permute-start.3 = (f32[256,4,128]{2,0,1:T(8,128)}, f32[256,4,128]{2,0,1:T(8,128)S(1)}, u32[]{:S(2)}, u32[]{:S(2)}) collective-permute-start(f32[256,4,128]{2,0,1:T(8,128)} %get-tuple-element.577), channel_id=1, source_target_pairs={{0,1},{1,2},{2,3},{3,4},{4,5},{5,6},{6,7},{7,8},{8,9},{9,10},{10,1... | collective-permute-start | bytes 1572872 | tf_op jit(solution)/shard_map/while/body/eval_jaxpr/ppermute | solution.py:97
  539.2 19.7 %collective-permute-start.2 = (f32[256,4,128]{2,0,1:T(8,128)}, f32[256,4,128]{2,0,1:T(8,128)S(1)}, u32[]{:S(2)}, u32[]{:S(2)}) collective-permute-start(f32[256,4,128]{2,0,1:T(8,128)} %get-tuple-element.576), channel_id=1, source_target_pairs={{0,1},{1,2},{2,3},{3,4},{4,5},{5,6},{6,7},{7,8},{8,9},{9,10},{10,1... | collective-permute-start | bytes 1572872 | tf_op jit(solution)/shard_map/while/body/eval_jaxpr/ppermute | solution.py:96
  546.0 8.9 collective-permute-start.1
  549.9 8.2 collective-permute-start
  584.5 23.7 %collective-permute-start.3 = (f32[256,4,128]{2,0,1:T(8,128)}, f32[256,4,128]{2,0,1:T(8,128)S(1)}, u32[]{:S(2)}, u32[]{:S(2)}) collective-permute-start(f32[256,4,128]{2,0,1:T(8,128)} %get-tuple-element.577), channel_id=1, source_target_pairs={{0,1},{1,2},{2,3},{3,4},{4,5},{5,6},{6,7},{7,8},{8,9},{9,10},{10,1... | collective-permute-start | bytes 1572872 | tf_op jit(solution)/shard_map/while/body/eval_jaxpr/ppermute | solution.py:97
  587.0 21.2 %collective-permute-start.2 = (f32[256,4,128]{2,0,1:T(8,128)}, f32[256,4,128]{2,0,1:T(8,128)S(1)}, u32[]{:S(2)}, u32[]{:S(2)}) collective-permute-start(f32[256,4,128]{2,0,1:T(8,128)} %get-tuple-element.576), channel_id=1, source_target_pairs={{0,1},{1,2},{2,3},{3,4},{4,5},{5,6},{6,7},{7,8},{8,9},{9,10},{10,1... | collective-permute-start | bytes 1572872 | tf_op jit(solution)/shard_map/while/body/eval_jaxpr/ppermute | solution.py:96
  595.7 8.9 collective-permute-start.1
  598.2 9.2 %collective-permute-start = (bf16[256,4,128]{2,0,1:T(8,128)(2,1)}, bf16[256,4,128]{2,0,1:T(8,128)(2,1)S(1)}, u32[]{:S(2)}, u32[]{:S(2)}) collective-permute-start(bf16[256,4,128]{2,0,1:T(8,128)(2,1)} %get-tuple-element.573), channel_id=1, source_target_pairs={{0,1},{1,2},{2,3},{3,4},{4,5},{5,6},{6,7},{7,8},{8,9},{9,10},{10,1... | collective-permute-start | bytes 786440 | tf_op jit(solution)/shard_map/while/body/eval_jaxpr/ppermute | solution.py:94
  633.8 21.8 %collective-permute-start.3 = (f32[256,4,128]{2,0,1:T(8,128)}, f32[256,4,128]{2,0,1:T(8,128)S(1)}, u32[]{:S(2)}, u32[]{:S(2)}) collective-permute-start(f32[256,4,128]{2,0,1:T(8,128)} %get-tuple-element.577), channel_id=1, source_target_pairs={{0,1},{1,2},{2,3},{3,4},{4,5},{5,6},{6,7},{7,8},{8,9},{9,10},{10,1... | collective-permute-start | bytes 1572872 | tf_op jit(solution)/shard_map/while/body/eval_jaxpr/ppermute | solution.py:97
  636.3 19.3 %collective-permute-start.2 = (f32[256,4,128]{2,0,1:T(8,128)}, f32[256,4,128]{2,0,1:T(8,128)S(1)}, u32[]{:S(2)}, u32[]{:S(2)}) collective-permute-start(f32[256,4,128]{2,0,1:T(8,128)} %get-tuple-element.576), channel_id=1, source_target_pairs={{0,1},{1,2},{2,3},{3,4},{4,5},{5,6},{6,7},{7,8},{8,9},{9,10},{10,1... | collective-permute-start | bytes 1572872 | tf_op jit(solution)/shard_map/while/body/eval_jaxpr/ppermute | solution.py:96
  643.1 8.9 collective-permute-start.1
  645.6 9.2 %collective-permute-start = (bf16[256,4,128]{2,0,1:T(8,128)(2,1)}, bf16[256,4,128]{2,0,1:T(8,128)(2,1)S(1)}, u32[]{:S(2)}, u32[]{:S(2)}) collective-permute-start(bf16[256,4,128]{2,0,1:T(8,128)(2,1)} %get-tuple-element.573), channel_id=1, source_target_pairs={{0,1},{1,2},{2,3},{3,4},{4,5},{5,6},{6,7},{7,8},{8,9},{9,10},{10,1... | collective-permute-start | bytes 786440 | tf_op jit(solution)/shard_map/while/body/eval_jaxpr/ppermute | solution.py:94
  681.2 21.8 %collective-permute-start.3 = (f32[256,4,128]{2,0,1:T(8,128)}, f32[256,4,128]{2,0,1:T(8,128)S(1)}, u32[]{:S(2)}, u32[]{:S(2)}) collective-permute-start(f32[256,4,128]{2,0,1:T(8,128)} %get-tuple-element.577), channel_id=1, source_target_pairs={{0,1},{1,2},{2,3},{3,4},{4,5},{5,6},{6,7},{7,8},{8,9},{9,10},{10,1... | collective-permute-start | bytes 1572872 | tf_op jit(solution)/shard_map/while/body/eval_jaxpr/ppermute | solution.py:97
  683.7 19.3 %collective-permute-start.2 = (f32[256,4,128]{2,0,1:T(8,128)}, f32[256,4,128]{2,0,1:T(8,128)S(1)}, u32[]{:S(2)}, u32[]{:S(2)}) collective-permute-start(f32[256,4,128]{2,0,1:T(8,128)} %get-tuple-element.576), channel_id=1, source_target_pairs={{0,1},{1,2},{2,3},{3,4},{4,5},{5,6},{6,7},{7,8},{8,9},{9,10},{10,1... | collective-permute-start | bytes 1572872 | tf_op jit(solution)/shard_map/while/body/eval_jaxpr/ppermute | solution.py:96
  690.5 8.9 collective-permute-start.1
  693.0 9.2 %collective-permute-start = (bf16[256,4,128]{2,0,1:T(8,128)(2,1)}, bf16[256,4,128]{2,0,1:T(8,128)(2,1)S(1)}, u32[]{:S(2)}, u32[]{:S(2)}) collective-permute-start(bf16[256,4,128]{2,0,1:T(8,128)(2,1)} %get-tuple-element.573), channel_id=1, source_target_pairs={{0,1},{1,2},{2,3},{3,4},{4,5},{5,6},{6,7},{7,8},{8,9},{9,10},{10,1... | collective-permute-start | bytes 786440 | tf_op jit(solution)/shard_map/while/body/eval_jaxpr/ppermute | solution.py:94
  728.6 21.8 %collective-permute-start.3 = (f32[256,4,128]{2,0,1:T(8,128)}, f32[256,4,128]{2,0,1:T(8,128)S(1)}, u32[]{:S(2)}, u32[]{:S(2)}) collective-permute-start(f32[256,4,128]{2,0,1:T(8,128)} %get-tuple-element.577), channel_id=1, source_target_pairs={{0,1},{1,2},{2,3},{3,4},{4,5},{5,6},{6,7},{7,8},{8,9},{9,10},{10,1... | collective-permute-start | bytes 1572872 | tf_op jit(solution)/shard_map/while/body/eval_jaxpr/ppermute | solution.py:97
  731.1 19.3 %collective-permute-start.2 = (f32[256,4,128]{2,0,1:T(8,128)}, f32[256,4,128]{2,0,1:T(8,128)S(1)}, u32[]{:S(2)}, u32[]{:S(2)}) collective-permute-start(f32[256,4,128]{2,0,1:T(8,128)} %get-tuple-element.576), channel_id=1, source_target_pairs={{0,1},{1,2},{2,3},{3,4},{4,5},{5,6},{6,7},{7,8},{8,9},{9,10},{10,1... | collective-permute-start | bytes 1572872 | tf_op jit(solution)/shard_map/while/body/eval_jaxpr/ppermute | solution.py:96
  737.9 8.9 collective-permute-start.1
  740.4 9.2 %collective-permute-start = (bf16[256,4,128]{2,0,1:T(8,128)(2,1)}, bf16[256,4,128]{2,0,1:T(8,128)(2,1)S(1)}, u32[]{:S(2)}, u32[]{:S(2)}) collective-permute-start(bf16[256,4,128]{2,0,1:T(8,128)(2,1)} %get-tuple-element.573), channel_id=1, source_target_pairs={{0,1},{1,2},{2,3},{3,4},{4,5},{5,6},{6,7},{7,8},{8,9},{9,10},{10,1... | collective-permute-start | bytes 786440 | tf_op jit(solution)/shard_map/while/body/eval_jaxpr/ppermute | solution.py:94
  776.0 21.8 %collective-permute-start.3 = (f32[256,4,128]{2,0,1:T(8,128)}, f32[256,4,128]{2,0,1:T(8,128)S(1)}, u32[]{:S(2)}, u32[]{:S(2)}) collective-permute-start(f32[256,4,128]{2,0,1:T(8,128)} %get-tuple-element.577), channel_id=1, source_target_pairs={{0,1},{1,2},{2,3},{3,4},{4,5},{5,6},{6,7},{7,8},{8,9},{9,10},{10,1... | collective-permute-start | bytes 1572872 | tf_op jit(solution)/shard_map/while/body/eval_jaxpr/ppermute | solution.py:97
  778.5 19.3 %collective-permute-start.2 = (f32[256,4,128]{2,0,1:T(8,128)}, f32[256,4,128]{2,0,1:T(8,128)S(1)}, u32[]{:S(2)}, u32[]{:S(2)}) collective-permute-start(f32[256,4,128]{2,0,1:T(8,128)} %get-tuple-element.576), channel_id=1, source_target_pairs={{0,1},{1,2},{2,3},{3,4},{4,5},{5,6},{6,7},{7,8},{8,9},{9,10},{10,1... | collective-permute-start | bytes 1572872 | tf_op jit(solution)/shard_map/while/body/eval_jaxpr/ppermute | solution.py:96
  785.3 8.9 collective-permute-start.1
  787.8 9.2 %collective-permute-start = (bf16[256,4,128]{2,0,1:T(8,128)(2,1)}, bf16[256,4,128]{2,0,1:T(8,128)(2,1)S(1)}, u32[]{:S(2)}, u32[]{:S(2)}) collective-permute-start(bf16[256,4,128]{2,0,1:T(8,128)(2,1)} %get-tuple-element.573), channel_id=1, source_target_pairs={{0,1},{1,2},{2,3},{3,4},{4,5},{5,6},{6,7},{7,8},{8,9},{9,10},{10,1... | collective-permute-start | bytes 786440 | tf_op jit(solution)/shard_map/while/body/eval_jaxpr/ppermute | solution.py:94
  825.0 46.7 %collective-permute-start.5 = (bf16[256,4,128]{2,1,0:T(4,128)(2,1)S(1)}, bf16[256,4,128]{2,1,0:T(4,128)(2,1)S(1)}, u32[]{:S(2)}, u32[]{:S(2)}) collective-permute-start(bf16[256,4,128]{2,1,0:T(4,128)(2,1)S(1)} %copy.33), channel_id=1, source_target_pairs={{0,1},{1,2},{2,3},{3,4},{4,5},{5,6},{6,7},{7,8},{8,9},{9,10},{10,1... | collective-permute-start | bytes 786440 | tf_op jit(solution)/shard_map/ppermute | solution.py:105
  827.5 44.2 %collective-permute-start.4 = (f32[256,4,128]{2,0,1:T(8,128)}, f32[256,4,128]{2,0,1:T(8,128)S(1)}, u32[]{:S(2)}, u32[]{:S(2)}) collective-permute-start(f32[256,4,128]{2,0,1:T(8,128)} %get-tuple-element.389), channel_id=1, source_target_pairs={{0,1},{1,2},{2,3},{3,4},{4,5},{5,6},{6,7},{7,8},{8,9},{9,10},{10,1... | collective-permute-start | bytes 1572872 | tf_op jit(solution)/shard_map/ppermute | solution.py:104
  (102 other events, 574.7 us)
where the time goes:
time: 919 us; the launch traced here: 910 us
  matrix products  230 us (25%)
  starting transfers between devices  209 us (23%)
  local copies, waits for them, and re-layouts  180 us (20%)
  other arithmetic  151 us (16%)
  waiting for transfers between devices  102 us (11%)
  blocking collectives  35.6 us (4%)
    concatenate x14, other arithmetic, late_source(): jnp.concatenate([dq_acc[:chunk_len], dq_acc[chunk_len:] + dq_part])  87.8 us
    dot_general x18, matrix products, pair_grads(): jnp.einsum('qngd,knd->qngk', do_blk, v_blk, preferred_element_type=jnp.fl...  76.4 us
    ppermute x15, waiting for transfers between devices, visit_source(): v_cur = lax.ppermute(v_cur, 'cp', shift_pairs)  70.1 us
    ppermute x15, starting transfers between devices, visit_source(): dk_cur = lax.ppermute(dk_cur, 'cp', shift_pairs)  68 us
    slice x14, local copies, waits for them, and re-layouts, late_source(): dq_acc[:chunk_len]  68 us
    ppermute x15, starting transfers between devices, visit_source(): k_cur = lax.ppermute(k_cur, 'cp', shift_pairs)  50.8 us
    dot_general x18, matrix products, pair_grads(): jnp.einsum('qngk,qngd->knd', score_grad, q_blk, preferred_element_type=jn...  44.9 us
    dot_general x18, matrix products, pair_grads(): jnp.einsum('qngk,qngd->knd', prob_bf, do_blk, preferred_element_type=jnp....  41.8 us
  transfers between devices with their start and end apart: 62, of which 29 were waited for; matrix products, arithmetic and copies ran while one was open for 6% of the time, Pallas kernels for 0%

commit v1 on v0

v1 whole, which is shorter than its diff:
```python
import functools

import jax
import jax.numpy as jnp
from jax import lax
from jax.experimental import pallas as pl
from jax.experimental.pallas import tpu as pltpu
from jax.sharding import PartitionSpec as P

HEAD_DIM = 128
ROPE_THETA = 1000000.0
NORM_EPS = 1e-6
SM_SCALE = HEAD_DIM ** -0.5
LOG2E = 1.4426950408889634
EXP_SCALE = SM_SCALE * LOG2E
F32, BF16 = jnp.float32, jnp.bfloat16


def rope_tables(positions):
    inv_freq = ROPE_THETA ** (-jnp.arange(0, HEAD_DIM, 2).astype(F32) / HEAD_DIM)
    angles = positions.astype(F32)[:, None] * inv_freq[None, :]
    cos_h, sin_h = jnp.cos(angles), jnp.sin(angles)
    return jnp.concatenate([cos_h, cos_h], -1), jnp.concatenate([-sin_h, sin_h], -1)


def swap_halves(x):
    half = x.shape[-1] // 2
    return jnp.concatenate([x[..., half:], x[..., :half]], axis=-1)


def norm_rope(raw_in, weight, cos_t, sin_t):
    mean_sq = jnp.mean(raw_in * raw_in, axis=-1, keepdims=True)
    normed = raw_in * lax.rsqrt(mean_sq + NORM_EPS) * weight
    return normed * cos_t + swap_halves(normed) * sin_t


def dot(a, b, ca, cb):
    return lax.dot_general(a, b, (((ca,), (cb,)), ((), ())), preferred_element_type=F32)


def roll_half(x):
    return pltpu.roll(x, HEAD_DIM // 2, axis=x.ndim - 1)


def head_kernel(group, cp_size, chunk, per_kv, q_ref, do_ref, out_ref, lse_ref, cos_ref, sin_ref, w_ref, kv_ref,
                dq_in, dq_out, dkv_ref, dw_ref, qb, dob, aux, dq):
    rank = lax.axis_index('cp')
    rows = chunk * per_kv
    step = 16
    lane = lax.broadcasted_iota(jnp.int32, (step * per_kv, HEAD_DIM), 1)
    lane3 = lax.broadcasted_iota(jnp.int32, (step, per_kv, HEAD_DIM), 2)
    head3 = lax.broadcasted_iota(jnp.int32, (step, per_kv, HEAD_DIM), 1)
    weight = w_ref[...]

    def prepare(i, carry):
        toks = pl.ds(i * step, step)
        dst = pl.ds(pl.multiple_of(i * step * per_kv, step * per_kv), step * per_kv)
        x = q_ref[toks].astype(F32)
        mean_sq = jnp.mean(x * x, axis=-1, keepdims=True)
        y = x * lax.rsqrt(mean_sq + NORM_EPS) * weight
        qr = y * cos_ref[toks] + roll_half(y) * sin_ref[toks]
        qb[dst, :] = qr.reshape(step * per_kv, HEAD_DIM).astype(BF16)
        do = do_ref[toks]
        dob[dst, :] = do.reshape(step * per_kv, HEAD_DIM)
        delta = jnp.sum(do.astype(F32) * out_ref[toks].astype(F32), axis=-1, keepdims=True)
        lse = jnp.sum(jnp.where(lane3 == head3 + group * per_kv, lse_ref[toks], 0.0), axis=-1, keepdims=True)
        r0 = jnp.where(lane3 < 3, lse * (-1.0 / SM_SCALE), -delta).reshape(step * per_kv, HEAD_DIM)
        r1 = r0 - r0.astype(BF16).astype(F32)
        r2 = r1 - r1.astype(BF16).astype(F32)
        val = jnp.where((lane == 0) | (lane == 3), r0, jnp.where((lane == 1) | (lane == 4), r1, r2))
        aux[dst, :] = jnp.where(lane < 6, val, 0.0).astype(BF16)
        return carry

    lax.fori_loop(0, 2 * chunk // step, prepare, 0)
    dkv_ref[...] = jnp.zeros_like(dkv_ref)
    dq[...] = jnp.zeros_like(dq)

    n_early = rank // 2 + 1
    n_units = cp_size + 1
    keys = 2 * chunk
    klane = lax.broadcasted_iota(jnp.int32, (keys, HEAD_DIM), 1)
    ones_k = jnp.where(klane < 3, 1.0, 0.0).astype(BF16)
    ones_v = jnp.where((klane >= 3) & (klane < 6), 1.0, 0.0).astype(BF16)

    def unit(u, carry):
        late = u >= n_early
        kb = jnp.where(late, u - n_early, u)
        q_chunk = jnp.where(late, 2 * cp_size - 1 - rank, rank)
        half = kb >= cp_size // 2
        dev_a = jnp.where(half, 2 * cp_size - 1 - 2 * kb, 2 * kb)
        dev_b = jnp.where(half, 2 * cp_size - 2 - 2 * kb, 2 * kb + 1)
        hf = jnp.where(half, 1, 0)
        r = pl.ds(pl.multiple_of(jnp.where(late, rows, 0), rows), rows)
        k = jnp.concatenate([kv_ref[dev_a, hf, 0], kv_ref[dev_b, hf, 0]], axis=0)
        v = jnp.concatenate([kv_ref[dev_a, hf, 1], kv_ref[dev_b, hf, 1]], axis=0)
        qq, dd, ax = qb[r, :], dob[r, :], aux[r, :]
        s = dot(jnp.concatenate([qq, ax], 1), jnp.concatenate([k, ones_k], 1), 1, 1)
        dp = dot(jnp.concatenate([dd, ax], 1), jnp.concatenate([v, ones_v], 1), 1, 1)
        p = jnp.exp2(s * EXP_SCALE)
        off = (q_chunk - 2 * kb) * chunk
        klan = lax.broadcasted_iota(jnp.int32, (per_kv, keys), 1)
        p = jnp.concatenate([jnp.where(klan <= off + t, p[per_kv * t:per_kv * (t + 1)], 0.0) for t in range(chunk)], 0)
        ds = (p * dp).astype(BF16)
        pb = p.astype(BF16)
        dv = dot(dd, pb, 0, 0)
        dk = dot(qq, ds, 0, 0)
        dkv_ref[dev_a, hf, 0] += dk[:, :chunk]
        dkv_ref[dev_b, hf, 0] += dk[:, chunk:]
        dkv_ref[dev_a, hf, 1] += dv[:, :chunk]
        dkv_ref[dev_b, hf, 1] += dv[:, chunk:]
        dq[r, :] += dot(ds, k, 1, 0)
        return carry

    lax.fori_loop(0, n_units, unit, 0)

    def finish(i, acc):
        toks = pl.ds(i * step, step)
        src = pl.ds(pl.multiple_of(i * step * per_kv, step * per_kv), step * per_kv)
        x = q_ref[toks].astype(F32)
        rstd = lax.rsqrt(jnp.mean(x * x, axis=-1, keepdims=True) + NORM_EPS)
        xhat = x * rstd
        g = (dq[src, :] * SM_SCALE).reshape(step, per_kv, HEAD_DIM)
        dy = g * cos_ref[toks] - roll_half(g) * sin_ref[toks]
        acc = acc + jnp.sum((dy * xhat).reshape(step * per_kv // 8, 8, HEAD_DIM), axis=0)
        dxh = dy * weight
        dx = rstd * (dxh - xhat * jnp.mean(dxh * xhat, axis=-1, keepdims=True))
        dq_out[toks] = dx.astype(BF16)
        return acc

    dw_ref[...] = lax.fori_loop(0, 2 * chunk // step, finish, jnp.zeros((8, HEAD_DIM), F32))


def head_grads(group, cp_size, q_raw, d_out, out_fwd, lse3, cos3, sin3, w3, kv, dq_prev):
    tokens, heads, hd = q_raw.shape
    chunk = tokens // 2
    per_kv = 16
    rows = tokens * per_kv
    grp = pl.BlockSpec((tokens, per_kv, hd), lambda i: (0, group, 0))
    full = lambda a: pl.BlockSpec(a.shape, lambda i: (0,) * a.ndim)
    args = [q_raw, d_out, out_fwd, lse3, cos3, sin3, w3, kv]
    in_specs = [grp, grp, grp] + [full(a) for a in args[3:]]
    aliases = {}
    kern = functools.partial(head_kernel, group, cp_size, chunk, per_kv)
    if dq_prev is not None:
        args.append(dq_prev)
        in_specs.append(pl.BlockSpec(memory_space=pl.ANY))
        aliases = {8: 0}
    else:
        base = kern
        kern = lambda *refs: base(*refs[:8], None, *refs[8:])
    dkv_shape = kv.shape[:3] + (hd, chunk)
    return pl.pallas_call(
        kern,
        grid=(1,),
        in_specs=in_specs,
        out_specs=[grp, pl.BlockSpec(dkv_shape, lambda i: (0,) * 5), pl.BlockSpec((8, hd), lambda i: (0, 0))],
        out_shape=[jax.ShapeDtypeStruct(q_raw.shape, BF16), jax.ShapeDtypeStruct(dkv_shape, F32),
                   jax.ShapeDtypeStruct((8, hd), F32)],
        scratch_shapes=[pltpu.VMEM((rows, hd), BF16), pltpu.VMEM((rows, hd), BF16), pltpu.VMEM((rows, hd), BF16),
                        pltpu.VMEM((rows, hd), F32)],
        input_output_aliases=aliases,
        name='attn_bwd',
        compiler_params=pltpu.CompilerParams(vmem_limit_bytes=50 * 2 ** 20),
        cost_estimate=pl.CostEstimate(flops=11 * 10 ** 9, bytes_accessed=10 * 2 ** 20, transcendentals=10 ** 7),
    )(*args)


def solution(mesh):
    cp_size = mesh.shape['cp']

    def local_grads(q_raw, k_raw, v_proj, out_fwd, lse_fwd, d_out, q_norm, k_norm):
        dev_rank = lax.axis_index('cp')
        tokens, num_heads = q_raw.shape[0], q_raw.shape[1]
        chunk = tokens // 2
        kv_heads = k_raw.shape[1]
        offsets = jnp.arange(chunk)
        positions = jnp.concatenate([dev_rank * chunk + offsets, (2 * cp_size - 1 - dev_rank) * chunk + offsets])
        cos_t, sin_t = rope_tables(positions)
        k_full, pull_k = jax.vjp(lambda a, w: norm_rope(a, w, cos_t[:, None], sin_t[:, None]), k_raw.astype(F32), k_norm)
        kv = jnp.stack([k_full.astype(BF16), v_proj], axis=0)
        kv = kv.reshape(2, 2, chunk, kv_heads, HEAD_DIM).transpose(3, 1, 0, 2, 4)
        lse3 = jnp.pad(lse_fwd, ((0, 0), (0, HEAD_DIM - num_heads)))[:, None, :]
        cos3, sin3 = cos_t[:, None, :], sin_t[:, None, :]
        w3 = q_norm.reshape(1, 1, HEAD_DIM)
        dq_raw, parts, dws = None, [], []
        for g in range(kv_heads):
            kv_all = lax.all_gather(kv[g], 'cp')
            dq_raw, dkv, dw = head_grads(g, cp_size, q_raw, d_out, out_fwd, lse3, cos3, sin3, w3, kv_all, dq_raw)
            parts.append(lax.psum_scatter(dkv, 'cp', scatter_dimension=0))
            dws.append(dw)
        total = jnp.stack(parts)
        total = total.transpose(2, 1, 4, 0, 3).reshape(2, tokens, kv_heads, HEAD_DIM)
        dk_raw, dk_weight = pull_k(total[0] * SM_SCALE)
        dq_weight = jnp.sum(sum(dws), axis=0)
        return (dq_raw, dk_raw.astype(BF16), total[1].astype(BF16),
                lax.psum(dq_weight, 'cp'), lax.psum(dk_weight, 'cp'))

    row_spec = P(('dp', 'cp'))
    in_specs = (row_spec, row_spec, row_spec, row_spec, row_spec, row_spec, P(), P())
    out_specs = (row_spec, row_spec, row_spec, P('dp'), P('dp'))
    return jax.shard_map(local_grads, mesh=mesh, in_specs=in_specs, out_specs=out_specs, check_vma=False)
```

time: 919 us -> 443 us (0.48)
  matrix products: 230 us -> 0 us
  starting transfers between devices: 209 us -> 0.68 us
  local copies, waits for them, and re-layouts: 180 us -> 10.9 us
  other arithmetic: 151 us -> 5.73 us
  Pallas kernels: 0 us -> 145 us
  waiting for transfers between devices: 102 us -> 239 us
  between operations: 1.38 us -> 14.4 us
    dot_general x90 -> x0, matrix products: 230 us -> none  [the longest x18 76.4 us: pair_grads(): jnp.einsum('qngd,knd->qngk', do_blk, v_blk, preferred_element_type=jnp.fl...]
    ppermute x62 -> x0, starting transfers between devices: 209 us -> none  [the longest x15 68 us: visit_source(): dk_cur = lax.ppermute(dk_cur, 'cp', shift_pairs)]
    reduce_scatter x0 -> x4, waiting for transfers between devices: none -> 197 us  [local_grads(): parts.append(lax.psum_scatter(dkv, 'cp', scatter_dimension=0))]
    pallas_call x0 -> x4, Pallas kernels: none -> 145 us  [head_grads(): pl.pallas_call(kern, grid=(1,), in_specs=in_specs, out_specs=[grp, pl.Blo...]
    slice x52 -> x6, local copies, waits for them, and re-layouts: 107 us -> 1.45 us  [the longest x1 0.8 us: local_grads(): kv_all = lax.all_gather(kv[g], 'cp')]
    ppermute x62 -> x0, waiting for transfers between devices: 102 us -> none  [the longest x15 70.1 us: visit_source(): v_cur = lax.ppermute(v_cur, 'cp', shift_pairs)]
    concatenate x18 -> x0, other arithmetic: 94.5 us -> none  [the longest x14 87.8 us: late_source(): jnp.concatenate([dq_acc[:chunk_len], dq_acc[chunk_len:] + dq_part])]
    while x35 -> x0, local copies, waits for them, and re-layouts: 44.9 us -> none  [the longest x5 23.9 us: local_grads(): lax.fori_loop(1, cp_size, visit_source, (k_b, v_proj, dq_acc, dk_acc, dv_...]
  transfers between devices with their start and end apart: 62 -> 8, of which waited for: 29 -> 5; matrix products, arithmetic and copies ran while one was open for 6% -> 0% of each run, Pallas kernels for 0% -> 33%
where the time goes in v1:
time: 443 us
  waiting for transfers between devices  239 us (54%)
  Pallas kernels  145 us (33%)
  blocking collectives  27.2 us (6%)
  between operations  14.4 us (3%)
  local copies, waits for them, and re-layouts  10.9 us (2%)
  other arithmetic  5.73 us (1%)
    reduce_scatter x4, waiting for transfers between devices, local_grads(): parts.append(lax.psum_scatter(dkv, 'cp', scatter_dimension=0))  197 us
    pallas_call x4, Pallas kernels, head_grads(): pl.pallas_call(kern, grid=(1,), in_specs=in_specs, out_specs=[grp, pl.Blo...  145 us
    all_gather x4, waiting for transfers between devices, local_grads(): kv_all = lax.all_gather(kv[g], 'cp')  39 us
    psum x1, blocking collectives, local_grads(): lax.psum(dq_weight, 'cp')  27.2 us
    unnamed x20, local copies, waits for them, and re-layouts  9.27 us
  transfers between devices with their start and end apart: 8, of which 5 were waited for; matrix products, arithmetic and copies ran while one was open for 0% of the time, Pallas kernels for 33%

profile of v1, /device:TPU:21, one launch (start us, length us, event | category | flops | bytes accessed | tf_op | source)
XLA Modules:
  0.0 443.0 jit_solution(17838913103130907158)
XLA Ops:
  7.2 0.0 copy-start.5
  7.2 0.0 copy-start.7
  7.2 0.1 all-gather.11.cloned.1.call-start
  7.3 1.2 fusion.4
  8.5 1.0 copy.36
  9.5 0.5 fusion.8
  10.0 0.0 copy-start.6
  10.1 0.1 broadcast_multiply_fusion.1
  10.2 0.0 copy-start.4
  10.2 1.2 fusion.1
  11.3 0.2 fusion.12
  11.5 0.1 broadcast_multiply_fusion.2
  11.7 0.0 copy-done.5
  11.7 0.0 copy-done.7
  11.7 0.3 fusion.7
  12.0 0.1 maximum_bitcast_fusion.1
  12.1 0.8 fusion.11
  12.9 0.1 all-gather.11.cloned.1.call-update
  13.0 0.1 all-gather.9.cloned.1.call-start
  13.0 0.7 all-gather.9.cloned.1.call-update
  13.8 0.1 all-gather.7.cloned.1.call-start
  13.8 0.7 all-gather.7.cloned.1.call-update
  14.6 0.1 all-gather.5.cloned.1.call-start
  14.6 0.6 all-gather.5.cloned.1.call-update
  15.2 0.1 reduce-scatter.5.cloned.1.call-start
  15.3 0.0 copy-done.6
  15.3 0.1 copy.34
  15.4 39.0 %all-gather.11.cloned.1.call-done.refs_7_ = bf16[16,2,2,128,128]{4,3,2,1,0:T(8,128)(2,1)} async-done(((bf16[1,2,2,128,128]{4,3,2,1,0:T(8,128)(2,1)}), bf16[16,2,2,128,128]{4,3,2,1,0:T(8,128)(2,1)}) %all-gather.11.cloned.1.call-update) | async-done | bytes 2097168 | tf_op jit(solution)/shard_map/all_gather | solution.py:187
  54.4 0.0 copy-done.4
  54.4 0.0 copy-start.3
  54.4 1.6 copy-done.3
  56.0 36.4 %attn_bwd.4 = (bf16[256,64,128]{2,1,0:T(8,128)(2,1)}, f32[16,2,2,128,128]{4,3,2,1,0:T(8,128)}, f32[8,128]{1,0:T(8,128)S(1)}) custom-call(bf16[256,64,128]{2,1,0:T(8,128)(2,1)} %q_ref.5, bf16[256,64,128]{2,1,0:T(8,128)(2,1)} %do_ref.5, bf16[256,64,128]{2,1,0:T(8,128)(2,1)} %out_ref.5, f32[256,1,128]{2,1,0:T(1,128)S(1)} %bitcast.24, ...), custom_call_target="tpu_custom_call" | custom-call | flops 11000000512 | bytes 10485760 | tf_op jit(solution)/shard_map/attn_bwd/pallas_call | solution.py:152
  92.3 0.1 reduce-scatter.5.cloned.1.call-update
  92.4 0.1 reduce-scatter.7.cloned.1.call-start
  92.5 0.0 all-gather.9.cloned.1.call-done.kv_ref
  92.5 0.0 copy-start.2
  92.5 1.6 copy-done.2
  94.1 36.4 %attn_bwd.5 = (bf16[256,64,128]{2,1,0:T(8,128)(2,1)}, f32[16,2,2,128,128]{4,3,2,1,0:T(8,128)}, f32[8,128]{1,0:T(8,128)S(1)}) custom-call(bf16[256,64,128]{2,1,0:T(8,128)(2,1)} %q_ref.5, bf16[256,64,128]{2,1,0:T(8,128)(2,1)} %do_ref.5, bf16[256,64,128]{2,1,0:T(8,128)(2,1)} %out_ref.5, f32[256,1,128]{2,1,0:T(1,128)S(1)} %bitcast.25, ...), custom_call_target="tpu_custom_call", output_to_operand_aliasing={{0}: (8, {})} | custom-call | flops 11000000512 | bytes 10485760 | tf_op jit(solution)/shard_map/attn_bwd/pallas_call | solution.py:152
  130.5 0.1 reduce-scatter.7.cloned.1.call-update
  130.5 0.1 reduce-scatter.9.cloned.1.call-start
  130.6 0.0 all-gather.7.cloned.1.call-done.kv_ref
  130.6 0.0 copy-start.1
  130.6 1.6 copy-done.1
  132.2 36.4 %attn_bwd.6 = (bf16[256,64,128]{2,1,0:T(8,128)(2,1)}, f32[16,2,2,128,128]{4,3,2,1,0:T(8,128)}, f32[8,128]{1,0:T(8,128)S(1)}) custom-call(bf16[256,64,128]{2,1,0:T(8,128)(2,1)} %q_ref.5, bf16[256,64,128]{2,1,0:T(8,128)(2,1)} %do_ref.5, bf16[256,64,128]{2,1,0:T(8,128)(2,1)} %out_ref.5, f32[256,1,128]{2,1,0:T(1,128)S(1)} %bitcast.26, ...), custom_call_target="tpu_custom_call", output_to_operand_aliasing={{0}: (8, {})} | custom-call | flops 11000000512 | bytes 10485760 | tf_op jit(solution)/shard_map/attn_bwd/pallas_call | solution.py:152
  168.6 0.1 reduce-scatter.9.cloned.1.call-update
  168.7 0.2 reduce-scatter.11.cloned.1.call-start
  168.9 0.0 all-gather.5.cloned.1.call-done.kv_ref
  168.9 0.0 copy-start
  168.9 1.6 copy-done
  170.5 36.3 %attn_bwd.7 = (bf16[256,64,128]{2,1,0:T(8,128)(2,1)}, f32[16,2,2,128,128]{4,3,2,1,0:T(8,128)}, f32[8,128]{1,0:T(8,128)S(1)}) custom-call(bf16[256,64,128]{2,1,0:T(8,128)(2,1)} %q_ref.5, bf16[256,64,128]{2,1,0:T(8,128)(2,1)} %do_ref.5, bf16[256,64,128]{2,1,0:T(8,128)(2,1)} %out_ref.5, f32[256,1,128]{2,1,0:T(1,128)S(1)} %bitcast.27, ...), custom_call_target="tpu_custom_call", output_to_operand_aliasing={{0}: (8, {})} | custom-call | flops 11000000512 | bytes 10485760 | tf_op jit(solution)/shard_map/attn_bwd/pallas_call | solution.py:152
  206.9 0.1 reduce-scatter.11.cloned.1.call-update
  206.9 14.9 %reduce-scatter.5.cloned.1.call-done = f32[1,2,2,128,128]{4,3,2,1,0:T(8,128)} async-done(((f32[16,2,2,128,128]{4,3,2,1,0:T(8,128)}), f32[1,2,2,128,128]{4,3,2,1,0:T(8,128)}) %reduce-scatter.5.cloned.1.call-update) | async-done | bytes 262160 | tf_op jit(solution)/shard_map/reduce_scatter | solution.py:189
  221.8 60.6 %reduce-scatter.7.cloned.1.call-done = f32[1,2,2,128,128]{4,3,2,1,0:T(8,128)} async-done(((f32[16,2,2,128,128]{4,3,2,1,0:T(8,128)}), f32[1,2,2,128,128]{4,3,2,1,0:T(8,128)}) %reduce-scatter.7.cloned.1.call-update) | async-done | bytes 262160 | tf_op jit(solution)/shard_map/reduce_scatter | solution.py:189
  282.4 60.9 %reduce-scatter.9.cloned.1.call-done = f32[1,2,2,128,128]{4,3,2,1,0:T(8,128)} async-done(((f32[16,2,2,128,128]{4,3,2,1,0:T(8,128)}), f32[1,2,2,128,128]{4,3,2,1,0:T(8,128)}) %reduce-scatter.9.cloned.1.call-update) | async-done | bytes 262160 | tf_op jit(solution)/shard_map/reduce_scatter | solution.py:189
  343.3 60.9 %reduce-scatter.11.cloned.1.call-done = f32[1,2,2,128,128]{4,3,2,1,0:T(8,128)} async-done(((f32[16,2,2,128,128]{4,3,2,1,0:T(8,128)}), f32[1,2,2,128,128]{4,3,2,1,0:T(8,128)}) %reduce-scatter.11.cloned.1.call-update) | async-done | bytes 262160 | tf_op jit(solution)/shard_map/reduce_scatter | solution.py:189
  404.2 1.3 maximum_bitcast_fusion
  405.6 0.2 copy.42
  405.8 0.2 copy.43
  406.0 0.9 copy.45
  407.0 0.2 fusion.10
  407.2 0.5 fusion.2
  407.7 0.3 fusion.3
  408.1 0.9 copy.44
  409.0 27.2 %all-reduce.3 = (f32[128]{0:T(128)}, f32[128]{0:T(128)}) all-reduce(f32[128]{0:T(128)S(1)} %add_reduce_fusion, f32[128]{0:T(128)S(1)} %get-tuple-element.39), channel_id=1, replica_groups=mesh['dp'=4,'cp'=16] {'cp'}, use_global_device_ids=true, to_apply=%region_7.8 | all-reduce | flops 256 | bytes 2048 | tf_op jit(solution)/shard_map/psum | solution.py:196
  (10 shorter events, 0.2 us)
Async XLA Ops:
  7.2 4.5 %copy-start.5 = (bf16[256,4,128]{2,1,0:T(4,128)(2,1)S(1)}, bf16[256,4,128]{2,1,0:T(4,128)(2,1)}, u32[]{:S(2)}) copy-start(bf16[256,4,128]{2,1,0:T(4,128)(2,1)} %param.9) | copy-start | bytes 786436
  7.2 4.5 %copy-start.7 = (f32[128]{0:T(128)S(1)}, f32[128]{0:T(128)}, u32[]{:S(2)}) copy-start(f32[128]{0:T(128)} %param.15) | copy-start | bytes 1540
  7.2 47.2 %all-gather.11.cloned.1.call-start = ((), (), s32[]{:S(2)}) async-start(), calls=%async_computation.7 | async-start | bytes 2228224 | tf_op jit(solution)/shard_map/all_gather | solution.py:187
  10.0 5.2 %copy-start.6 = (f32[256,64]{0,1:T(8,128)S(1)}, f32[256,64]{0,1:T(8,128)}, u32[]{:S(2)}) copy-start(f32[256,64]{0,1:T(8,128)} %param.12) | copy-start | bytes 196612
  10.2 44.2 %copy-start.4 = (f32[128]{0:T(128)S(1)}, f32[128]{0:T(128)}, u32[]{:S(2)}) copy-start(f32[128]{0:T(128)} %param.14) | copy-start | bytes 1540
  13.0 79.5 %all-gather.9.cloned.1.call-start = ((), (), s32[]{:S(2)}) async-start(), calls=%async_computation.6 | async-start | bytes 2228224 | tf_op jit(solution)/shard_map/all_gather | solution.py:187
  13.8 116.9 %all-gather.7.cloned.1.call-start = ((), (), s32[]{:S(2)}) async-start(), calls=%async_computation.5 | async-start | bytes 2228224 | tf_op jit(solution)/shard_map/all_gather | solution.py:187
  14.6 154.4 %all-gather.5.cloned.1.call-start = ((), (), s32[]{:S(2)}) async-start(), calls=%async_computation.4 | async-start | bytes 2228224 | tf_op jit(solution)/shard_map/all_gather | solution.py:187
  15.2 206.6 %reduce-scatter.5.cloned.1.call-start = ((), (), s32[]{:S(2)}) async-start(), calls=%async_computation.8 | async-start | bytes 4456448 | tf_op jit(solution)/shard_map/reduce_scatter | solution.py:189
  54.4 1.6 copy-start.3
  92.4 190.1 %reduce-scatter.7.cloned.1.call-start = ((), (), s32[]{:S(2)}) async-start(), calls=%async_computation.9 | async-start | bytes 4456448 | tf_op jit(solution)/shard_map/reduce_scatter | solution.py:189
  92.5 1.6 copy-start.2
  130.5 212.8 %reduce-scatter.9.cloned.1.call-start = ((), (), s32[]{:S(2)}) async-start(), calls=%async_computation.10 | async-start | bytes 4456448 | tf_op jit(solution)/shard_map/reduce_scatter | solution.py:189
  130.6 1.6 copy-start.1
  168.7 235.6 %reduce-scatter.11.cloned.1.call-start = ((), (), s32[]{:S(2)}) async-start(), calls=%async_computation.11 | async-start | bytes 4456448 | tf_op jit(solution)/shard_map/reduce_scatter | solution.py:189
  168.9 1.6 copy-start
Sparse Core Ops, SparseCore 0:
  13.1 41.2 all-gather.10
  56.6 34.8 all-gather.8
  93.1 34.8 all-gather.6
  129.4 34.8 all-gather.4
  166.5 55.2 reduce-scatter.4
  224.0 58.3 reduce-scatter.6
  284.8 58.5 reduce-scatter.8
  345.7 58.5 reduce-scatter.10

commit v2 on v1

v2 whole, which is shorter than its diff:
```python
import functools

import jax
import jax.numpy as jnp
from jax import lax
from jax.experimental import pallas as pl
from jax.experimental.pallas import tpu as pltpu
from jax.sharding import PartitionSpec as P

HEAD_DIM = 128
ROPE_THETA = 1000000.0
NORM_EPS = 1e-6
SM_SCALE = HEAD_DIM ** -0.5
EXP_SCALE = SM_SCALE * 1.4426950408889634
F32, BF16 = jnp.float32, jnp.bfloat16
MESH = pl.DeviceIdType.MESH

ORDER_A = (-1, 1, 4, -3, 3, -2, 2)
ORDER_B = (4, -3, 3, -2, 2, -1, 1)
REACH = ((4, 3), (3, 4))
GATHER_AT = (-1, -1, -1, 0, 2, 3, 5, 7, 9, 11, 8, 10, 13, 15, 17, 20, 22, 25, 28, 31)
REDUCE_AT = (17, 18, 25, 26, 34, 37, 41, 45, 49, 53, 54, 56, 60, 64, 68, 71, 75, 79, 200, 201)
PREP_TOKENS = 32
FIN_STEPS = 16


def rope_tables(positions):
    inv_freq = ROPE_THETA ** (-jnp.arange(0, HEAD_DIM, 2).astype(F32) / HEAD_DIM)
    angles = positions.astype(F32)[:, None] * inv_freq[None, :]
    cos_h, sin_h = jnp.cos(angles), jnp.sin(angles)
    return jnp.concatenate([cos_h, cos_h], -1), jnp.concatenate([-sin_h, sin_h], -1)


def swap_halves(x):
    half = x.shape[-1] // 2
    return jnp.concatenate([x[..., half:], x[..., :half]], axis=-1)


def norm_rope(raw_in, weight, cos_t, sin_t):
    mean_sq = jnp.mean(raw_in * raw_in, axis=-1, keepdims=True)
    normed = raw_in * lax.rsqrt(mean_sq + NORM_EPS) * weight
    return normed * cos_t + swap_halves(normed) * sin_t


def dot(a, b, ca, cb):
    return lax.dot_general(a, b, (((ca,), (cb,)), ((), ())), preferred_element_type=F32)


def roll_half(x):
    return pltpu.roll(x, HEAD_DIM // 2, axis=x.ndim - 1)


def row_sum(prod, ones):
    high = prod.astype(BF16)
    low = (prod - high.astype(F32)).astype(BF16)
    return dot(jnp.concatenate([high, low], 1), ones, 1, 0)


def select_const(index, values):
    out = jnp.int32(values[0])
    for i, v in enumerate(values[1:], 1):
        out = jnp.where(index == i, v, out)
    return out


def lookup(step, table):
    out = jnp.int32(0)
    for i, at in enumerate(table):
        out = jnp.where(step == at, i + 1, out)
    return out


def mega_kernel(nz, chunk, per_kv,
                q_hbm, do_hbm, out_hbm, lse_hbm, kv_hbm, cos_hbm, sin_hbm, w_ref,
                dq_hbm, dkv_hbm, dw_ref,
                xq, xdo, xout, qb, aux, dq, kvall, acc, rsb, lse, cos_t, sin_t,
                ld_sem, xs_sem, xr_sem, kl_sem, ks_sem, kr_sem, tab_sem,
                ag_send, ag_recv, rs_send, rs_recv, dq_loc, dq_snd, dq_rcv, dk_loc, dk_snd, dk_rcv):
    me = lax.axis_index('cp')
    cp = 2 * nz
    z, core = me // 2, me % 2
    other = 1 - core
    sib = 2 * z + other
    right = 2 * lax.rem(z + 1, nz) + core
    left = 2 * lax.rem(z + nz - 1, nz) + core
    tok = 2 * chunk
    rows = tok * per_kv

    def wrap(i):
        return lax.rem(i + 2 * nz, nz)

    barrier = pltpu.get_barrier_semaphore()

    def say(i, carry):
        pl.semaphore_signal(barrier, inc=1, device_id={'cp': lax.rem(me + i, cp)}, device_id_type=MESH)
        return carry

    lax.fori_loop(1, cp, say, 0)

    def my_off(el):
        return pl.multiple_of((core if el == 0 else other) * chunk, chunk)

    def sib_off(el):
        return pl.multiple_of((other if el == 0 else core) * chunk, chunk)

    kv_loads, loads = [], []
    for h in range(2):
        for el in range(2):
            kv_loads.append(pltpu.make_async_copy(kv_hbm.at[core, h, el], kvall.at[z, h, el, :, pl.ds(my_off(el), chunk), :], kl_sem.at[h, el]))
    tables = [pltpu.make_async_copy(cos_hbm, cos_t, tab_sem.at[0]), pltpu.make_async_copy(sin_hbm, sin_t, tab_sem.at[1])]
    for h in range(2):
        for el in range(2):
            heads = lambda c: pl.ds(pl.multiple_of((2 * c + h) * per_kv, per_kv), per_kv)
            src = pl.ds(el * chunk, chunk)
            dst = pl.ds(my_off(el), chunk)
            row = []
            for i, (hbm, buf) in enumerate(((q_hbm, xq), (do_hbm, xdo), (out_hbm, xout))):
                row.append((pltpu.make_async_copy(hbm.at[src, heads(core), :], buf.at[h, el, dst], ld_sem.at[h, el, i]),
                            pltpu.make_async_remote_copy(hbm.at[src, heads(other), :], buf.at[h, el, dst], xs_sem.at[h, el, i],
                                                         xr_sem.at[h, el, i], device_id={'cp': sib}, device_id_type=MESH)))
            row.append((pltpu.make_async_copy(lse_hbm.at[core, h, src], lse.at[h, el, dst], ld_sem.at[h, el, 3]),
                        pltpu.make_async_remote_copy(lse_hbm.at[other, h, src], lse.at[h, el, dst], xs_sem.at[h, el, 3],
                                                     xr_sem.at[h, el, 3], device_id={'cp': sib}, device_id_type=MESH)))
            loads.append(row)
    for cpy in kv_loads + tables:
        cpy.start()
    for row in loads:
        for loc, _ in row:
            loc.start()
    pl.semaphore_wait(barrier, cp - 1)

    kv_swaps = []
    for h in range(2):
        for el in range(2):
            kv_swaps.append(pltpu.make_async_remote_copy(
                kv_hbm.at[other, h, el], kvall.at[z, h, el, :, pl.ds(my_off(el), chunk), :], ks_sem.at[h, el], kr_sem.at[h, el],
                device_id={'cp': sib}, device_id_type=MESH))
    for cpy in kv_swaps:
        cpy.start()
    for row in loads:
        for _, rem in row:
            rem.start()

    def reach(direction, h):
        return jnp.where(h == 0, REACH[0][direction], REACH[1][direction])

    def gather_copy(direction, h, s, el):
        owner = wrap(z - (s - 1)) if direction == 0 else wrap(z + (s - 1))
        ref = kvall.at[owner, h, el]
        return pltpu.make_async_remote_copy(ref, ref, ag_send.at[direction, h, s - 1, el], ag_recv.at[direction, h, s - 1, el],
                                            device_id={'cp': (right, left)[direction]}, device_id_type=MESH)

    def gather_arrival(direction, h, s, el):
        owner = wrap(z - s) if direction == 0 else wrap(z + s)
        ref = kvall.at[owner, h, el]
        return pltpu.make_async_remote_copy(ref, ref, ag_send.at[direction, h, s - 1, el], ag_recv.at[direction, h, s - 1, el],
                                            device_id={'cp': (right, left)[direction]}, device_id_type=MESH)

    def gather_sends(direction, h, s, el):
        dist = reach(direction, h)
        if direction == 0:
            ok = (el == 0) | (wrap(z - (s - 1)) + dist >= nz)
        else:
            ok = (el == 0) | ((z >= 1) & (z + s - 1 <= nz - 1))
        return (s <= dist) & ok

    def gather_arrives(direction, h, s, el):
        dist = reach(direction, h)
        if direction == 0:
            ok = (el == 0) | (wrap(z - s) + dist >= nz)
        else:
            ok = (el == 0) | (z + s <= nz - 1)
        return (s >= 1) & (s <= dist) & ok

    def gather_step(a):
        h, s, el = a // 10, lax.rem(a, 10) // 2 + 1, lax.rem(a, 2)
        for direction in range(2):
            @pl.when(gather_arrives(direction, h, s - 1, el))
            def _():
                gather_arrival(direction, h, jnp.maximum(s - 1, 1), el).wait_recv()

            @pl.when(gather_sends(direction, h, s, el))
            def _():
                gather_copy(direction, h, jnp.minimum(s, 4), el).start()

    def reduce_copy(direction, h, d, el):
        owner = wrap(z + d) if direction == 0 else wrap(z - d)
        return pltpu.make_async_remote_copy(acc.at[owner, h, el], rsb.at[direction, d - 1, h, el],
                                            rs_send.at[direction, d - 1, h, el], rs_recv.at[direction, d - 1, h, el],
                                            device_id={'cp': (right, left)[direction]}, device_id_type=MESH)

    def reduce_sends(direction, h, d, el):
        dist = reach(direction, h)
        if direction == 0:
            ok = (el == 0) | (z + d <= nz - 1)
        else:
            ok = (el == 0) | (wrap(z - d) + dist >= nz)
        return (d >= 1) & (d <= dist) & ok

    def reduce_arrives(direction, h, d, el):
        dist = reach(direction, h)
        if direction == 0:
            ok = (el == 0) | ((z >= 1) & (z + d <= nz - 1))
        else:
            ok = (el == 0) | (wrap(z - d) + dist >= nz)
        return (d + 1 <= dist) & ok

    def reduce_step(b):
        h, d, el = b // 10, 4 - lax.rem(b, 10) // 2, lax.rem(b, 2)
        for direction in range(2):
            owner = wrap(z + d) if direction == 0 else wrap(z - d)

            @pl.when(reduce_arrives(direction, h, d, el))
            def _():
                slot = jnp.minimum(d, 3)
                pltpu.make_async_remote_copy(acc.at[owner, h, el], rsb.at[direction, slot, h, el],
                                             rs_send.at[direction, slot, h, el], rs_recv.at[direction, slot, h, el],
                                             device_id={'cp': (right, left)[direction]}, device_id_type=MESH).wait_recv()
                acc[owner, h, el] += rsb[direction, slot, h, el]

            @pl.when(reduce_sends(direction, h, d, el))
            def _():
                reduce_copy(direction, h, jnp.maximum(d, 1), el).start()

    def ticks(g):
        a = lookup(g, GATHER_AT)

        @pl.when(a > 0)
        def _():
            gather_step(a - 1)

        b = lookup(g, REDUCE_AT)

        @pl.when(b > 0)
        def _():
            reduce_step(b - 1)

    for i in range(4):
        kv_loads[i].wait()
        kv_swaps[i].wait_recv()
        if i < 2:
            gather_step(jnp.int32(i))

    sub = PREP_TOKENS
    weight = w_ref[...]
    ones = jnp.ones((2 * HEAD_DIM, HEAD_DIM), BF16)
    lane3 = lax.broadcasted_iota(jnp.int32, (sub, per_kv, HEAD_DIM), 2)
    head3 = lax.broadcasted_iota(jnp.int32, (sub, per_kv, HEAD_DIM), 1)
    n_l = 3 * per_kv
    lse_mask = (lane3 - head3 == 0) | (lane3 - head3 == per_kv) | (lane3 - head3 == 2 * per_kv)
    flat = lambda x: x.reshape(x.shape[0] * per_kv, HEAD_DIM)

    def prepare(h, el, i):
        toks = pl.ds(pl.multiple_of(i * sub, sub), sub)
        tabs = pl.ds(pl.multiple_of(el * tok + i * sub, sub), sub)
        dst = pl.ds(pl.multiple_of(((h * 2 + el) * tok + i * sub) * per_kv, sub * per_kv), sub * per_kv)
        x = xq[h, el, toks].astype(F32)
        ms = row_sum(flat(x * x), ones) * (1.0 / HEAD_DIM)
        y = flat(x) * lax.rsqrt(ms + NORM_EPS) * weight
        y3 = y.reshape(x.shape)
        qr = y3 * cos_t[tabs] + roll_half(y3) * sin_t[tabs]
        qb[dst, :] = flat(qr).astype(BF16)
        prod = flat(xdo[h, el, toks].astype(F32) * xout[h, el, toks].astype(F32))
        r0 = -row_sum(prod, ones)
        r1 = r0 - r0.astype(BF16).astype(F32)
        r2 = r1 - r1.astype(BF16).astype(F32)
        lane = lax.broadcasted_iota(jnp.int32, r0.shape, 1)
        dpart = jnp.where(lane == n_l, r0, jnp.where(lane == n_l + 1, r1, jnp.where(lane == n_l + 2, r2, 0.0)))
        aux[dst, :] = flat(jnp.where(lse_mask, lse[h, el, toks], dpart.reshape(x.shape))).astype(BF16)

    for t in tables:
        t.wait()
    for h in range(2):
        for el in range(2):
            for loc, rem in loads[h * 2 + el]:
                loc.wait()
                rem.wait_recv()
            pl.loop(0, tok // sub)(functools.partial(prepare, h, el))
        if h == 0:
            gather_step(jnp.int32(2))

    acc[...] = jnp.zeros_like(acc)
    dq[...] = jnp.zeros_like(dq)

    keys = tok
    half_rows = rows // 2
    klane = lax.broadcasted_iota(jnp.int32, (keys, HEAD_DIM), 1)
    ones_k = jnp.where(klane < n_l, 1.0, 0.0).astype(BF16)
    ones_v = jnp.where((klane >= n_l) & (klane < n_l + 3), 1.0, 0.0).astype(BF16)
    own_steps = 6
    head_steps = own_steps + 4 * (nz - 1)

    def work(g, carry):
        h = jnp.where(g >= head_steps, 1, 0)
        u = g - h * head_steps
        own = jnp.where(h == 0, u < own_steps, u >= 4 * (nz - 1))
        ou = jnp.where(h == 0, u, u - 4 * (nz - 1))
        bu = jnp.where(h == 0, u - own_steps, u)
        bu = jnp.clip(bu, 0, 4 * (nz - 1) - 1)
        ou = jnp.clip(ou, 0, own_steps - 1)
        k_idx, j = bu // 4, lax.rem(bu, 4) // 2
        half = jnp.where(own, lax.rem(ou, 2), lax.rem(bu, 2))
        delta = jnp.where(h == 0, select_const(k_idx, ORDER_A), select_const(k_idx, ORDER_B))
        kz = jnp.where(own, z, wrap(z + delta))
        lower = kz < z
        q_late = jnp.where(own, jnp.where(ou >= 2, 1, 0), jnp.where(lower, j, 1))
        k_late = jnp.where(own, jnp.where(ou >= 4, 1, 0), jnp.where(lower, 0, j))
        q_blk = jnp.where(q_late == 1, 2 * nz - 1 - z, z)
        k_blk = jnp.where(k_late == 1, 2 * nz - 1 - kz, kz)
        off = (q_blk - k_blk) * tok + half * chunk
        r = pl.ds(pl.multiple_of(((h * 2 + q_late) * 2 + half) * half_rows, half_rows), half_rows)
        k, v = kvall[kz, h, k_late, 0], kvall[kz, h, k_late, 1]
        qq, ax = qb[r, :], aux[r, :]
        dd = flat(xdo[h, q_late, pl.ds(pl.multiple_of(half * chunk, chunk), chunk)])
        s = dot(jnp.concatenate([qq, ax], 1), jnp.concatenate([k, ones_k], 1), 1, 1)
        dp = dot(jnp.concatenate([dd, ax], 1), jnp.concatenate([v, ones_v], 1), 1, 1)
        p = jnp.exp2(s * EXP_SCALE)
        klan = lax.broadcasted_iota(jnp.int32, (per_kv, keys), 1)
        p = jnp.concatenate([jnp.where(klan <= off + t, p[per_kv * t:per_kv * (t + 1)], 0.0) for t in range(chunk)], 0)
        ds = (p * dp).astype(BF16)
        pb = p.astype(BF16)
        acc[kz, h, k_late, 0] += dot(qq, ds, 0, 0)
        acc[kz, h, k_late, 1] += dot(dd, pb, 0, 0)
        dq[r, :] += dot(ds, k, 1, 0)
        ticks(g)
        return carry

    n_steps = 2 * head_steps
    lax.fori_loop(0, n_steps, work, 0)

    ftok = 4 * tok // FIN_STEPS
    per_blk = FIN_STEPS // 4

    def finish(i, carry):
        hel = i // per_blk
        h, el, part = hel // 2, lax.rem(hel, 2), lax.rem(i, per_blk)

        def piece(jj, wsum):
            t0 = part * ftok + jj * sub
            toks = pl.ds(pl.multiple_of(t0, sub), sub)
            tabs = pl.ds(pl.multiple_of(el * tok + t0, sub), sub)
            src = pl.ds(pl.multiple_of((hel * tok + t0) * per_kv, sub * per_kv), sub * per_kv)
            x3 = xq[h, el, toks].astype(F32)
            x = flat(x3)
            rstd = lax.rsqrt(row_sum(x * x, ones) * (1.0 / HEAD_DIM) + NORM_EPS)
            xhat = x * rstd
            gq = (dq[src, :] * SM_SCALE).reshape(x3.shape)
            dy = flat(gq * cos_t[tabs] - roll_half(gq) * sin_t[tabs])
            wsum = wsum + jnp.sum((dy * xhat).reshape(sub * per_kv // 8, 8, HEAD_DIM), axis=0)
            dxh = dy * weight
            dx = rstd * (dxh - xhat * jnp.mean(dxh * xhat, axis=-1, keepdims=True))
            xq[h, el, toks] = dx.reshape(x3.shape).astype(BF16)
            return wsum

        wsum = lax.fori_loop(0, ftok // sub, piece, jnp.zeros((8, HEAD_DIM), F32))
        dw_ref[...] += wsum
        ticks(n_steps + i)
        return carry

    dw_ref[...] = jnp.zeros_like(dw_ref)
    lax.fori_loop(0, FIN_STEPS, finish, 0)

    outs = []
    for h in range(2):
        for el in range(2):
            heads = pl.ds(pl.multiple_of((2 * core + h) * per_kv, per_kv), per_kv)
            dst = dq_hbm.at[pl.ds(el * chunk, chunk), heads, :]
            outs.append((pltpu.make_async_copy(xq.at[h, el, pl.ds(my_off(el), chunk)], dst, dq_loc.at[h, el]),
                         pltpu.make_async_remote_copy(xq.at[h, el, pl.ds(sib_off(el), chunk)], dst, dq_snd.at[h, el], dq_rcv.at[h, el],
                                                      device_id={'cp': sib}, device_id_type=MESH)))
    for loc, rem in outs:
        loc.start()
        rem.start()

    def rest(b, carry):
        reduce_step(b)
        return carry

    done = sum(1 for at in REDUCE_AT if at < n_steps + FIN_STEPS)
    lax.fori_loop(done, len(REDUCE_AT), rest, 0)

    for h in range(2):
        for el in range(2):
            dst = dkv_hbm.at[2 * core + h, el]
            outs.append((pltpu.make_async_copy(acc.at[z, h, el, :, :, pl.ds(my_off(el), chunk)], dst, dk_loc.at[h, el]),
                         pltpu.make_async_remote_copy(acc.at[z, h, el, :, :, pl.ds(sib_off(el), chunk)], dst, dk_snd.at[h, el],
                                                      dk_rcv.at[h, el], device_id={'cp': sib}, device_id_type=MESH)))
    for loc, rem in outs[4:]:
        loc.start()
        rem.start()

    for cpy in kv_swaps:
        cpy.wait_send()
    for row in loads:
        for _, rem in row:
            rem.wait_send()

    def drain(i, carry):
        h, s, el = i // 8, lax.rem(i, 8) // 2 + 1, lax.rem(i, 2)
        for direction in range(2):
            @pl.when(gather_sends(direction, h, s, el))
            def _():
                gather_copy(direction, h, s, el).wait_send()

            @pl.when(reduce_sends(direction, h, s, el))
            def _():
                reduce_copy(direction, h, s, el).wait_send()
        return carry

    lax.fori_loop(0, 16, drain, 0)
    for loc, rem in outs:
        loc.wait()
        rem.wait()


def mega(nz, q_raw, d_out, out_fwd, lse_arr, kv_loc, cos3, sin3, weight):
    tokens, heads, hd = q_raw.shape
    chunk, per_kv = tokens // 2, 16
    tok = tokens
    any_spec = pl.BlockSpec(memory_space=pl.ANY)
    vmem = pl.BlockSpec(memory_space=pltpu.VMEM)
    dma = pltpu.SemaphoreType.DMA
    x_shape = (2, 2, tok, per_kv, hd)
    n_rows = 4 * tok * per_kv
    hbm = lambda a: pltpu.with_memory_space_constraint(a, pltpu.HBM)
    return pl.pallas_call(
        functools.partial(mega_kernel, nz, chunk, per_kv),
        in_specs=[any_spec] * 7 + [vmem],
        out_specs=[any_spec, any_spec, vmem],
        out_shape=[jax.ShapeDtypeStruct(q_raw.shape, BF16), jax.ShapeDtypeStruct((4, 2, 2, hd, chunk), F32),
                   jax.ShapeDtypeStruct((8, hd), F32)],
        scratch_shapes=[
            pltpu.VMEM(x_shape, BF16), pltpu.VMEM(x_shape, BF16), pltpu.VMEM(x_shape, BF16),
            pltpu.VMEM((n_rows, hd), BF16), pltpu.VMEM((n_rows, hd), BF16), pltpu.VMEM((n_rows, hd), F32),
            pltpu.VMEM((nz, 2, 2, 2, tok, hd), BF16),
            pltpu.VMEM((nz, 2, 2, 2, hd, tok), F32),
            pltpu.VMEM((2, 4, 2, 2, 2, hd, tok), F32),
            pltpu.VMEM((2, 2, tok, 1, hd), F32),
            pltpu.VMEM((2 * tok, 1, hd), F32), pltpu.VMEM((2 * tok, 1, hd), F32),
            dma((2, 2, 4)), dma((2, 2, 4)), dma((2, 2, 4)),
            dma((2, 2)), dma((2, 2)), dma((2, 2)), dma((2,)),
            dma((2, 2, 4, 2)), dma((2, 2, 4, 2)), dma((2, 4, 2, 2)), dma((2, 4, 2, 2)),
            dma((2, 2)), dma((2, 2)), dma((2, 2)), dma((2, 2)), dma((2, 2)), dma((2, 2)),
        ],
        name='attn_bwd',
        compiler_params=pltpu.CompilerParams(vmem_limit_bytes=67000000, collective_id=0, has_side_effects=True),
    )(*[hbm(a) for a in (q_raw, d_out, out_fwd, lse_arr, kv_loc, cos3, sin3)], weight)


def sum_kernel(cp, x_ref, o_ref, slots, send_sem, recv_sem):
    me = lax.axis_index('cp')
    barrier = pltpu.get_barrier_semaphore()

    def say(i, carry):
        pl.semaphore_signal(barrier, inc=1, device_id={'cp': lax.rem(me + i, cp)}, device_id_type=MESH)
        return carry

    lax.fori_loop(1, cp, say, 0)
    pl.semaphore_wait(barrier, cp - 1)

    def copy(i):
        return pltpu.make_async_remote_copy(x_ref, slots.at[cp - i], send_sem.at[i], recv_sem.at[cp - i],
                                            device_id={'cp': lax.rem(me + i, cp)}, device_id_type=MESH)

    for i in range(1, cp):
        copy(i).start()
    total = x_ref[...]
    for i in range(1, cp):
        pltpu.make_async_remote_copy(x_ref, slots.at[i], send_sem.at[i], recv_sem.at[i],
                                     device_id={'cp': lax.rem(me + i, cp)}, device_id_type=MESH).wait_recv()
    slots[0] = x_ref[...]

    def add(i, acc):
        return acc + slots[lax.rem(i - me + cp, cp)]

    o_ref[...] = lax.fori_loop(0, cp, add, jnp.zeros_like(total))
    for i in range(1, cp):
        copy(i).wait_send()


def sum_over_ring(cp, x):
    vmem = pl.BlockSpec(memory_space=pltpu.VMEM)
    return pl.pallas_call(
        functools.partial(sum_kernel, cp),
        in_specs=[vmem], out_specs=vmem,
        out_shape=jax.ShapeDtypeStruct(x.shape, F32),
        scratch_shapes=[pltpu.VMEM((cp,) + x.shape, F32), pltpu.SemaphoreType.DMA((cp,)), pltpu.SemaphoreType.DMA((cp,))],
        name='weight_sum',
        compiler_params=pltpu.CompilerParams(collective_id=1, has_side_effects=True),
    )(x)


def solution(mesh):
    cp_size = mesh.shape['cp']
    nz = cp_size // 2

    def local_grads(q_raw, k_raw, v_proj, out_fwd, lse_fwd, d_out, q_norm, k_norm):
        dev_rank = lax.axis_index('cp')
        z = dev_rank // 2
        tokens, num_heads = q_raw.shape[0], q_raw.shape[1]
        chunk = tokens // 2
        kv_heads = k_raw.shape[1]
        per_kv = num_heads // kv_heads
        offsets = jnp.arange(chunk)
        positions = jnp.concatenate([dev_rank * chunk + offsets, (2 * cp_size - 1 - dev_rank) * chunk + offsets])
        cos_t, sin_t = rope_tables(positions)
        k_full, pull_k = jax.vjp(lambda a, w: norm_rope(a, w, cos_t[:, None], sin_t[:, None]), k_raw.astype(F32), k_norm)
        kv = jnp.stack([k_full.astype(BF16), v_proj], axis=0)
        kv = kv.reshape(2, 2, chunk, 2, kv_heads // 2, HEAD_DIM).transpose(3, 4, 1, 0, 2, 5)
        chip_off = jnp.arange(tokens)
        chip_pos = jnp.concatenate([z * tokens + chip_off, (2 * nz - 1 - z) * tokens + chip_off])
        cos_c, sin_c = rope_tables(chip_pos)
        neg = (lse_fwd * (-1.0 / SM_SCALE)).reshape(tokens, 2, kv_heads // 2, per_kv)
        hi = lax.reduce_precision(neg, 8, 7)
        mid = lax.reduce_precision(neg - hi, 8, 7)
        low = neg - hi - mid
        zero = jnp.zeros((tokens, 2, kv_heads // 2, HEAD_DIM - 3 * per_kv), F32)
        lse_arr = jnp.concatenate([hi, mid, low, zero], -1).transpose(1, 2, 0, 3)[:, :, :, None, :]
        dq_raw, dkv, dw = mega(nz, q_raw, d_out, out_fwd, lse_arr, kv, cos_c[:, None], sin_c[:, None], q_norm.reshape(1, HEAD_DIM))
        total = dkv.transpose(2, 1, 4, 0, 3).reshape(2, tokens, kv_heads, HEAD_DIM)
        dk_raw, dk_weight = pull_k(total[0] * SM_SCALE)
        sums = jnp.concatenate([jnp.sum(dw, axis=0)[None], dk_weight[None], jnp.zeros((6, HEAD_DIM), F32)], axis=0)
        sums = sum_over_ring(cp_size, sums)
        return dq_raw, dk_raw.astype(BF16), total[1].astype(BF16), sums[0], sums[1]

    row_spec = P(('dp', 'cp'))
    in_specs = (row_spec, row_spec, row_spec, row_spec, row_spec, row_spec, P(), P())
    out_specs = (row_spec, row_spec, row_spec, P('dp'), P('dp'))
    return jax.shard_map(local_grads, mesh=mesh, in_specs=in_specs, out_specs=out_specs, check_vma=False)
```

time: 443 us -> 219 us (0.49)
  waiting for transfers between devices: 239 us -> 0 us
  Pallas kernels: 145 us -> 194 us
  blocking collectives: 27.2 us -> 0 us
  between operations: 14.4 us -> 0.9 us
  other arithmetic: 5.73 us -> 12.1 us
    reduce_scatter x4 -> x0, waiting for transfers between devices: 197 us -> none  [local_grads(): parts.append(lax.psum_scatter(dkv, 'cp', scatter_dimension=0))]
    pallas_call x4 -> x2, Pallas kernels: 145 us -> 194 us  [the longest x1 181 us: mega(): pl.pallas_call(functools.partial(mega_kernel, nz, chunk, per_kv), in_spec...]
    all_gather x4 -> x0, waiting for transfers between devices: 39 us -> none  [local_grads(): kv_all = lax.all_gather(kv[g], 'cp')]
    psum x1 -> x0, blocking collectives: 27.2 us -> none  [local_grads(): lax.psum(dq_weight, 'cp')]
    unnamed x20 -> x18, local copies, waits for them, and re-layouts: 9.27 us -> 7.05 us
  transfers between devices with their start and end apart: 8 -> 0, of which waited for: 5 -> 0; matrix products, arithmetic and copies ran while one was open for 0% -> 0% of each run, Pallas kernels for 33% -> 0%
where the time goes in v2:
time: 219 us
  Pallas kernels  194 us (89%)
  other arithmetic  12.1 us (6%)
  local copies, waits for them, and re-layouts  11.9 us (5%)
    pallas_call x1, Pallas kernels, mega(): pl.pallas_call(functools.partial(mega_kernel, nz, chunk, per_kv), in_spec...  181 us
    pallas_call x1, Pallas kernels, sum_over_ring(): pl.pallas_call(functools.partial(sum_kernel, cp), in_specs=[vmem], out_sp...  13.1 us
    unnamed x18, local copies, waits for them, and re-layouts  7.05 us

profile of v2, /device:TPU:21, one launch (start us, length us, event | category | flops | bytes accessed | tf_op | source)
XLA Modules:
  0.0 219.0 jit_solution(463729985118926557)
XLA Ops:
  0.6 0.0 copy-start
  0.6 0.0 copy-start.5
  0.7 0.0 copy-start.3
  0.7 1.0 fusion.8
  1.7 0.8 pad_maximum_fusion.1
  2.6 0.0 copy-start.4
  2.6 0.8 pad_maximum_fusion
  3.4 0.5 multiply_cosine_fusion.1
  4.0 0.8 broadcast_multiply_fusion.2
  4.7 0.8 broadcast_multiply_fusion.1
  5.5 1.2 fusion.4
  6.7 1.2 fusion.1
  7.8 0.2 fusion.12
  8.0 0.0 copy-done
  8.0 0.0 copy-done.5
  8.1 0.3 fusion.7
  8.4 0.0 copy-done.3
  8.5 0.9 maximum_bitcast_fusion.kv_hbm
  9.3 0.0 copy-done.4
  9.4 0.2 copy.27
  9.6 0.2 copy.25
  9.8 0.1 subtract_reduce-precision_fusion
  9.9 0.1 pad.30.clone
  9.9 1.1 maximum_maximum_fusion
  11.1 181.1 %attn_bwd.1 = (bf16[256,64,128]{2,1,0:T(8,128)(2,1)}, f32[4,2,2,128,128]{4,3,2,1,0:T(8,128)}, f32[8,128]{1,0:T(8,128)}) custom-call(bf16[256,64,128]{2,1,0:T(8,128)(2,1)} %q_hbm.1, bf16[256,64,128]{2,1,0:T(8,128)(2,1)} %do_hbm.1, bf16[256,64,128]{2,1,0:T(8,128)(2,1)} %out_hbm.1, f32[2,2,256,1,128]{4,3,2,1,0:T(1,128)} %bitcast.24, ...), custom_call_target="tpu_custom_call" | custom-call | tf_op jit(solution)/shard_map/attn_bwd/pallas_call | solution.py:426
  192.2 0.0 copy-start.1
  192.2 0.0 copy-start.2
  192.2 0.0 copy-start.6
  192.2 1.1 slice.29
  193.4 0.2 copy.31
  193.6 1.0 broadcast_multiply_fusion
  194.5 0.2 fusion.11
  194.7 0.0 copy-done.1
  194.7 0.0 copy-done.2
  194.7 0.5 fusion.2
  195.3 0.0 copy-done.6
  195.3 0.1 pad.10.clone
  195.4 0.7 maximum_maximum_fusion.1.x_ref
  196.0 13.1 %weight_sum.1 = f32[8,128]{1,0:T(8,128)} custom-call(f32[8,128]{1,0:T(8,128)} %maximum_maximum_fusion.1.x_ref), custom_call_target="tpu_custom_call" | custom-call | tf_op jit(solution)/shard_map/weight_sum/pallas_call | solution.py:483
  209.1 1.3 slice_bitcast_fusion
  210.4 0.3 fusion.3
  210.7 0.9 copy.33
  211.7 1.1 slice.34
  212.7 0.2 copy.32
  212.9 0.9 copy.34
  213.8 5.2 %copy.43 = bf16[256,64,128]{2,1,0:T(8,128)(2,1)} copy(bf16[256,64,128]{2,1,0:T(8,128)(2,1)} %get-tuple-element.51) | data formatting | bytes 8388608
  (13 shorter events, 0.1 us)
Async XLA Ops:
  0.6 7.4 %copy-start = (bf16[256,4,128]{2,1,0:T(4,128)(2,1)S(1)}, bf16[256,4,128]{2,1,0:T(4,128)(2,1)}, u32[]{:S(2)}) copy-start(bf16[256,4,128]{2,1,0:T(4,128)(2,1)} %param.9) | copy-start | bytes 786436
  0.6 7.4 %copy-start.5 = (f32[128]{0:T(128)S(1)}, f32[128]{0:T(128)}, u32[]{:S(2)}) copy-start(f32[128]{0:T(128)} %param.15) | copy-start | bytes 1540
  0.7 7.7 %copy-start.3 = (bf16[256,4,128]{2,1,0:T(4,128)(2,1)S(1)}, bf16[256,4,128]{2,1,0:T(4,128)(2,1)}, u32[]{:S(2)}) copy-start(bf16[256,4,128]{2,1,0:T(4,128)(2,1)} %param.10) | copy-start | bytes 786436
  2.6 6.8 %copy-start.4 = (f32[256,64]{0,1:T(8,128)S(1)}, f32[256,64]{0,1:T(8,128)}, u32[]{:S(2)}) copy-start(f32[256,64]{0,1:T(8,128)} %param.12) | copy-start | bytes 196612
  192.2 2.5 %copy-start.1 = (bf16[256,4,128]{2,1,0:T(4,128)(2,1)S(1)}, bf16[256,4,128]{2,1,0:T(4,128)(2,1)}, u32[]{:S(2)}) copy-start(bf16[256,4,128]{2,1,0:T(4,128)(2,1)} %param.9) | copy-start | bytes 786436
  192.2 2.5 %copy-start.2 = (f32[256,128]{1,0:T(8,128)S(1)}, f32[256,128]{1,0:T(8,128)}, u32[]{:S(2)}) copy-start(f32[256,128]{1,0:T(8,128)} %get-tuple-element.32) | copy-start | bytes 393220
  192.2 3.1 %copy-start.6 = (f32[8,128]{1,0:T(8,128)S(1)}, f32[8,128]{1,0:T(8,128)}, u32[]{:S(2)}) copy-start(f32[8,128]{1,0:T(8,128)} %get-tuple-element.10) | copy-start | bytes 12292

commit v3 on v0

v3 whole, which is shorter than its diff:
```python
import functools

import jax
import jax.numpy as jnp
import numpy as np
from jax import lax
from jax.experimental import pallas as pl
from jax.experimental.pallas import tpu as pltpu
from jax.sharding import PartitionSpec as P

HEAD_DIM = 128
ROPE_THETA = 1000000.0
NORM_EPS = 1e-6
SM_SCALE = HEAD_DIM ** -0.5
EXP_SCALE = SM_SCALE * 1.4426950408889634
F32, BF16 = jnp.float32, jnp.bfloat16
MESH = pl.DeviceIdType.MESH
PAIR = range(2)

ORDER = (43817265, 48172635)
GATHER = (3, 2, 229, 292, 519, 550, 585, 595, 616, 658, 683, 693, 682, 724, 823, 822, 1016, 1049, 1178, 1179)
REDUCE = (400, 402, 654, 652, 717, 719, 970, 971, 1097, 1158, 1223, 1392, 1394, 1477, 1647, 1646, 1709, 1667, 1708, 1899, 1962,
    2089, 2598, 2791, 2789, 3171, 3201, 3233)
GATHER_RIGHT = (34444334, 34344333, 443, 4333)
GATHER_LEFT = (43333443, 43433444, 1234334, 1233444)
REDUCE_RIGHT = (43434433, 33444334, 1233344, 1233443)
REDUCE_LEFT = (34343344, 44333443, 4433, 4334)
PREP_TOKENS = 32


def digits(numbers):
    return [int(c) for n in numbers for c in str(n).zfill(8)]


GATHER_REACH = (digits(GATHER_RIGHT), digits(GATHER_LEFT))
REDUCE_REACH = (digits(REDUCE_RIGHT), digits(REDUCE_LEFT))
GATHER_AT = [n // 32 for n in GATHER]
GATHER_CODE = [n % 32 for n in GATHER]
REDUCE_AT = [n // 64 for n in REDUCE]
REDUCE_CODE = [n % 64 for n in REDUCE]
SLOTS = [[4 * int(d) + j for d in str(order) for j in range(3 if d == '4' else 2)] for order in ORDER]


def dot(a, b, ca, cb):
    return lax.dot_general(a, b, (((ca,), (cb,)), ((), ())), preferred_element_type=F32)


def lane_sum(x):
    return jnp.sum(x, axis=-1, keepdims=True)


def lane_mean(x):
    return lane_sum(x) * (1.0 / HEAD_DIM)


def roll_half(x):
    return pltpu.roll(x, HEAD_DIM // 2, axis=x.ndim - 1)


def row_sum(prod, ones):
    high = prod.astype(BF16)
    low = (prod - high.astype(F32)).astype(BF16)
    return dot(jnp.concatenate([high, low], 1), ones, 1, 0)


def select_const(index, values):
    if len(values) == 1:
        return jnp.int32(values[0])
    top = 1 << ((len(values) - 1).bit_length() - 1)
    low, high = select_const(index, values[:top]), select_const(index, values[top:])
    return jnp.where((index & top) != 0, high, low)


def packed(index, values, bits):
    per, shift = (4, 2) if bits > 3 else (8, 3)
    words = []
    for i in range(0, len(values), per):
        words.append(sum(v << (bits * k) for k, v in enumerate(values[i:i + per])))
    return (select_const(index >> shift, words) >> ((index & (per - 1)) * bits)) & ((1 << bits) - 1)


def split(code, *bits):
    out = []
    for b in reversed(bits):
        out.append(code & ((1 << b) - 1))
        code = code >> b
    return out[::-1]


def action_masks(nz, sequence, active):
    words = []
    for direction in PAIR:
        chips = [[int(active(direction, zz, *act)) for act in sequence] for zz in range(nz)]
        words.append([[sum(bit << k for k, bit in enumerate(c[i:i + 16])) for c in chips] for i in range(0, len(sequence), 16)])
    return words


def count_at(table, last):
    return [sum(1 for at in table if at == g) for g in range(last)]


def mega_kernel(nz, chunk, per_kv, kv_heads,
                q_hbm, do_hbm, out_hbm, lse_hbm, k_hbm, v_hbm, offc3_hbm, offs3_hbm, offc_hbm, offs_hbm, basec_ref, bases_ref, qw_ref, kw_ref,
                dq_hbm, dkv_hbm, w_ref,
                xq, xdo, xout, qb_a, qb_b, aux_a, aux_b, dq, dq_b, kvall, acc, rsb, kland, lland, pieces, cos_t, sin_t, cos_d, sin_d, kout, dwq, wmine, wslots,
                in_sem, sw_snd, sw_rcv, ld_sem, xs_sem, xr_sem, tab_sem,
                ag_send, ag_recv, rs_send, rs_recv, dq_loc, dq_snd, dq_rcv, dk_loc, dk_snd, dk_rcv, w_snd, w_rcv):
    me = lax.axis_index('cp')
    cp = 2 * nz
    z, core = me // 2, me % 2
    other = 1 - core
    sib = 2 * z + other
    right = 2 * lax.rem(z + 1, nz) + core
    left = 2 * lax.rem(z + nz - 1, nz) + core
    tok = 2 * chunk
    rows = tok * per_kv
    qb, aux, dqs = (qb_a, qb_b), (aux_a, aux_b), (dq, dq_b)
    k_rows = tok * kv_heads

    def wrap(i):
        return (i + 2 * nz) & (nz - 1)

    def to(device):
        return dict(device_id={'cp': device}, device_id_type=MESH)

    barrier = pltpu.get_barrier_semaphore()

    def say(i, carry):
        pl.semaphore_signal(barrier, inc=1, **to(lax.rem(me + i, cp)))
        return carry

    lax.fori_loop(1, cp, say, 0)

    def off_of(el, mine):
        return pl.multiple_of((core if (el == 0) == mine else other) * chunk, chunk)

    def x_rows(h, el, token, count):
        return pl.ds(pl.multiple_of(((h * 2 + el) * tok + token) * per_kv, chunk), count * per_kv)

    def h_rows(el, token, count):
        return pl.ds(pl.multiple_of((el * tok + token) * per_kv, chunk), count * per_kv)

    lands = ((k_hbm, kland.at[0]), (v_hbm, kland.at[1]), (lse_hbm, lland))
    own_in = [pltpu.make_async_copy(hbm, buf.at[0], in_sem.at[i]) for i, (hbm, buf) in enumerate(lands)]
    swaps = [pltpu.make_async_remote_copy(hbm, buf.at[1], sw_snd.at[i], sw_rcv.at[i], **to(sib)) for i, (hbm, buf) in enumerate(lands)]
    tables = [pltpu.make_async_copy(src, dst, tab_sem.at[i]) for i, (src, dst) in enumerate((
        (offc_hbm, cos_d.at[pl.ds(0, tok)]), (offs_hbm, sin_d.at[pl.ds(0, tok)]),
        (offc3_hbm, cos_t.at[pl.ds(0, tok)]), (offs3_hbm, sin_t.at[pl.ds(0, tok)])))]
    loads = []
    for h in PAIR:
        for el in PAIR:
            heads = lambda c: pl.ds(pl.multiple_of((2 * c + h) * per_kv, per_kv), per_kv)
            src = pl.ds(el * chunk, chunk)
            dst = x_rows(h, el, off_of(el, True), chunk)
            row = []
            for i, (hbm, buf) in enumerate(((q_hbm, xq), (do_hbm, xdo), (out_hbm, xout))):
                there = buf.at[dst].reshape(chunk, per_kv, HEAD_DIM)
                row.append((pltpu.make_async_copy(hbm.at[src, heads(core), :], there, ld_sem.at[h, el, i]),
                            pltpu.make_async_remote_copy(hbm.at[src, heads(other), :], there, xs_sem.at[h, el, i], xr_sem.at[h, el, i],
                                                         **to(sib))))
            loads.append(row)
    for cpy in own_in + tables:
        cpy.start()
    for row in loads:
        for loc, _ in row:
            loc.start()
    acc[...] = jnp.zeros_like(acc)
    dq_b[...] = jnp.zeros_like(dq_b)

    def base(el):
        blk = z if el == 0 else 2 * nz - 1 - z
        return basec_ref[blk], bases_ref[blk]

    def turn(cos_ref, sin_ref, lift):
        for el in (1, 0):
            bc, bs = base(el)
            bc, bs = lift(bc), lift(bs)
            step = 32

            def part(i, carry):
                src = pl.ds(pl.multiple_of(i * step, step), step)
                dst = pl.ds(pl.multiple_of(el * tok + i * step, step), step)
                oc, os = cos_ref[src], sin_ref[src]
                cos_ref[dst] = bc * oc - bs * os
                sin_ref[dst] = bs * oc + bc * os
                return carry

            lax.fori_loop(0, tok // step, part, 0)

    for t in tables:
        t.wait()
    turn(cos_d, sin_d, lambda x: x)
    turn(cos_t, sin_t, lambda x: x[:, None, :])

    def raw_rows(what, side):
        return pl.ds((what * 2 + side) * k_rows, k_rows)

    def raw(what, side, h, el):
        return dq[pl.ds((what * 2 + side) * k_rows + el * chunk * kv_heads + 2 * core + h, chunk, stride=kv_heads), :]

    def unpack_keys(what, side):
        dq[raw_rows(what, side), :] = kland[what, side].astype(F32)

    kw = kw_ref[...]

    def keys_of(side):
        for i in PAIR:
            unpack_keys(i, side)
        for h in PAIR:
            for el in PAIR:
                off = off_of(el, side == 0)
                x = raw(0, side, h, el)
                y = x * lax.rsqrt(lane_mean(x * x) + NORM_EPS) * kw
                tabs = pl.ds(pl.multiple_of(el * tok + off, chunk), chunk)
                kvall[z, h, el, 0, pl.ds(off, chunk), :] = (y * cos_d[tabs] + roll_half(y) * sin_d[tabs]).astype(BF16)
                kvall[z, h, el, 1, pl.ds(off, chunk), :] = raw(1, side, h, el).astype(BF16)

    n_l = 3 * per_kv
    lane_c = lax.broadcasted_iota(jnp.int32, (chunk, HEAD_DIM), 1)

    def pieces_of(side):
        for h in PAIR:
            for el in PAIR:
                val = lland[side, pl.ds(el * chunk, chunk), :] * (-1.0 / SM_SCALE)
                val = jnp.concatenate([val, jnp.zeros((chunk, HEAD_DIM - val.shape[1]), F32)], axis=1)
                val = pltpu.roll(val, (HEAD_DIM - (2 * core + h) * per_kv) & (HEAD_DIM - 1), axis=1)
                hi = val.astype(BF16).astype(F32)
                mid = (val - hi).astype(BF16).astype(F32)
                low = val - hi - mid
                pc = jnp.where(lane_c < per_kv, hi, jnp.where(lane_c < 2 * per_kv, pltpu.roll(mid, per_kv, axis=1),
                               jnp.where(lane_c < n_l, pltpu.roll(low, 2 * per_kv, axis=1), 0.0)))
                pieces[h, pl.ds(pl.multiple_of(el * tok + off_of(el, side == 0), chunk), chunk)] = pc[:, None, :]

    for cpy in own_in:
        cpy.wait()
    keys_of(0)
    pieces_of(0)
    pl.semaphore_wait(barrier, cp - 1)
    for cpy in swaps:
        cpy.start()
    for row in loads:
        for _, rem in row:
            rem.start()
    for i in PAIR:
        swaps[i].wait_recv()
    keys_of(1)

    def lives(reach, el, h, hop, owner):
        return 1 <= hop <= reach[(el * 2 + h) * nz + owner % nz]

    sides = (1, -1)
    g_seq, r_seq = [split(c, 1, 3, 1) for c in GATHER_CODE], [split(c, 1, 3, 1, 1) for c in REDUCE_CODE]
    g_wait, g_send, r_wait, r_send = (
        [[select_const(z, w) for w in words] for words in action_masks(nz, seq, active)] for seq, active in (
            (g_seq, lambda dr, zz, h, s, el: lives(GATHER_REACH[dr], el, h, s - 1, zz - sides[dr] * (s - 1))),
            (g_seq, lambda dr, zz, h, s, el: lives(GATHER_REACH[dr], el, h, s, zz - sides[dr] * (s - 1))),
            (r_seq, lambda dr, zz, h, d, el, on: on and lives(REDUCE_REACH[dr], el, h, d + 1, zz + sides[dr] * d)),
            (r_seq, lambda dr, zz, h, d, el, on: lives(REDUCE_REACH[dr], el, h, d, zz + sides[dr] * d)
             and on == lives(REDUCE_REACH[dr], el, h, d + 1, zz + sides[dr] * d))))

    def on(words, index):
        word = words[0]
        for i, w in enumerate(words[1:], 1):
            word = jnp.where(index >> 4 == i, w, word)
        return (word >> (index & 15)) & 1 == 1

    def gather_owner(direction, s):
        return wrap(z - sides[direction] * s)

    def gather_copy(direction, h, s, el):
        ref = kvall.at[gather_owner(direction, s - 1), h, el]
        return pltpu.make_async_remote_copy(ref, ref, ag_send.at[direction, h, s - 1, el], ag_recv.at[direction, h, s - 1, el],
                                            **to((right, left)[direction]))

    def gather_arrival(direction, h, s, el):
        ref = kvall.at[gather_owner(direction, s), h, el]
        return pltpu.make_async_remote_copy(ref, ref, ag_send.at[direction, h, s - 1, el], ag_recv.at[direction, h, s - 1, el],
                                            **to((right, left)[direction]))

    def gather_step(a):
        h, s, el = split(packed(a, GATHER_CODE, 5), 1, 3, 1)
        for direction in PAIR:
            @pl.when(on(g_wait[direction], a))
            def _():
                gather_arrival(direction, h, s - 1, el).wait_recv()

            @pl.when(on(g_send[direction], a))
            def _():
                gather_copy(direction, h, s, el).start()

    def reduce_copy(direction, h, d, el):
        return pltpu.make_async_remote_copy(acc.at[wrap(z + sides[direction] * d), h, el], rsb.at[direction, d - 1, h, el],
                                            rs_send.at[direction, d - 1, h, el], rs_recv.at[direction, d - 1, h, el],
                                            **to((right, left)[direction]))

    def reduce_arrival(direction, h, d, el):
        return pltpu.make_async_remote_copy(acc.at[wrap(z + sides[direction] * d), h, el], rsb.at[direction, d, h, el],
                                            rs_send.at[direction, d, h, el], rs_recv.at[direction, d, h, el],
                                            **to((right, left)[direction]))

    def reduce_step(b):
        h, d, el, _ = split(packed(b, REDUCE_CODE, 6), 1, 3, 1, 1)
        for direction in PAIR:
            @pl.when(on(r_wait[direction], b))
            def _():
                reduce_arrival(direction, h, d, el).wait_recv()
                acc[wrap(z + sides[direction] * d), h, el] += rsb[direction, d, h, el]

            @pl.when(on(r_send[direction], b))
            def _():
                reduce_copy(direction, h, d, el).start()

    def run_actions(step, first, count):
        def one(i, carry):
            step(i)
            return carry

        lax.fori_loop(first, first + count, one, 0)
        return first + count

    head_steps = 3 + 2 * (nz - 1)
    n_steps = 2 * head_steps
    n_pieces = 2 * tok // PREP_TOKENS
    first = n_pieces + 1
    n_ticks = n_steps + n_pieces
    gather_counts = count_at(GATHER_AT, first + n_ticks)
    reduce_counts = count_at(REDUCE_AT, n_ticks)

    def ticks(g, done):
        ga = run_actions(gather_step, done[0], packed(first + g, gather_counts, 3))
        ra = run_actions(reduce_step, done[1], packed(g, reduce_counts, 4))
        return ga, ra

    gathered = run_actions(gather_step, 0, gather_counts[0])

    dq[...] = jnp.zeros_like(dq)

    swaps[2].wait_recv()
    pieces_of(1)

    sub = PREP_TOKENS
    weight = qw_ref[...]
    ones = jnp.ones((2 * HEAD_DIM, HEAD_DIM), BF16)
    lane = lax.broadcasted_iota(jnp.int32, (sub * per_kv, HEAD_DIM), 1)
    head = lax.rem(lax.broadcasted_iota(jnp.int32, (sub * per_kv, HEAD_DIM), 0), per_kv)
    lse_mask = (lane == head) | (lane == head + per_kv) | (lane == head + 2 * per_kv)
    flat = lambda x: x.reshape(x.shape[0] * per_kv, HEAD_DIM)
    tall = lambda x: x.reshape(x.shape[0] // per_kv, per_kv, HEAD_DIM)

    def sums(prod, on_mxu):
        return row_sum(prod, ones) if on_mxu else lane_sum(prod)

    def prepare(h, el, t0, on_mxu):
        tabs = pl.ds(pl.multiple_of(el * tok + t0, sub), sub)
        r = x_rows(h, el, t0, sub)
        x = xq[r, :].astype(F32)
        ms = sums(x * x, on_mxu) * (1.0 / HEAD_DIM)
        y = tall(x * lax.rsqrt(ms + NORM_EPS) * weight)
        hr = h_rows(el, t0, sub)
        qb[h][hr, :] = flat(y * cos_t[tabs] + roll_half(y) * sin_t[tabs]).astype(BF16)
        r0 = -sums(xdo[r, :].astype(F32) * xout[r, :].astype(F32), on_mxu)
        r1 = r0 - r0.astype(BF16).astype(F32)
        r2 = r1 - r1.astype(BF16).astype(F32)
        dpart = jnp.where(lane == n_l, r0, jnp.where(lane == n_l + 1, r1, jnp.where(lane == n_l + 2, r2, 0.0)))
        consts = flat(jnp.broadcast_to(pieces[h, tabs], (sub, per_kv, HEAD_DIM)))
        aux[h][hr, :] = jnp.where(lse_mask, consts, dpart).astype(BF16)

    def finish(h, el, t0, on_mxu):
        tabs = pl.ds(pl.multiple_of(el * tok + t0, sub), sub)
        r = x_rows(h, el, t0, sub)
        x = xq[r, :].astype(F32)
        rstd = lax.rsqrt(sums(x * x, on_mxu) * (1.0 / HEAD_DIM) + NORM_EPS)
        xhat = x * rstd
        hr = h_rows(el, t0, sub)
        gq = tall(dqs[h][hr, :] * SM_SCALE)
        dy = flat(gq * cos_t[tabs] - roll_half(gq) * sin_t[tabs])
        dxh = dy * weight
        qb[h][hr, :] = (rstd * (dxh - xhat * lane_mean(dxh * xhat))).astype(BF16)
        return jnp.sum((dy * xhat).reshape(-1, 8, HEAD_DIM), axis=0)

    def piece_at(i):
        el = jnp.where(i >= n_pieces // 2, 1, 0)
        return el, (i - el * (n_pieces // 2)) * sub

    for part in PAIR:
        for el in PAIR:
            for loc, rem in loads[el]:
                if part == 0:
                    loc.wait()
                else:
                    rem.wait_recv()
        n = chunk // sub

        def piece(i, gathered):
            el = jnp.where(i >= n, 1, 0)
            mine = core if part == 0 else other
            prepare(0, el, jnp.where(el == 0, mine, 1 - mine) * chunk + (i - el * n) * sub, True)
            return run_actions(gather_step, gathered, packed(1 + part * 2 * n + i, gather_counts, 3))

        gathered = lax.fori_loop(0, 2 * n, piece, gathered)
    for el in PAIR:
        for loc, rem in loads[2 + el]:
            loc.wait()
            rem.wait_recv()
    dwq[...] = jnp.zeros_like(dwq)

    keys = tok
    klane = lax.broadcasted_iota(jnp.int32, (keys, HEAD_DIM), 1)
    ones_k = jnp.where(klane < n_l, 1.0, 0.0).astype(BF16)
    ones_v = jnp.where((klane >= n_l) & (klane < n_l + 3), 1.0, 0.0).astype(BF16)
    klan = lax.broadcasted_iota(jnp.int32, (per_kv, keys), 1)

    def work(h, g, done):
        u = g - h * head_steps
        slot = packed(u, SLOTS[h], 6)
        delta, j = (slot >> 2) - 4, slot & 3
        own = delta == 0
        kz = wrap(z + delta)
        lower = kz < z
        q_late = jnp.where(own, jnp.where(j >= 1, 1, 0), jnp.where(lower, j, 1))
        k_late = jnp.where(own, jnp.where(j >= 2, 1, 0), jnp.where(lower, 0, j))
        q_blk = jnp.where(q_late == 1, 2 * nz - 1 - z, z)
        k_blk = jnp.where(k_late == 1, 2 * nz - 1 - kz, kz)
        off = (q_blk - k_blk) * tok
        r = pl.ds(pl.multiple_of((h * 2 + q_late) * rows, rows), rows)
        k, v = kvall[kz, h, k_late, 0], kvall[kz, h, k_late, 1]
        hr = pl.ds(pl.multiple_of(q_late * rows, rows), rows)
        qq, ax, dd = qb[h][hr, :], aux[h][hr, :], xdo[r, :]
        s = dot(jnp.concatenate([qq, ax], 1), jnp.concatenate([k, ones_k], 1), 1, 1)
        dp = dot(jnp.concatenate([dd, ax], 1), jnp.concatenate([v, ones_v], 1), 1, 1)
        p = jnp.exp2(s * EXP_SCALE)
        p = jnp.concatenate([jnp.where(klan <= off + t, p[per_kv * t:per_kv * (t + 1)], 0.0) for t in range(tok)], 0)
        ds = (p * dp).astype(BF16)
        pb = p.astype(BF16)
        dqs[h][hr, :] += dot(ds, k, 1, 0)
        acc[kz, h, k_late, 0] += dot(qq, ds, 0, 0)
        acc[kz, h, k_late, 1] += dot(dd, pb, 0, 0)
        el, t0 = piece_at(jnp.minimum(u, n_pieces - 1))
        if h == 0:
            prepare(1, el, t0, False)
        else:
            dwq[...] += jnp.where(u < n_pieces, finish(0, el, t0, False), 0.0)
        return ticks(g, done)

    done = (gathered, jnp.int32(0))
    for h in PAIR:
        done = lax.fori_loop(h * head_steps, (h + 1) * head_steps, functools.partial(work, h), done)

    def last(i, done):
        el, t0 = piece_at(i)
        dwq[...] += finish(1, el, t0, True)
        return ticks(n_steps + i, done)

    done = lax.fori_loop(0, n_pieces, last, done)

    def back(x, ssum, g, cos, sin, w):
        rstd = lax.rsqrt(ssum * (1.0 / HEAD_DIM) + NORM_EPS)
        xhat = x * rstd
        dy = g * cos - roll_half(g) * sin
        dxh = dy * w
        dx = rstd * (dxh - xhat * lane_mean(dxh * xhat))
        return dx, jnp.sum((dy * xhat).reshape(-1, 8, HEAD_DIM), axis=0)

    outs = []
    for h in PAIR:
        for el in PAIR:
            heads = pl.ds(pl.multiple_of((2 * core + h) * per_kv, per_kv), per_kv)
            dst = dq_hbm.at[pl.ds(el * chunk, chunk), heads, :]
            part = lambda mine: qb[h].at[h_rows(el, off_of(el, mine), chunk)].reshape(chunk, per_kv, HEAD_DIM)
            outs.append((pltpu.make_async_copy(part(True), dst, dq_loc.at[h, el]),
                         pltpu.make_async_remote_copy(part(False), dst, dq_snd.at[h, el], dq_rcv.at[h, el], **to(sib))))
    for loc, rem in outs:
        loc.start()
        rem.start()
    for side in PAIR:
        unpack_keys(0, side)

    run_actions(reduce_step, done[1], len(REDUCE) - done[1])

    hold = 4 * k_rows
    dwk = jnp.zeros((8, HEAD_DIM), F32)
    for h in PAIR:
        for el in PAIR:
            kout[h, el, 1] = acc[z, h, el, 1].T.astype(BF16)
            dq[pl.ds(hold, tok), :] = acc[z, h, el, 0].T * SM_SCALE
            for side in PAIR:
                off = off_of(el, side == 0)
                x = raw(0, side, h, el)
                tabs = pl.ds(pl.multiple_of(el * tok + off, chunk), chunk)
                dx, dwp = back(x, lane_sum(x * x), dq[pl.ds(pl.multiple_of(hold + off, chunk), chunk), :],
                               cos_d[tabs], sin_d[tabs], kw)
                kout[h, el, 0, pl.ds(off, chunk), :] = dx.astype(BF16)
                dwk = dwk + dwp
            hold += tok
    top = lax.broadcasted_iota(jnp.int32, (8, HEAD_DIM), 0)
    wmine[...] = jnp.where(top == 0, jnp.sum(dwq[...], axis=0, keepdims=True),
                           jnp.where(top == 1, jnp.sum(dwk, axis=0, keepdims=True), 0.0))

    def weight_copy(i):
        return pltpu.make_async_remote_copy(wmine, wslots.at[cp - i], w_snd.at[i], w_rcv.at[cp - i], **to(lax.rem(me + i, cp)))

    def weight_send(i, carry):
        weight_copy(i).start()
        return carry

    lax.fori_loop(1, cp, weight_send, 0)
    for h in PAIR:
        for el in PAIR:
            dst = dkv_hbm.at[2 * core + h, el]
            outs.append((pltpu.make_async_copy(kout.at[h, el, :, pl.ds(off_of(el, True), chunk), :], dst, dk_loc.at[h, el]),
                         pltpu.make_async_remote_copy(kout.at[h, el, :, pl.ds(off_of(el, False), chunk), :], dst, dk_snd.at[h, el],
                                                      dk_rcv.at[h, el], **to(sib))))
    for loc, rem in outs[4:]:
        loc.start()
        rem.start()

    for cpy in swaps:
        cpy.wait_send()
    for row in loads:
        for _, rem in row:
            rem.wait_send()

    def drain_gather(a, carry):
        h, s, el = split(packed(a, GATHER_CODE, 5), 1, 3, 1)
        for direction in PAIR:
            @pl.when(on(g_send[direction], a))
            def _():
                gather_copy(direction, h, s, el).wait_send()
        return carry

    def drain_reduce(b, carry):
        h, d, el, _ = split(packed(b, REDUCE_CODE, 6), 1, 3, 1, 1)
        for direction in PAIR:
            @pl.when(on(r_send[direction], b))
            def _():
                reduce_copy(direction, h, d, el).wait_send()
        return carry

    lax.fori_loop(0, len(GATHER), drain_gather, 0)
    lax.fori_loop(0, len(REDUCE), drain_reduce, 0)

    def weight_wait(i, carry):
        pltpu.make_async_remote_copy(wmine, wslots.at[i], w_snd.at[i], w_rcv.at[i], **to(lax.rem(me + i, cp))).wait()
        return carry

    lax.fori_loop(1, cp, weight_wait, 0)
    wslots[0] = wmine[...]
    w_ref[...] = lax.fori_loop(0, cp, lambda i, total: total + wslots[lax.rem(i - me + cp, cp)], jnp.zeros((8, HEAD_DIM), F32))
    for loc, rem in outs:
        loc.wait()
        rem.wait()


def mega(nz, kv_heads, q_raw, d_out, out_fwd, lse, k_rows, v_rows, offc, offs, basec, bases, qw, kw):
    tok, heads, hd = q_raw.shape
    chunk, per_kv = tok // 2, heads // kv_heads
    any_spec = pl.BlockSpec(memory_space=pl.ANY)
    vmem = pl.BlockSpec(memory_space=pltpu.VMEM)
    dma, scr = pltpu.SemaphoreType.DMA, pltpu.VMEM
    n_rows = 2 * tok * per_kv
    hbm = lambda a: pltpu.with_memory_space_constraint(a, pltpu.HBM)
    args = [q_raw, d_out, out_fwd, lse, k_rows, v_rows, offc[:, None], offs[:, None], offc, offs]
    return pl.pallas_call(
        functools.partial(mega_kernel, nz, chunk, per_kv, kv_heads),
        in_specs=[any_spec] * len(args) + [vmem] * 4,
        out_specs=[any_spec, any_spec, vmem],
        out_shape=[jax.ShapeDtypeStruct(q_raw.shape, BF16), jax.ShapeDtypeStruct((kv_heads, 2, 2, chunk, hd), BF16),
                   jax.ShapeDtypeStruct((8, hd), F32)],
        scratch_shapes=[
            *[scr((2 * n_rows, hd), BF16)] * 3, *[scr((n_rows, hd), BF16)] * 4, *[scr((n_rows, hd), F32)] * 2,
            scr((nz, 2, 2, 2, tok, hd), BF16), scr((nz, 2, 2, 2, hd, tok), F32), scr((2, 4, 2, 2, 2, hd, tok), F32),
            scr((2, 2) + k_rows.shape, BF16), scr((2,) + lse.shape, F32), scr((2, 2 * tok, 1, hd), F32),
            *[scr((2 * tok, 1, hd), F32)] * 2, *[scr((2 * tok, hd), F32)] * 2,
            scr((2, 2, 2, tok, hd), BF16), *[scr((8, hd), F32)] * 2, scr((2 * nz, 8, hd), F32),
            *[dma((3,))] * 3, *[dma((2, 2, 3))] * 3, dma((4,)), *[dma((2, 2, 4, 2))] * 2, *[dma((2, 4, 2, 2))] * 2,
            *[dma((2, 2))] * 6, *[dma((2 * nz,))] * 2,
        ],
        name='attn_bwd',
        compiler_params=pltpu.CompilerParams(vmem_limit_bytes=67000000, collective_id=0, has_side_effects=True),
    )(*[hbm(a) for a in args], basec, bases, qw, kw)


def emit_kernel(dq_in, dkv_in, dq_out, dk_out, dv_out):
    dq_out[...] = dq_in[...]
    for ref, i in ((dk_out, 0), (dv_out, 1)):
        x = dkv_in[:, 0, i].astype(F32)
        ref[...] = jnp.stack([x[h] for h in range(x.shape[0])], axis=1).astype(BF16)


def emit(dq, dkv):
    tok, heads, hd = dq.shape
    kv_heads, _, _, chunk, _ = dkv.shape
    step = 32
    per = chunk // step
    return pl.pallas_call(
        emit_kernel,
        grid=(tok // step,),
        in_specs=[pl.BlockSpec((step, heads, hd), lambda i: (i, 0, 0)),
                  pl.BlockSpec((kv_heads, 1, 2, step, hd), lambda i: (0, i // per, 0, i % per, 0))],
        out_specs=[pl.BlockSpec((step, heads, hd), lambda i: (i, 0, 0)), pl.BlockSpec((step, kv_heads, hd), lambda i: (i, 0, 0)),
                   pl.BlockSpec((step, kv_heads, hd), lambda i: (i, 0, 0))],
        out_shape=[jax.ShapeDtypeStruct(dq.shape, BF16)] + [jax.ShapeDtypeStruct((tok, kv_heads, hd), BF16)] * 2,
        name='emit',
    )(dq, dkv)


def solution(mesh):
    cp_size = mesh.shape['cp']
    nz = cp_size // 2

    def local_grads(q_raw, k_raw, v_proj, out_fwd, lse_fwd, d_out, q_norm, k_norm):
        tok, kv_heads = k_raw.shape[0], k_raw.shape[1]
        inv_freq = ROPE_THETA ** (-np.arange(0, HEAD_DIM, 2, dtype=np.float64) / HEAD_DIM)
        inv_freq = np.concatenate([inv_freq, inv_freq])
        sign = np.where(np.arange(HEAD_DIM) < HEAD_DIM // 2, -1.0, 1.0)
        off_ang = np.arange(tok)[:, None] * inv_freq
        base_ang = (np.arange(cp_size) * tok)[:, None] * inv_freq
        table = lambda x: jnp.asarray(x, F32)
        rows = lambda a: a.reshape(tok * kv_heads, HEAD_DIM)
        dq_raw, dkv, sums = mega(nz, kv_heads, q_raw, d_out, out_fwd, lse_fwd, rows(k_raw), rows(v_proj),
                                 table(np.cos(off_ang)), table(np.sin(off_ang) * sign),
                                 table(np.cos(base_ang))[:, None], table(np.sin(base_ang) * sign)[:, None],
                                 q_norm.reshape(1, HEAD_DIM), k_norm.reshape(1, HEAD_DIM))
        dq_raw, dk_raw, dv = emit(dq_raw, dkv)
        return dq_raw, dk_raw, dv, sums[0], sums[1]

    row_spec = P(('dp', 'cp'))
    in_specs = (row_spec, row_spec, row_spec, row_spec, row_spec, row_spec, P(), P())
    out_specs = (row_spec, row_spec, row_spec, P('dp'), P('dp'))
    return jax.shard_map(local_grads, mesh=mesh, in_specs=in_specs, out_specs=out_specs, check_vma=False)
```

time: 919 us -> 151 us (0.16)
  matrix products: 230 us -> 0 us
  starting transfers between devices: 209 us -> 0 us
  local copies, waits for them, and re-layouts: 180 us -> 2.86 us
  other arithmetic: 151 us -> 0 us
  Pallas kernels: 0 us -> 147 us
  waiting for transfers between devices: 102 us -> 0 us
  blocking collectives: 35.6 us -> 0 us
    dot_general x90 -> x0, matrix products: 230 us -> none  [the longest x18 76.4 us: pair_grads(): jnp.einsum('qngd,knd->qngk', do_blk, v_blk, preferred_element_type=jnp.fl...]
    ppermute x62 -> x0, starting transfers between devices: 209 us -> none  [the longest x15 68 us: visit_source(): dk_cur = lax.ppermute(dk_cur, 'cp', shift_pairs)]
    pallas_call x0 -> x2, Pallas kernels: none -> 147 us  [the longest x1 141 us: mega(): pl.pallas_call(functools.partial(mega_kernel, nz, chunk, per_kv, kv_heads...]
    slice x52 -> x0, local copies, waits for them, and re-layouts: 107 us -> none  [the longest x14 68 us: late_source(): dq_acc[:chunk_len]]
    ppermute x62 -> x0, waiting for transfers between devices: 102 us -> none  [the longest x15 70.1 us: visit_source(): v_cur = lax.ppermute(v_cur, 'cp', shift_pairs)]
    concatenate x18 -> x0, other arithmetic: 94.5 us -> none  [the longest x14 87.8 us: late_source(): jnp.concatenate([dq_acc[:chunk_len], dq_acc[chunk_len:] + dq_part])]
    while x35 -> x0, local copies, waits for them, and re-layouts: 44.9 us -> none  [the longest x5 23.9 us: local_grads(): lax.fori_loop(1, cp_size, visit_source, (k_b, v_proj, dq_acc, dk_acc, dv_...]
    psum x1 -> x0, blocking collectives: 35.6 us -> none  [local_grads(): lax.psum(dq_weight, 'cp')]
  transfers between devices with their start and end apart: 62 -> 0, of which waited for: 29 -> 0; matrix products, arithmetic and copies ran while one was open for 6% -> 0% of each run, Pallas kernels for 0% -> 0%
where the time goes in v3:
time: 151 us
  Pallas kernels  147 us (97%)
  local copies, waits for them, and re-layouts  2.86 us (2%)
    pallas_call x1, Pallas kernels, mega(): pl.pallas_call(functools.partial(mega_kernel, nz, chunk, per_kv, kv_heads...  141 us
    pallas_call x1, Pallas kernels, emit(): pl.pallas_call(emit_kernel, grid=(tok // step,), in_specs=[pl.BlockSpec((...  6.71 us

profile of v3, /device:TPU:21, one launch (start us, length us, event | category | flops | bytes accessed | tf_op | source)
XLA Modules:
  0.0 150.8 jit_solution(14667268979763719912)
XLA Ops:
  0.6 1.6 %copy.17.lse_hbm = f32[256,64]{1,0:T(8,128)} copy(f32[256,64]{0,1:T(8,128)} %param.16) | data formatting | bytes 131072 | tf_op args[4]
  2.2 140.6 %attn_bwd.1 = (bf16[256,64,128]{2,1,0:T(8,128)(2,1)}, bf16[4,2,2,128,128]{4,3,2,1,0:T(8,128)(2,1)}, f32[8,128]{1,0:T(8,128)}) custom-call(bf16[256,64,128]{2,1,0:T(8,128)(2,1)} %q_hbm.1, bf16[256,64,128]{2,1,0:T(8,128)(2,1)} %do_hbm.1, bf16[256,64,128]{2,1,0:T(8,128)(2,1)} %out_hbm.1, f32[256,64]{1,0:T(8,128)} %copy.17.lse_hbm, bf16[1024,128]{1,0:T(8,128)(2,1)} %bitcast.8, ...), custom_call_target="tpu_custom_call" | custom-call | tf_op jit(solution)/shard_map/attn_bwd/pallas_call | solution.py:563
  142.8 6.7 %emit.1 = (bf16[256,64,128]{2,1,0:T(8,128)(2,1)}, bf16[256,4,128]{2,1,0:T(4,128)(2,1)}, bf16[256,4,128]{2,1,0:T(4,128)(2,1)}) custom-call(bf16[256,64,128]{2,1,0:T(8,128)(2,1)} %get-tuple-element.11.dq_in, bf16[4,2,2,128,128]{4,3,2,1,0:T(8,128)(2,1)} %get-tuple-element.12.dkv_in), custom_call_target="tpu_custom_call" | custom-call | tf_op jit(solution)/shard_map/emit/pallas_call | solution.py:595
  149.6 1.3 slice_bitcast_fusion

commit v4 on v3

--- a/solution.py
+++ b/solution.py
@@ -17,14 +17,16 @@
 MESH = pl.DeviceIdType.MESH
 PAIR = range(2)
 
-ORDER = (43817265, 48172635)
-GATHER = (3, 2, 229, 292, 519, 550, 585, 595, 616, 658, 683, 693, 682, 724, 823, 822, 1016, 1049, 1178, 1179)
-REDUCE = (400, 402, 654, 652, 717, 719, 970, 971, 1097, 1158, 1223, 1392, 1394, 1477, 1647, 1646, 1709, 1667, 1708, 1899, 1962,
-    2089, 2598, 2791, 2789, 3171, 3201, 3233)
-GATHER_RIGHT = (34444334, 34344333, 443, 4333)
-GATHER_LEFT = (43333443, 43433444, 1234334, 1233444)
-REDUCE_RIGHT = (43434433, 33444334, 1233344, 1233443)
-REDUCE_LEFT = (34343344, 44333443, 4433, 4334)
+ORDER = (46781235, 78136245)
+GATHER = (356001960000600070, 1674014820106000388, 2382023180218402120, 2578024720244402508, 2704027680264202664,
+    2982029880302802918, 3306031800303002964, 3566035680337003376, 4212040820401403892, 459804402)
+REDUCE = (1106010420078000650, 1614014170148701232, 2054018070186901678, 2505023150225102053, 2759026950260802674,
+    3246031170305202738, 3819035250350303311, 4073040100388303753, 5315048670496704645, 5861057980576105287, 6497063710617706209,
+    6435)
+GATHER_RIGHT = (33344444, 44444333, 333, 333)
+GATHER_LEFT = (44433333, 33333444, 1234444, 1234444)
+REDUCE_RIGHT = (33333333, 44444444, 1233444, 1234333)
+REDUCE_LEFT = (44444444, 33333333, 4333, 444)
 PREP_TOKENS = 32
 
 
@@ -34,10 +36,20 @@
 
 GATHER_REACH = (digits(GATHER_RIGHT), digits(GATHER_LEFT))
 REDUCE_REACH = (digits(REDUCE_RIGHT), digits(REDUCE_LEFT))
-GATHER_AT = [n // 32 for n in GATHER]
-GATHER_CODE = [n % 32 for n in GATHER]
-REDUCE_AT = [n // 64 for n in REDUCE]
-REDUCE_CODE = [n % 64 for n in REDUCE]
+
+
+def unpacked(numbers):
+    out = []
+    for n in numbers:
+        while n:
+            out.append(n % 100000)
+            n //= 100000
+    return out
+
+
+G_SEQ, R_SEQ = unpacked(GATHER), unpacked(REDUCE)
+GATHER_AT, GATHER_CODE = [n >> 7 for n in G_SEQ], [n & 127 for n in G_SEQ]
+REDUCE_AT, REDUCE_CODE = [n >> 7 for n in R_SEQ], [n & 127 for n in R_SEQ]
 SLOTS = [[4 * int(d) + j for d in str(order) for j in range(3 if d == '4' else 2)] for order in ORDER]
 
 
@@ -73,6 +85,7 @@
 
 def packed(index, values, bits):
     per, shift = (4, 2) if bits > 3 else (8, 3)
+    assert max(values) < 1 << bits
     words = []
     for i in range(0, len(values), per):
         words.append(sum(v << (bits * k) for k, v in enumerate(values[i:i + per])))
@@ -88,11 +101,8 @@
 
 
 def action_masks(nz, sequence, active):
-    words = []
-    for direction in PAIR:
-        chips = [[int(active(direction, zz, *act)) for act in sequence] for zz in range(nz)]
-        words.append([[sum(bit << k for k, bit in enumerate(c[i:i + 16])) for c in chips] for i in range(0, len(sequence), 16)])
-    return words
+    chips = [[int(active(zz, *act)) for act in sequence] for zz in range(nz)]
+    return [[sum(bit << k for k, bit in enumerate(c[i:i + 16])) for c in chips] for i in range(0, len(sequence), 16)]
 
 
 def count_at(table, last):
@@ -164,9 +174,6 @@
     for row in loads:
         for loc, _ in row:
             loc.start()
-    acc[...] = jnp.zeros_like(acc)
-    dq_b[...] = jnp.zeros_like(dq_b)
-
     def base(el):
         blk = z if el == 0 else 2 * nz - 1 - z
         return basec_ref[blk], bases_ref[blk]
@@ -190,7 +197,6 @@
     for t in tables:
         t.wait()
     turn(cos_d, sin_d, lambda x: x)
-    turn(cos_t, sin_t, lambda x: x[:, None, :])
 
     def raw_rows(what, side):
         return pl.ds((what * 2 + side) * k_rows, k_rows)
@@ -221,7 +227,7 @@
     def pieces_of(side):
         for h in PAIR:
             for el in PAIR:
-                val = lland[side, pl.ds(el * chunk, chunk), :] * (-1.0 / SM_SCALE)
+                val = (lland[side, :, pl.ds(el * chunk, chunk)] * (-1.0 / SM_SCALE)).T
                 val = jnp.concatenate([val, jnp.zeros((chunk, HEAD_DIM - val.shape[1]), F32)], axis=1)
                 val = pltpu.roll(val, (HEAD_DIM - (2 * core + h) * per_kv) & (HEAD_DIM - 1), axis=1)
                 hi = val.astype(BF16).astype(F32)
@@ -234,13 +240,13 @@
     for cpy in own_in:
         cpy.wait()
     keys_of(0)
-    pieces_of(0)
     pl.semaphore_wait(barrier, cp - 1)
     for cpy in swaps:
         cpy.start()
     for row in loads:
         for _, rem in row:
             rem.start()
+    acc[...] = jnp.zeros_like(acc)
     for i in PAIR:
         swaps[i].wait_recv()
     keys_of(1)
@@ -248,15 +254,17 @@
     def lives(reach, el, h, hop, owner):
         return 1 <= hop <= reach[(el * 2 + h) * nz + owner % nz]
 
-    sides = (1, -1)
-    g_seq, r_seq = [split(c, 1, 3, 1) for c in GATHER_CODE], [split(c, 1, 3, 1, 1) for c in REDUCE_CODE]
+    def sign(direction):
+        return 1 - 2 * direction
+
+    g_seq, r_seq = [split(c, 1, 1, 3, 1, 1) for c in GATHER_CODE], [split(c, 1, 1, 3, 1, 1) for c in REDUCE_CODE]
     g_wait, g_send, r_wait, r_send = (
-        [[select_const(z, w) for w in words] for words in action_masks(nz, seq, active)] for seq, active in (
-            (g_seq, lambda dr, zz, h, s, el: lives(GATHER_REACH[dr], el, h, s - 1, zz - sides[dr] * (s - 1))),
-            (g_seq, lambda dr, zz, h, s, el: lives(GATHER_REACH[dr], el, h, s, zz - sides[dr] * (s - 1))),
-            (r_seq, lambda dr, zz, h, d, el, on: on and lives(REDUCE_REACH[dr], el, h, d + 1, zz + sides[dr] * d)),
-            (r_seq, lambda dr, zz, h, d, el, on: lives(REDUCE_REACH[dr], el, h, d, zz + sides[dr] * d)
-             and on == lives(REDUCE_REACH[dr], el, h, d + 1, zz + sides[dr] * d))))
+        [select_const(z, w) for w in action_masks(nz, seq, active)] for seq, active in (
+            (g_seq, lambda zz, dr, h, s, el, _: lives(GATHER_REACH[dr], el, h, s - 1, zz - sign(dr) * (s - 1))),
+            (g_seq, lambda zz, dr, h, s, el, _: lives(GATHER_REACH[dr], el, h, s, zz - sign(dr) * (s - 1))),
+            (r_seq, lambda zz, dr, h, d, el, on: on and lives(REDUCE_REACH[dr], el, h, d + 1, zz + sign(dr) * d)),
+            (r_seq, lambda zz, dr, h, d, el, on: lives(REDUCE_REACH[dr], el, h, d, zz + sign(dr) * d)
+             and on == lives(REDUCE_REACH[dr], el, h, d + 1, zz + sign(dr) * d))))
 
     def on(words, index):
         word = words[0]
@@ -264,51 +272,51 @@
             word = jnp.where(index >> 4 == i, w, word)
         return (word >> (index & 15)) & 1 == 1
 
-    def gather_owner(direction, s):
-        return wrap(z - sides[direction] * s)
+    def neighbour(direction):
+        return to(jnp.where(direction == 0, right, left))
 
     def gather_copy(direction, h, s, el):
-        ref = kvall.at[gather_owner(direction, s - 1), h, el]
+        ref = kvall.at[wrap(z - sign(direction) * (s - 1)), h, el]
         return pltpu.make_async_remote_copy(ref, ref, ag_send.at[direction, h, s - 1, el], ag_recv.at[direction, h, s - 1, el],
-                                            **to((right, left)[direction]))
+                                            **neighbour(direction))
 
     def gather_arrival(direction, h, s, el):
-        ref = kvall.at[gather_owner(direction, s), h, el]
+        ref = kvall.at[wrap(z - sign(direction) * s), h, el]
         return pltpu.make_async_remote_copy(ref, ref, ag_send.at[direction, h, s - 1, el], ag_recv.at[direction, h, s - 1, el],
-                                            **to((right, left)[direction]))
+                                            **neighbour(direction))
 
     def gather_step(a):
-        h, s, el = split(packed(a, GATHER_CODE, 5), 1, 3, 1)
-        for direction in PAIR:
-            @pl.when(on(g_wait[direction], a))
-            def _():
-                gather_arrival(direction, h, s - 1, el).wait_recv()
-
-            @pl.when(on(g_send[direction], a))
-            def _():
-                gather_copy(direction, h, s, el).start()
+        direction, h, s, el, _ = split(packed(a, GATHER_CODE, 7), 1, 1, 3, 1, 1)
+
+        @pl.when(on(g_wait, a))
+        def _():
+            gather_arrival(direction, h, s - 1, el).wait_recv()
+
+        @pl.when(on(g_send, a))
+        def _():
+            gather_copy(direction, h, s, el).start()
 
     def reduce_copy(direction, h, d, el):
-        return pltpu.make_async_remote_copy(acc.at[wrap(z + sides[direction] * d), h, el], rsb.at[direction, d - 1, h, el],
+        return pltpu.make_async_remote_copy(acc.at[wrap(z + sign(direction) * d), h, el], rsb.at[direction, d - 1, h, el],
                                             rs_send.at[direction, d - 1, h, el], rs_recv.at[direction, d - 1, h, el],
-                                            **to((right, left)[direction]))
+                                            **neighbour(direction))
 
     def reduce_arrival(direction, h, d, el):
-        return pltpu.make_async_remote_copy(acc.at[wrap(z + sides[direction] * d), h, el], rsb.at[direction, d, h, el],
+        return pltpu.make_async_remote_copy(acc.at[wrap(z + sign(direction) * d), h, el], rsb.at[direction, d, h, el],
                                             rs_send.at[direction, d, h, el], rs_recv.at[direction, d, h, el],
-                                            **to((right, left)[direction]))
+                                            **neighbour(direction))
 
     def reduce_step(b):
-        h, d, el, _ = split(packed(b, REDUCE_CODE, 6), 1, 3, 1, 1)
-        for direction in PAIR:
-            @pl.when(on(r_wait[direction], b))
-            def _():
-                reduce_arrival(direction, h, d, el).wait_recv()
-                acc[wrap(z + sides[direction] * d), h, el] += rsb[direction, d, h, el]
-
-            @pl.when(on(r_send[direction], b))
-            def _():
-                reduce_copy(direction, h, d, el).start()
+        direction, h, d, el, _ = split(packed(b, REDUCE_CODE, 7), 1, 1, 3, 1, 1)
+
+        @pl.when(on(r_wait, b))
+        def _():
+            reduce_arrival(direction, h, d, el).wait_recv()
+            acc[wrap(z + sign(direction) * d), h, el] += rsb[direction, d, h, el]
+
+        @pl.when(on(r_send, b))
+        def _():
+            reduce_copy(direction, h, d, el).start()
 
     def run_actions(step, first, count):
         def one(i, carry):
@@ -324,16 +332,20 @@
     first = n_pieces + 1
     n_ticks = n_steps + n_pieces
     gather_counts = count_at(GATHER_AT, first + n_ticks)
+    prep_counts = gather_counts[:1] + [a + b for a, b in zip(gather_counts[1:first:2], gather_counts[2:first:2])]
     reduce_counts = count_at(REDUCE_AT, n_ticks)
 
     def ticks(g, done):
-        ga = run_actions(gather_step, done[0], packed(first + g, gather_counts, 3))
+        ga = run_actions(gather_step, done[0], packed(first + g, gather_counts, 4))
         ra = run_actions(reduce_step, done[1], packed(g, reduce_counts, 4))
         return ga, ra
 
     gathered = run_actions(gather_step, 0, gather_counts[0])
 
+    turn(cos_t, sin_t, lambda x: x[:, None, :])
+    pieces_of(0)
     dq[...] = jnp.zeros_like(dq)
+    dq_b[...] = jnp.zeros_like(dq_b)
 
     swaps[2].wait_recv()
     pieces_of(1)
@@ -341,24 +353,27 @@
     sub = PREP_TOKENS
     weight = qw_ref[...]
     ones = jnp.ones((2 * HEAD_DIM, HEAD_DIM), BF16)
-    lane = lax.broadcasted_iota(jnp.int32, (sub * per_kv, HEAD_DIM), 1)
-    head = lax.rem(lax.broadcasted_iota(jnp.int32, (sub * per_kv, HEAD_DIM), 0), per_kv)
-    lse_mask = (lane == head) | (lane == head + per_kv) | (lane == head + 2 * per_kv)
+
+    def masks(count):
+        lane = lax.broadcasted_iota(jnp.int32, (count * per_kv, HEAD_DIM), 1)
+        head = lax.broadcasted_iota(jnp.int32, (count * per_kv, HEAD_DIM), 0) & (per_kv - 1)
+        return count, (lane == head) | (lane == head + per_kv) | (lane == head + 2 * per_kv), lane
+
     flat = lambda x: x.reshape(x.shape[0] * per_kv, HEAD_DIM)
     tall = lambda x: x.reshape(x.shape[0] // per_kv, per_kv, HEAD_DIM)
 
     def sums(prod, on_mxu):
         return row_sum(prod, ones) if on_mxu else lane_sum(prod)
 
-    def prepare(h, el, t0, on_mxu):
+    def prepare(h, el, t0, sub, lse_mask, lane):
         tabs = pl.ds(pl.multiple_of(el * tok + t0, sub), sub)
         r = x_rows(h, el, t0, sub)
         x = xq[r, :].astype(F32)
-        ms = sums(x * x, on_mxu) * (1.0 / HEAD_DIM)
+        ms = lane_mean(x * x)
         y = tall(x * lax.rsqrt(ms + NORM_EPS) * weight)
         hr = h_rows(el, t0, sub)
         qb[h][hr, :] = flat(y * cos_t[tabs] + roll_half(y) * sin_t[tabs]).astype(BF16)
-        r0 = -sums(xdo[r, :].astype(F32) * xout[r, :].astype(F32), on_mxu)
+        r0 = -lane_sum(xdo[r, :].astype(F32) * xout[r, :].astype(F32))
         r1 = r0 - r0.astype(BF16).astype(F32)
         r2 = r1 - r1.astype(BF16).astype(F32)
         dpart = jnp.where(lane == n_l, r0, jnp.where(lane == n_l + 1, r1, jnp.where(lane == n_l + 2, r2, 0.0)))
@@ -389,13 +404,13 @@
                     loc.wait()
                 else:
                     rem.wait_recv()
-        n = chunk // sub
+        n = chunk // (2 * sub)
 
         def piece(i, gathered):
             el = jnp.where(i >= n, 1, 0)
             mine = core if part == 0 else other
-            prepare(0, el, jnp.where(el == 0, mine, 1 - mine) * chunk + (i - el * n) * sub, True)
-            return run_actions(gather_step, gathered, packed(1 + part * 2 * n + i, gather_counts, 3))
+            prepare(0, el, jnp.where(el == 0, mine, 1 - mine) * chunk + (i - el * n) * 2 * sub, *masks(2 * sub))
+            return run_actions(gather_step, gathered, packed(1 + part * 2 * n + i, prep_counts, 4))
 
         gathered = lax.fori_loop(0, 2 * n, piece, gathered)
     for el in PAIR:
@@ -437,7 +452,7 @@
         acc[kz, h, k_late, 1] += dot(dd, pb, 0, 0)
         el, t0 = piece_at(jnp.minimum(u, n_pieces - 1))
         if h == 0:
-            prepare(1, el, t0, False)
+            prepare(1, el, t0, *masks(sub))
         else:
             dwq[...] += jnp.where(u < n_pieces, finish(0, el, t0, False), 0.0)
         return ticks(g, done)
@@ -475,69 +490,71 @@
     for side in PAIR:
         unpack_keys(0, side)
 
-    run_actions(reduce_step, done[1], len(REDUCE) - done[1])
-
-    hold = 4 * k_rows
-    dwk = jnp.zeros((8, HEAD_DIM), F32)
-    for h in PAIR:
-        for el in PAIR:
-            kout[h, el, 1] = acc[z, h, el, 1].T.astype(BF16)
-            dq[pl.ds(hold, tok), :] = acc[z, h, el, 0].T * SM_SCALE
-            for side in PAIR:
-                off = off_of(el, side == 0)
-                x = raw(0, side, h, el)
-                tabs = pl.ds(pl.multiple_of(el * tok + off, chunk), chunk)
-                dx, dwp = back(x, lane_sum(x * x), dq[pl.ds(pl.multiple_of(hold + off, chunk), chunk), :],
-                               cos_d[tabs], sin_d[tabs], kw)
-                kout[h, el, 0, pl.ds(off, chunk), :] = dx.astype(BF16)
-                dwk = dwk + dwp
-            hold += tok
-    top = lax.broadcasted_iota(jnp.int32, (8, HEAD_DIM), 0)
-    wmine[...] = jnp.where(top == 0, jnp.sum(dwq[...], axis=0, keepdims=True),
-                           jnp.where(top == 1, jnp.sum(dwk, axis=0, keepdims=True), 0.0))
-
-    def weight_copy(i):
-        return pltpu.make_async_remote_copy(wmine, wslots.at[cp - i], w_snd.at[i], w_rcv.at[cp - i], **to(lax.rem(me + i, cp)))
-
-    def weight_send(i, carry):
-        weight_copy(i).start()
+    def drain_gather(a, carry):
+        direction, h, s, el, _ = split(packed(a, GATHER_CODE, 7), 1, 1, 3, 1, 1)
+
+        @pl.when(on(g_send, a))
+        def _():
+            gather_copy(direction, h, s, el).wait_send()
+
         return carry
 
-    lax.fori_loop(1, cp, weight_send, 0)
-    for h in PAIR:
-        for el in PAIR:
-            dst = dkv_hbm.at[2 * core + h, el]
-            outs.append((pltpu.make_async_copy(kout.at[h, el, :, pl.ds(off_of(el, True), chunk), :], dst, dk_loc.at[h, el]),
-                         pltpu.make_async_remote_copy(kout.at[h, el, :, pl.ds(off_of(el, False), chunk), :], dst, dk_snd.at[h, el],
-                                                      dk_rcv.at[h, el], **to(sib))))
-    for loc, rem in outs[4:]:
-        loc.start()
-        rem.start()
-
+    lax.fori_loop(0, len(G_SEQ), drain_gather, 0)
     for cpy in swaps:
         cpy.wait_send()
     for row in loads:
         for _, rem in row:
             rem.wait_send()
 
-    def drain_gather(a, carry):
-        h, s, el = split(packed(a, GATHER_CODE, 5), 1, 3, 1)
-        for direction in PAIR:
-            @pl.when(on(g_send[direction], a))
-            def _():
-                gather_copy(direction, h, s, el).wait_send()
+    hold = 4 * k_rows
+
+    def key_gradients(h, dwk):
+        for el in PAIR:
+            kout[h, el, 1] = acc[z, h, el, 1].T.astype(BF16)
+            dq[pl.ds(hold, tok), :] = acc[z, h, el, 0].T * SM_SCALE
+            for s in PAIR:
+                off = off_of(el, s == 0)
+                x = raw(0, s, h, el)
+                tabs = pl.ds(pl.multiple_of(el * tok + off, chunk), chunk)
+                dx, dwp = back(x, lane_sum(x * x), dq[pl.ds(pl.multiple_of(hold + off, chunk), chunk), :], cos_d[tabs], sin_d[tabs], kw)
+                kout[h, el, 0, pl.ds(off, chunk), :] = dx.astype(BF16)
+                dwk = dwk + dwp
+            dst = dkv_hbm.at[2 * core + h, el]
+            both = (pltpu.make_async_copy(kout.at[h, el, :, pl.ds(off_of(el, True), chunk), :], dst, dk_loc.at[h, el]),
+                    pltpu.make_async_remote_copy(kout.at[h, el, :, pl.ds(off_of(el, False), chunk), :], dst, dk_snd.at[h, el],
+                                                 dk_rcv.at[h, el], **to(sib)))
+            outs.append(both)
+            for cpy in both:
+                cpy.start()
+        return dwk
+
+    assert all(at < n_ticks for at, (_, h, d, _, _) in zip(REDUCE_AT, r_seq) if h == 0 and d == 0)
+    dwk = key_gradients(0, jnp.zeros((8, HEAD_DIM), F32))
+    run_actions(reduce_step, done[1], len(R_SEQ) - done[1])
+    dwk = key_gradients(1, dwk)
+    top = lax.broadcasted_iota(jnp.int32, (8, HEAD_DIM), 0)
+    wmine[...] = jnp.where(top == 0, jnp.sum(dwq[...], axis=0, keepdims=True),
+                           jnp.where(top == 1, jnp.sum(dwk, axis=0, keepdims=True), 0.0))
+
+    def weight_copy(i):
+        return pltpu.make_async_remote_copy(wmine, wslots.at[cp - i], w_snd.at[i], w_rcv.at[cp - i], **to(lax.rem(me + i, cp)))
+
+    def weight_send(i, carry):
+        weight_copy(i).start()
         return carry
 
+    lax.fori_loop(1, cp, weight_send, 0)
+
     def drain_reduce(b, carry):
-        h, d, el, _ = split(packed(b, REDUCE_CODE, 6), 1, 3, 1, 1)
-        for direction in PAIR:
-            @pl.when(on(r_send[direction], b))
-            def _():
-                reduce_copy(direction, h, d, el).wait_send()
+        direction, h, d, el, _ = split(packed(b, REDUCE_CODE, 7), 1, 1, 3, 1, 1)
+
+        @pl.when(on(r_send, b))
+        def _():
+            reduce_copy(direction, h, d, el).wait_send()
+
         return carry
 
-    lax.fori_loop(0, len(GATHER), drain_gather, 0)
-    lax.fori_loop(0, len(REDUCE), drain_reduce, 0)
+    lax.fori_loop(0, len(R_SEQ), drain_reduce, 0)
 
     def weight_wait(i, carry):
         pltpu.make_async_remote_copy(wmine, wslots.at[i], w_snd.at[i], w_rcv.at[i], **to(lax.rem(me + i, cp))).wait()
@@ -580,28 +597,40 @@
     )(*[hbm(a) for a in args], basec, bases, qw, kw)
 
 
-def emit_kernel(dq_in, dkv_in, dq_out, dk_out, dv_out):
-    dq_out[...] = dq_in[...]
-    for ref, i in ((dk_out, 0), (dv_out, 1)):
-        x = dkv_in[:, 0, i].astype(F32)
-        ref[...] = jnp.stack([x[h] for h in range(x.shape[0])], axis=1).astype(BF16)
-
-
-def emit(dq, dkv):
-    tok, heads, hd = dq.shape
-    kv_heads, _, _, chunk, _ = dkv.shape
-    step = 32
-    per = chunk // step
+def emit_kernel(n, dq_in, dkv_in, w_in, dq_out, dk_out, dv_out, wq_out, wk_out, buf, in_sem, out_sem):
+    step = dq_in.shape[0] // n
+    part = lambda ref, i: ref.at[pl.ds(i * step, step)]
+    reads = [pltpu.make_async_copy(part(dq_in, i), part(buf, i), in_sem.at[i]) for i in range(n)]
+    writes = [pltpu.make_async_copy(part(buf, i), part(dq_out, i), out_sem.at[i]) for i in range(n)]
+    for cpy in reads:
+        cpy.start()
+    wq_out[...], wk_out[...] = w_in[0:1, :], w_in[1:2, :]
+    kv_heads, halves, _, chunk, _ = dkv_in.shape
+    for i in range(n):
+        reads[i].wait()
+        writes[i].start()
+        if i < 2 * halves:
+            ref, half, what = (dk_out, dv_out)[i & 1], i >> 1, i & 1
+            x = dkv_in[:, half, what].astype(F32)
+            ref[pl.ds(half * chunk, chunk)] = jnp.stack([x[h] for h in range(kv_heads)], axis=1).astype(BF16)
+    for cpy in writes:
+        cpy.wait()
+
+
+def emit(dq, dkv, weights):
+    tok, _, hd = dq.shape
+    kv_heads = dkv.shape[0]
+    n = 8
+    any_spec, vmem = pl.BlockSpec(memory_space=pl.ANY), pl.BlockSpec(memory_space=pltpu.VMEM)
     return pl.pallas_call(
-        emit_kernel,
-        grid=(tok // step,),
-        in_specs=[pl.BlockSpec((step, heads, hd), lambda i: (i, 0, 0)),
-                  pl.BlockSpec((kv_heads, 1, 2, step, hd), lambda i: (0, i // per, 0, i % per, 0))],
-        out_specs=[pl.BlockSpec((step, heads, hd), lambda i: (i, 0, 0)), pl.BlockSpec((step, kv_heads, hd), lambda i: (i, 0, 0)),
-                   pl.BlockSpec((step, kv_heads, hd), lambda i: (i, 0, 0))],
-        out_shape=[jax.ShapeDtypeStruct(dq.shape, BF16)] + [jax.ShapeDtypeStruct((tok, kv_heads, hd), BF16)] * 2,
+        functools.partial(emit_kernel, n),
+        in_specs=[any_spec, vmem, vmem],
+        out_specs=[any_spec] + [vmem] * 4,
+        out_shape=[jax.ShapeDtypeStruct(dq.shape, BF16)] + [jax.ShapeDtypeStruct((tok, kv_heads, hd), BF16)] * 2
+        + [jax.ShapeDtypeStruct((1, hd), F32)] * 2,
+        scratch_shapes=[pltpu.VMEM(dq.shape, BF16), *[pltpu.SemaphoreType.DMA((n,))] * 2],
         name='emit',
-    )(dq, dkv)
+    )(pltpu.with_memory_space_constraint(dq, pltpu.HBM), dkv, weights)
 
 
 def solution(mesh):
@@ -617,12 +646,12 @@
         base_ang = (np.arange(cp_size) * tok)[:, None] * inv_freq
         table = lambda x: jnp.asarray(x, F32)
         rows = lambda a: a.reshape(tok * kv_heads, HEAD_DIM)
-        dq_raw, dkv, sums = mega(nz, kv_heads, q_raw, d_out, out_fwd, lse_fwd, rows(k_raw), rows(v_proj),
+        dq_raw, dkv, sums = mega(nz, kv_heads, q_raw, d_out, out_fwd, lse_fwd.T, rows(k_raw), rows(v_proj),
                                  table(np.cos(off_ang)), table(np.sin(off_ang) * sign),
                                  table(np.cos(base_ang))[:, None], table(np.sin(base_ang) * sign)[:, None],
                                  q_norm.reshape(1, HEAD_DIM), k_norm.reshape(1, HEAD_DIM))
-        dq_raw, dk_raw, dv = emit(dq_raw, dkv)
-        return dq_raw, dk_raw, dv, sums[0], sums[1]
+        dq_raw, dk_raw, dv, wq, wk = emit(dq_raw, dkv, sums)
+        return dq_raw, dk_raw, dv, wq.reshape(HEAD_DIM), wk.reshape(HEAD_DIM)
 
     row_spec = P(('dp', 'cp'))
     in_specs = (row_spec, row_spec, row_spec, row_spec, row_spec, row_spec, P(), P())

time: 151 us -> 143 us (0.947)
  Pallas kernels: 147 us -> 142 us
  local copies, waits for them, and re-layouts: 2.86 us -> 0 us
    pallas_call x1, Pallas kernels: 141 us -> 136 us  [mega(): pl.pallas_call(functools.partial(mega_kernel, nz, chunk, per_kv, kv_heads...]
    unnamed x1 -> x0, local copies, waits for them, and re-layouts: 1.59 us -> none
where the time goes in v4:
time: 143 us; the launch traced here: 142 us
  Pallas kernels  142 us (99%)
    pallas_call x1, Pallas kernels, mega(): pl.pallas_call(functools.partial(mega_kernel, nz, chunk, per_kv, kv_heads...  136 us
    pallas_call x1, Pallas kernels, emit(): pl.pallas_call(functools.partial(emit_kernel, n), in_specs=[any_spec, vme...  5.41 us

profile of v4, /device:TPU:21, one launch (start us, length us, event | category | flops | bytes accessed | tf_op | source)
XLA Modules:
  0.0 142.4 jit_solution(14624311360280966407)
XLA Ops:
  0.6 136.3 %attn_bwd.1 = (bf16[256,64,128]{2,1,0:T(8,128)(2,1)}, bf16[4,2,2,128,128]{4,3,2,1,0:T(8,128)(2,1)}, f32[8,128]{1,0:T(8,128)}) custom-call(bf16[256,64,128]{2,1,0:T(8,128)(2,1)} %q_hbm.1, bf16[256,64,128]{2,1,0:T(8,128)(2,1)} %do_hbm.1, bf16[256,64,128]{2,1,0:T(8,128)(2,1)} %out_hbm.1, f32[64,256]{1,0:T(8,128)} %bitcast.9, bf16[1024,128]{1,0:T(8,128)(2,1)} %bitcast.7, ...), custom_call_target="tpu_custom_call" | custom-call | tf_op jit(solution)/shard_map/attn_bwd/pallas_call | solution.py:580
  136.9 5.4 %emit.1 = (bf16[256,64,128]{2,1,0:T(8,128)(2,1)}, bf16[256,4,128]{2,1,0:T(4,128)(2,1)}, bf16[256,4,128]{2,1,0:T(4,128)(2,1)}, f32[1,128]{1,0:T(1,128)}, f32[1,128]{1,0:T(1,128)}) custom-call(bf16[256,64,128]{2,1,0:T(8,128)(2,1)} %get-tuple-element.13.dq_in, bf16[4,2,2,128,128]{4,3,2,1,0:T(8,128)(2,1)} %get-tuple-element.14.dkv_in, ...), custom_call_target="tpu_custom_call" | custom-call | tf_op jit(solution)/shard_map/emit/pallas_call | solution.py:625

commit v5 on v4

--- a/solution.py
+++ b/solution.py
@@ -17,16 +17,16 @@
 MESH = pl.DeviceIdType.MESH
 PAIR = range(2)
 
-ORDER = (46781235, 78136245)
-GATHER = (356001960000600070, 1674014820106000388, 2382023180218402120, 2578024720244402508, 2704027680264202664,
-    2982029880302802918, 3306031800303002964, 3566035680337003376, 4212040820401403892, 459804402)
-REDUCE = (1106010420078000650, 1614014170148701232, 2054018070186901678, 2505023150225102053, 2759026950260802674,
-    3246031170305202738, 3819035250350303311, 4073040100388303753, 5315048670496704645, 5861057980576105287, 6497063710617706209,
-    6435)
-GATHER_RIGHT = (33344444, 44444333, 333, 333)
-GATHER_LEFT = (44433333, 33333444, 1234444, 1234444)
-REDUCE_RIGHT = (33333333, 44444444, 1233444, 1234333)
-REDUCE_LEFT = (44444444, 33333333, 4333, 444)
+ORDER = (56817234, 87162354)
+GATHER = (452004200007000004, 1608009020084200776, 2252021500206002126, 2342023200238602186, 2532024460238402472,
+    2730027940264602580, 2988029680290602920, 3376033080311803054, 4214040180395203698, 4730044080434004148, 4856)
+REDUCE = (784006460072000658, 1228011670116600974, 1611014210142001357, 1929018650167501674, 2416023540218302119,
+    2862026290260402546, 3183029910305302821, 3689034990337003369, 4197038770394703905, 5351051230426204135, 6305060830592305377,
+    637106369)
+GATHER_RIGHT = (54555555, 22554322, 22, 322)
+GATHER_LEFT = (23222222, 55223455, 1234555, 1234455)
+REDUCE_RIGHT = (33443444, 33333333, 1234444, 1234333)
+REDUCE_LEFT = (44334333, 44444444, 333, 444)
 PREP_TOKENS = 32
 
 
@@ -50,6 +50,7 @@
 G_SEQ, R_SEQ = unpacked(GATHER), unpacked(REDUCE)
 GATHER_AT, GATHER_CODE = [n >> 7 for n in G_SEQ], [n & 127 for n in G_SEQ]
 REDUCE_AT, REDUCE_CODE = [n >> 7 for n in R_SEQ], [n & 127 for n in R_SEQ]
+MAX_HOP = max(map(max, GATHER_REACH + REDUCE_REACH))
 SLOTS = [[4 * int(d) + j for d in str(order) for j in range(3 if d == '4' else 2)] for order in ORDER]
 
 
@@ -103,6 +104,17 @@
 def action_masks(nz, sequence, active):
     chips = [[int(active(zz, *act)) for act in sequence] for zz in range(nz)]
     return [[sum(bit << k for k, bit in enumerate(c[i:i + 16])) for c in chips] for i in range(0, len(sequence), 16)]
+
+
+def landing_slots(nz, sequence, reach):
+    slots, users = {}, []
+    for key in sorted({act[:4] for act in sequence if act[4]}):
+        dr, h, d, el = key
+        chips = {zz for zz in range(nz) if d + 1 <= reach[dr][(el * 2 + h) * nz + (zz + (1 - 2 * dr) * d) % nz]}
+        n = next((i for i, u in enumerate(users) if not u & chips), len(users))
+        users[n:n + 1] = [(users[n] if n < len(users) else set()) | chips]
+        slots[key] = n
+    return slots, len(users)
 
 
 def count_at(table, last):
@@ -117,11 +129,11 @@
                 ag_send, ag_recv, rs_send, rs_recv, dq_loc, dq_snd, dq_rcv, dk_loc, dk_snd, dk_rcv, w_snd, w_rcv):
     me = lax.axis_index('cp')
     cp = 2 * nz
-    z, core = me // 2, me % 2
+    z, core = me >> 1, me & 1
     other = 1 - core
     sib = 2 * z + other
-    right = 2 * lax.rem(z + 1, nz) + core
-    left = 2 * lax.rem(z + nz - 1, nz) + core
+    right = 2 * ((z + 1) & (nz - 1)) + core
+    left = 2 * ((z + nz - 1) & (nz - 1)) + core
     tok = 2 * chunk
     rows = tok * per_kv
     qb, aux, dqs = (qb_a, qb_b), (aux_a, aux_b), (dq, dq_b)
@@ -136,7 +148,7 @@
     barrier = pltpu.get_barrier_semaphore()
 
     def say(i, carry):
-        pl.semaphore_signal(barrier, inc=1, **to(lax.rem(me + i, cp)))
+        pl.semaphore_signal(barrier, inc=1, **to((me + i) & (cp - 1)))
         return carry
 
     lax.fori_loop(1, cp, say, 0)
@@ -218,8 +230,8 @@
                 x = raw(0, side, h, el)
                 y = x * lax.rsqrt(lane_mean(x * x) + NORM_EPS) * kw
                 tabs = pl.ds(pl.multiple_of(el * tok + off, chunk), chunk)
-                kvall[z, h, el, 0, pl.ds(off, chunk), :] = (y * cos_d[tabs] + roll_half(y) * sin_d[tabs]).astype(BF16)
-                kvall[z, h, el, 1, pl.ds(off, chunk), :] = raw(1, side, h, el).astype(BF16)
+                kvall[z, h, el, 0, :, pl.ds(off, chunk)] = (y * cos_d[tabs] + roll_half(y) * sin_d[tabs]).T.astype(BF16)
+                kvall[z, h, el, 1, :, pl.ds(off, chunk)] = raw(1, side, h, el).T.astype(BF16)
 
     n_l = 3 * per_kv
     lane_c = lax.broadcasted_iota(jnp.int32, (chunk, HEAD_DIM), 1)
@@ -257,7 +269,10 @@
     def sign(direction):
         return 1 - 2 * direction
 
-    g_seq, r_seq = [split(c, 1, 1, 3, 1, 1) for c in GATHER_CODE], [split(c, 1, 1, 3, 1, 1) for c in REDUCE_CODE]
+    g_seq, r_seq = [[tuple(split(c, 1, 1, 3, 1, 1)) for c in codes] for codes in (GATHER_CODE, REDUCE_CODE)]
+    slots, _ = landing_slots(nz, r_seq, REDUCE_REACH)
+    slot_in = [slots.get(act[:4], 0) for act in r_seq]
+    slot_out = [slots.get((dr, h, d - 1, el), 0) for dr, h, d, el, _ in r_seq]
     g_wait, g_send, r_wait, r_send = (
         [select_const(z, w) for w in action_masks(nz, seq, active)] for seq, active in (
             (g_seq, lambda zz, dr, h, s, el, _: lives(GATHER_REACH[dr], el, h, s - 1, zz - sign(dr) * (s - 1))),
@@ -296,13 +311,13 @@
         def _():
             gather_copy(direction, h, s, el).start()
 
-    def reduce_copy(direction, h, d, el):
-        return pltpu.make_async_remote_copy(acc.at[wrap(z + sign(direction) * d), h, el], rsb.at[direction, d - 1, h, el],
+    def reduce_copy(direction, h, d, el, slot):
+        return pltpu.make_async_remote_copy(acc.at[wrap(z + sign(direction) * d), h, el], rsb.at[slot],
                                             rs_send.at[direction, d - 1, h, el], rs_recv.at[direction, d - 1, h, el],
                                             **neighbour(direction))
 
-    def reduce_arrival(direction, h, d, el):
-        return pltpu.make_async_remote_copy(acc.at[wrap(z + sign(direction) * d), h, el], rsb.at[direction, d, h, el],
+    def reduce_arrival(direction, h, d, el, slot):
+        return pltpu.make_async_remote_copy(acc.at[wrap(z + sign(direction) * d), h, el], rsb.at[slot],
                                             rs_send.at[direction, d, h, el], rs_recv.at[direction, d, h, el],
                                             **neighbour(direction))
 
@@ -311,12 +326,13 @@
 
         @pl.when(on(r_wait, b))
         def _():
-            reduce_arrival(direction, h, d, el).wait_recv()
-            acc[wrap(z + sign(direction) * d), h, el] += rsb[direction, d, h, el]
+            slot = packed(b, slot_in, 7)
+            reduce_arrival(direction, h, d, el, slot).wait_recv()
+            acc[wrap(z + sign(direction) * d), h, el] += rsb[slot]
 
         @pl.when(on(r_send, b))
         def _():
-            reduce_copy(direction, h, d, el).start()
+            reduce_copy(direction, h, d, el, packed(b, slot_out, 7)).start()
 
     def run_actions(step, first, count):
         def one(i, carry):
@@ -344,8 +360,6 @@
 
     turn(cos_t, sin_t, lambda x: x[:, None, :])
     pieces_of(0)
-    dq[...] = jnp.zeros_like(dq)
-    dq_b[...] = jnp.zeros_like(dq_b)
 
     swaps[2].wait_recv()
     pieces_of(1)
@@ -379,6 +393,7 @@
         dpart = jnp.where(lane == n_l, r0, jnp.where(lane == n_l + 1, r1, jnp.where(lane == n_l + 2, r2, 0.0)))
         consts = flat(jnp.broadcast_to(pieces[h, tabs], (sub, per_kv, HEAD_DIM)))
         aux[h][hr, :] = jnp.where(lse_mask, consts, dpart).astype(BF16)
+        dqs[h][hr, :] = jnp.zeros((sub * per_kv, HEAD_DIM), F32)
 
     def finish(h, el, t0, on_mxu):
         tabs = pl.ds(pl.multiple_of(el * tok + t0, sub), sub)
@@ -397,22 +412,25 @@
         el = jnp.where(i >= n_pieces // 2, 1, 0)
         return el, (i - el * (n_pieces // 2)) * sub
 
-    for part in PAIR:
-        for el in PAIR:
-            for loc, rem in loads[el]:
-                if part == 0:
-                    loc.wait()
-                else:
+    for el in PAIR:
+        for loc, _ in loads[el]:
+            loc.wait()
+    quarter = chunk // (2 * sub)
+    wide = masks(2 * sub)
+
+    def piece(i, gathered):
+        @pl.when(i == 2 * quarter)
+        def _():
+            for el in PAIR:
+                for _, rem in loads[el]:
                     rem.wait_recv()
-        n = chunk // (2 * sub)
-
-        def piece(i, gathered):
-            el = jnp.where(i >= n, 1, 0)
-            mine = core if part == 0 else other
-            prepare(0, el, jnp.where(el == 0, mine, 1 - mine) * chunk + (i - el * n) * 2 * sub, *masks(2 * sub))
-            return run_actions(gather_step, gathered, packed(1 + part * 2 * n + i, prep_counts, 4))
-
-        gathered = lax.fori_loop(0, 2 * n, piece, gathered)
+
+        part, k = jnp.where(i >= 2 * quarter, 1, 0), i & (2 * quarter - 1)
+        el = jnp.where(k >= quarter, 1, 0)
+        prepare(0, el, (core ^ part ^ el) * chunk + (k - el * quarter) * 2 * sub, *wide)
+        return run_actions(gather_step, gathered, packed(1 + i, prep_counts, 4))
+
+    gathered = lax.fori_loop(0, 4 * quarter, piece, gathered)
     for el in PAIR:
         for loc, rem in loads[2 + el]:
             loc.wait()
@@ -420,9 +438,9 @@
     dwq[...] = jnp.zeros_like(dwq)
 
     keys = tok
-    klane = lax.broadcasted_iota(jnp.int32, (keys, HEAD_DIM), 1)
-    ones_k = jnp.where(klane < n_l, 1.0, 0.0).astype(BF16)
-    ones_v = jnp.where((klane >= n_l) & (klane < n_l + 3), 1.0, 0.0).astype(BF16)
+    krow = lax.broadcasted_iota(jnp.int32, (HEAD_DIM, keys), 0)
+    ones_k = jnp.where(krow < n_l, 1.0, 0.0).astype(BF16)
+    ones_v = jnp.where((krow >= n_l) & (krow < n_l + 3), 1.0, 0.0).astype(BF16)
     klan = lax.broadcasted_iota(jnp.int32, (per_kv, keys), 1)
 
     def work(h, g, done):
@@ -441,13 +459,13 @@
         k, v = kvall[kz, h, k_late, 0], kvall[kz, h, k_late, 1]
         hr = pl.ds(pl.multiple_of(q_late * rows, rows), rows)
         qq, ax, dd = qb[h][hr, :], aux[h][hr, :], xdo[r, :]
-        s = dot(jnp.concatenate([qq, ax], 1), jnp.concatenate([k, ones_k], 1), 1, 1)
-        dp = dot(jnp.concatenate([dd, ax], 1), jnp.concatenate([v, ones_v], 1), 1, 1)
+        s = dot(jnp.concatenate([qq, ax], 1), jnp.concatenate([k, ones_k], 0), 1, 0)
+        dp = dot(jnp.concatenate([dd, ax], 1), jnp.concatenate([v, ones_v], 0), 1, 0)
         p = jnp.exp2(s * EXP_SCALE)
         p = jnp.concatenate([jnp.where(klan <= off + t, p[per_kv * t:per_kv * (t + 1)], 0.0) for t in range(tok)], 0)
         ds = (p * dp).astype(BF16)
         pb = p.astype(BF16)
-        dqs[h][hr, :] += dot(ds, k, 1, 0)
+        dqs[h][hr, :] += dot(ds, k, 1, 1)
         acc[kz, h, k_late, 0] += dot(qq, ds, 0, 0)
         acc[kz, h, k_late, 1] += dot(dd, pb, 0, 0)
         el, t0 = piece_at(jnp.minimum(u, n_pieces - 1))
@@ -537,7 +555,7 @@
                            jnp.where(top == 1, jnp.sum(dwk, axis=0, keepdims=True), 0.0))
 
     def weight_copy(i):
-        return pltpu.make_async_remote_copy(wmine, wslots.at[cp - i], w_snd.at[i], w_rcv.at[cp - i], **to(lax.rem(me + i, cp)))
+        return pltpu.make_async_remote_copy(wmine, wslots.at[cp - i], w_snd.at[i], w_rcv.at[cp - i], **to((me + i) & (cp - 1)))
 
     def weight_send(i, carry):
         weight_copy(i).start()
@@ -550,19 +568,19 @@
 
         @pl.when(on(r_send, b))
         def _():
-            reduce_copy(direction, h, d, el).wait_send()
+            reduce_copy(direction, h, d, el, 0).wait_send()
 
         return carry
 
     lax.fori_loop(0, len(R_SEQ), drain_reduce, 0)
 
     def weight_wait(i, carry):
-        pltpu.make_async_remote_copy(wmine, wslots.at[i], w_snd.at[i], w_rcv.at[i], **to(lax.rem(me + i, cp))).wait()
+        pltpu.make_async_remote_copy(wmine, wslots.at[i], w_snd.at[i], w_rcv.at[i], **to((me + i) & (cp - 1))).wait()
         return carry
 
     lax.fori_loop(1, cp, weight_wait, 0)
     wslots[0] = wmine[...]
-    w_ref[...] = lax.fori_loop(0, cp, lambda i, total: total + wslots[lax.rem(i - me + cp, cp)], jnp.zeros((8, HEAD_DIM), F32))
+    w_ref[...] = lax.fori_loop(0, cp, lambda i, total: total + wslots[(i - me + cp) & (cp - 1)], jnp.zeros((8, HEAD_DIM), F32))
     for loc, rem in outs:
         loc.wait()
         rem.wait()
@@ -575,6 +593,7 @@
     vmem = pl.BlockSpec(memory_space=pltpu.VMEM)
     dma, scr = pltpu.SemaphoreType.DMA, pltpu.VMEM
     n_rows = 2 * tok * per_kv
+    _, n_slots = landing_slots(nz, [tuple(split(c, 1, 1, 3, 1, 1)) for c in REDUCE_CODE], REDUCE_REACH)
     hbm = lambda a: pltpu.with_memory_space_constraint(a, pltpu.HBM)
     args = [q_raw, d_out, out_fwd, lse, k_rows, v_rows, offc[:, None], offs[:, None], offc, offs]
     return pl.pallas_call(
@@ -585,11 +604,11 @@
                    jax.ShapeDtypeStruct((8, hd), F32)],
         scratch_shapes=[
             *[scr((2 * n_rows, hd), BF16)] * 3, *[scr((n_rows, hd), BF16)] * 4, *[scr((n_rows, hd), F32)] * 2,
-            scr((nz, 2, 2, 2, tok, hd), BF16), scr((nz, 2, 2, 2, hd, tok), F32), scr((2, 4, 2, 2, 2, hd, tok), F32),
+            scr((nz, 2, 2, 2, hd, tok), BF16), scr((nz, 2, 2, 2, hd, tok), F32), scr((n_slots, 2, hd, tok), F32),
             scr((2, 2) + k_rows.shape, BF16), scr((2,) + lse.shape, F32), scr((2, 2 * tok, 1, hd), F32),
             *[scr((2 * tok, 1, hd), F32)] * 2, *[scr((2 * tok, hd), F32)] * 2,
             scr((2, 2, 2, tok, hd), BF16), *[scr((8, hd), F32)] * 2, scr((2 * nz, 8, hd), F32),
-            *[dma((3,))] * 3, *[dma((2, 2, 3))] * 3, dma((4,)), *[dma((2, 2, 4, 2))] * 2, *[dma((2, 4, 2, 2))] * 2,
+            *[dma((3,))] * 3, *[dma((2, 2, 3))] * 3, dma((4,)), *[dma((2, 2, MAX_HOP, 2))] * 2, *[dma((2, MAX_HOP, 2, 2))] * 2,
             *[dma((2, 2))] * 6, *[dma((2 * nz,))] * 2,
         ],
         name='attn_bwd',
@@ -597,22 +616,28 @@
     )(*[hbm(a) for a in args], basec, bases, qw, kw)
 
 
-def emit_kernel(n, dq_in, dkv_in, w_in, dq_out, dk_out, dv_out, wq_out, wk_out, buf, in_sem, out_sem):
+def emit_kernel(n, dq_in, dkv_in, w_in, dq_out, dk_out, dv_out, wq_out, wk_out, buf, kv_buf, k_buf, v_buf, kv_sem, in_sem, out_sem):
     step = dq_in.shape[0] // n
     part = lambda ref, i: ref.at[pl.ds(i * step, step)]
     reads = [pltpu.make_async_copy(part(dq_in, i), part(buf, i), in_sem.at[i]) for i in range(n)]
     writes = [pltpu.make_async_copy(part(buf, i), part(dq_out, i), out_sem.at[i]) for i in range(n)]
-    for cpy in reads:
+    kv_heads, halves, _, chunk, _ = dkv_in.shape
+    rows = lambda ref, half: ref.at[pl.ds(half * chunk, chunk)]
+    kv_reads = [pltpu.make_async_copy(dkv_in.at[:, half], kv_buf.at[:, half], kv_sem.at[half]) for half in range(halves)]
+    for cpy in kv_reads + reads:
         cpy.start()
     wq_out[...], wk_out[...] = w_in[0:1, :], w_in[1:2, :]
-    kv_heads, halves, _, chunk, _ = dkv_in.shape
+    for half in range(halves):
+        kv_reads[half].wait()
+        for what, (ref, out) in enumerate(((k_buf, dk_out), (v_buf, dv_out))):
+            x = kv_buf[:, half, what].astype(F32)
+            ref[pl.ds(half * chunk, chunk)] = jnp.stack([x[h] for h in range(kv_heads)], axis=1).astype(BF16)
+            writes.append(pltpu.make_async_copy(rows(ref, half), rows(out, half), kv_sem.at[halves + 2 * half + what]))
     for i in range(n):
         reads[i].wait()
         writes[i].start()
-        if i < 2 * halves:
-            ref, half, what = (dk_out, dv_out)[i & 1], i >> 1, i & 1
-            x = dkv_in[:, half, what].astype(F32)
-            ref[pl.ds(half * chunk, chunk)] = jnp.stack([x[h] for h in range(kv_heads)], axis=1).astype(BF16)
+    for cpy in writes[n:]:
+        cpy.start()
     for cpy in writes:
         cpy.wait()
 
@@ -622,15 +647,18 @@
     kv_heads = dkv.shape[0]
     n = 8
     any_spec, vmem = pl.BlockSpec(memory_space=pl.ANY), pl.BlockSpec(memory_space=pltpu.VMEM)
+    kv_shape = (tok, kv_heads, hd)
+    hbm = lambda a: pltpu.with_memory_space_constraint(a, pltpu.HBM)
+    dma = pltpu.SemaphoreType.DMA
     return pl.pallas_call(
         functools.partial(emit_kernel, n),
-        in_specs=[any_spec, vmem, vmem],
-        out_specs=[any_spec] + [vmem] * 4,
-        out_shape=[jax.ShapeDtypeStruct(dq.shape, BF16)] + [jax.ShapeDtypeStruct((tok, kv_heads, hd), BF16)] * 2
+        in_specs=[any_spec, any_spec, vmem],
+        out_specs=[any_spec] * 3 + [vmem] * 2,
+        out_shape=[jax.ShapeDtypeStruct(dq.shape, BF16)] + [jax.ShapeDtypeStruct(kv_shape, BF16)] * 2
         + [jax.ShapeDtypeStruct((1, hd), F32)] * 2,
-        scratch_shapes=[pltpu.VMEM(dq.shape, BF16), *[pltpu.SemaphoreType.DMA((n,))] * 2],
+        scratch_shapes=[*[pltpu.VMEM(shape, BF16) for shape in (dq.shape, dkv.shape, kv_shape, kv_shape)], dma((n,)), *[dma((n,))] * 2],
         name='emit',
-    )(pltpu.with_memory_space_constraint(dq, pltpu.HBM), dkv, weights)
+    )(hbm(dq), hbm(dkv), weights)
 
 
 def solution(mesh):

time: 143 us -> 143 us (level)
  no operation moved by 1% of the time
where the time goes in v5:
time: 143 us
  Pallas kernels  142 us (99%)
    pallas_call x1, Pallas kernels, mega(): pl.pallas_call(functools.partial(mega_kernel, nz, chunk, per_kv, kv_heads...  136 us
    pallas_call x1, Pallas kernels, emit(): pl.pallas_call(functools.partial(emit_kernel, n), in_specs=[any_spec, any...  6.41 us

profile of v5, /device:TPU:21, one launch (start us, length us, event | category | flops | bytes accessed | tf_op | source)
XLA Modules:
  0.0 142.6 jit_solution(2664787432047933283)
XLA Ops:
  0.6 135.6 %attn_bwd.1 = (bf16[256,64,128]{2,1,0:T(8,128)(2,1)}, bf16[4,2,2,128,128]{4,3,2,1,0:T(8,128)(2,1)}, f32[8,128]{1,0:T(8,128)}) custom-call(bf16[256,64,128]{2,1,0:T(8,128)(2,1)} %q_hbm.1, bf16[256,64,128]{2,1,0:T(8,128)(2,1)} %do_hbm.1, bf16[256,64,128]{2,1,0:T(8,128)(2,1)} %out_hbm.1, f32[64,256]{1,0:T(8,128)} %bitcast.9, bf16[1024,128]{1,0:T(8,128)(2,1)} %bitcast.7, ...), custom_call_target="tpu_custom_call" | custom-call | tf_op jit(solution)/shard_map/attn_bwd/pallas_call | solution.py:599
  136.2 6.4 %emit.1 = (bf16[256,64,128]{2,1,0:T(8,128)(2,1)}, bf16[256,4,128]{2,1,0:T(4,128)(2,1)}, bf16[256,4,128]{2,1,0:T(4,128)(2,1)}, f32[1,128]{1,0:T(1,128)}, f32[1,128]{1,0:T(1,128)}) custom-call(bf16[256,64,128]{2,1,0:T(8,128)(2,1)} %get-tuple-element.13.dq_in, bf16[4,2,2,128,128]{4,3,2,1,0:T(8,128)(2,1)} %get-tuple-element.14.dkv_in, ...), custom_call_target="tpu_custom_call" | custom-call | tf_op jit(solution)/shard_map/emit/pallas_call | solution.py:653

commit v6 on v5

--- a/solution.py
+++ b/solution.py
@@ -17,16 +17,15 @@
 MESH = pl.DeviceIdType.MESH
 PAIR = range(2)
 
-ORDER = (56817234, 87162354)
-GATHER = (452004200007000004, 1608009020084200776, 2252021500206002126, 2342023200238602186, 2532024460238402472,
-    2730027940264602580, 2988029680290602920, 3376033080311803054, 4214040180395203698, 4730044080434004148, 4856)
-REDUCE = (784006460072000658, 1228011670116600974, 1611014210142001357, 1929018650167501674, 2416023540218302119,
-    2862026290260402546, 3183029910305302821, 3689034990337003369, 4197038770394703905, 5351051230426204135, 6305060830592305377,
-    637106369)
-GATHER_RIGHT = (54555555, 22554322, 22, 322)
-GATHER_LEFT = (23222222, 55223455, 1234555, 1234455)
-REDUCE_RIGHT = (33443444, 33333333, 1234444, 1234333)
-REDUCE_LEFT = (44334333, 44444444, 333, 444)
+ORDER = (43215687, 78135264)
+GATHER = (260003560000600070, 1994019300138201092, 2376023180228002184, 2706027940257202468, 3020030520296002894,
+    3348032380318203112, 3736038240362603478, 4268039200392203954, 4858045260446804470, 485604784)
+REDUCE = (1354013000104600968, 1991019390180901861, 2422023180218902066, 2826026970244702420, 3393031850308302931,
+    3591035900343903333, 4010038800394703693, 4227042910422504201, 5093047110464604389, 6369061150604905287, 6435)
+GATHER_RIGHT = (55554445, 22333322, 4444, 22)
+GATHER_LEFT = (22223332, 55444455, 1233333, 1234555)
+REDUCE_RIGHT = (55555555, 22222222, 1234555, 1222222)
+REDUCE_LEFT = (22222222, 55555555, 22, 55555)
 PREP_TOKENS = 32
 
 
@@ -206,9 +205,6 @@
 
             lax.fori_loop(0, tok // step, part, 0)
 
-    for t in tables:
-        t.wait()
-    turn(cos_d, sin_d, lambda x: x)
 
     def raw_rows(what, side):
         return pl.ds((what * 2 + side) * k_rows, k_rows)
@@ -249,15 +245,20 @@
                                jnp.where(lane_c < n_l, pltpu.roll(low, 2 * per_kv, axis=1), 0.0)))
                 pieces[h, pl.ds(pl.multiple_of(el * tok + off_of(el, side == 0), chunk), chunk)] = pc[:, None, :]
 
-    for cpy in own_in:
-        cpy.wait()
-    keys_of(0)
     pl.semaphore_wait(barrier, cp - 1)
     for cpy in swaps:
         cpy.start()
     for row in loads:
         for _, rem in row:
             rem.start()
+    for t in tables:
+        t.wait()
+    turn(cos_d, sin_d, lambda x: x)
+    for cpy in own_in:
+        cpy.wait()
+    keys_of(0)
+    turn(cos_t, sin_t, lambda x: x[:, None, :])
+    pieces_of(0)
     acc[...] = jnp.zeros_like(acc)
     for i in PAIR:
         swaps[i].wait_recv()
@@ -358,8 +359,6 @@
 
     gathered = run_actions(gather_step, 0, gather_counts[0])
 
-    turn(cos_t, sin_t, lambda x: x[:, None, :])
-    pieces_of(0)
 
     swaps[2].wait_recv()
     pieces_of(1)
@@ -484,8 +483,6 @@
         dwq[...] += finish(1, el, t0, True)
         return ticks(n_steps + i, done)
 
-    done = lax.fori_loop(0, n_pieces, last, done)
-
     def back(x, ssum, g, cos, sin, w):
         rstd = lax.rsqrt(ssum * (1.0 / HEAD_DIM) + NORM_EPS)
         xhat = x * rstd
@@ -495,34 +492,16 @@
         return dx, jnp.sum((dy * xhat).reshape(-1, 8, HEAD_DIM), axis=0)
 
     outs = []
-    for h in PAIR:
-        for el in PAIR:
-            heads = pl.ds(pl.multiple_of((2 * core + h) * per_kv, per_kv), per_kv)
-            dst = dq_hbm.at[pl.ds(el * chunk, chunk), heads, :]
-            part = lambda mine: qb[h].at[h_rows(el, off_of(el, mine), chunk)].reshape(chunk, per_kv, HEAD_DIM)
-            outs.append((pltpu.make_async_copy(part(True), dst, dq_loc.at[h, el]),
-                         pltpu.make_async_remote_copy(part(False), dst, dq_snd.at[h, el], dq_rcv.at[h, el], **to(sib))))
-    for loc, rem in outs:
-        loc.start()
-        rem.start()
-    for side in PAIR:
-        unpack_keys(0, side)
-
-    def drain_gather(a, carry):
-        direction, h, s, el, _ = split(packed(a, GATHER_CODE, 7), 1, 1, 3, 1, 1)
-
-        @pl.when(on(g_send, a))
-        def _():
-            gather_copy(direction, h, s, el).wait_send()
-
-        return carry
-
-    lax.fori_loop(0, len(G_SEQ), drain_gather, 0)
-    for cpy in swaps:
-        cpy.wait_send()
-    for row in loads:
-        for _, rem in row:
-            rem.wait_send()
+
+    def send_queries(h, el):
+        heads = pl.ds(pl.multiple_of((2 * core + h) * per_kv, per_kv), per_kv)
+        dst = dq_hbm.at[pl.ds(el * chunk, chunk), heads, :]
+        part = lambda mine: qb[h].at[h_rows(el, off_of(el, mine), chunk)].reshape(chunk, per_kv, HEAD_DIM)
+        both = (pltpu.make_async_remote_copy(part(False), dst, dq_snd.at[h, el], dq_rcv.at[h, el], **to(sib)),
+                pltpu.make_async_copy(part(True), dst, dq_loc.at[h, el]))
+        outs.append(both)
+        for cpy in both:
+            cpy.start()
 
     hold = 4 * k_rows
 
@@ -546,8 +525,32 @@
                 cpy.start()
         return dwk
 
-    assert all(at < n_ticks for at, (_, h, d, _, _) in zip(REDUCE_AT, r_seq) if h == 0 and d == 0)
+    assert all(at < n_steps for at, (_, h, d, _, _) in zip(REDUCE_AT, r_seq) if h == 0 and d == 0)
+    for el in PAIR:
+        send_queries(0, el)
+    for side in PAIR:
+        unpack_keys(0, side)
     dwk = key_gradients(0, jnp.zeros((8, HEAD_DIM), F32))
+
+    def drain_gather(a, carry):
+        direction, h, s, el, _ = split(packed(a, GATHER_CODE, 7), 1, 1, 3, 1, 1)
+
+        @pl.when(on(g_send, a))
+        def _():
+            gather_copy(direction, h, s, el).wait_send()
+
+        return carry
+
+    lax.fori_loop(0, len(G_SEQ), drain_gather, 0)
+    for cpy in swaps:
+        cpy.wait_send()
+    for row in loads:
+        for _, rem in row:
+            rem.wait_send()
+
+    for el in PAIR:
+        done = lax.fori_loop(el * n_pieces // 2, (el + 1) * n_pieces // 2, last, done)
+        send_queries(1, el)
     run_actions(reduce_step, done[1], len(R_SEQ) - done[1])
     dwk = key_gradients(1, dwk)
     top = lax.broadcasted_iota(jnp.int32, (8, HEAD_DIM), 0)
@@ -616,28 +619,22 @@
     )(*[hbm(a) for a in args], basec, bases, qw, kw)
 
 
-def emit_kernel(n, dq_in, dkv_in, w_in, dq_out, dk_out, dv_out, wq_out, wk_out, buf, kv_buf, k_buf, v_buf, kv_sem, in_sem, out_sem):
+def emit_kernel(n, dq_in, dkv_in, w_in, dq_out, dk_out, dv_out, wq_out, wk_out, buf, in_sem, out_sem):
     step = dq_in.shape[0] // n
     part = lambda ref, i: ref.at[pl.ds(i * step, step)]
     reads = [pltpu.make_async_copy(part(dq_in, i), part(buf, i), in_sem.at[i]) for i in range(n)]
     writes = [pltpu.make_async_copy(part(buf, i), part(dq_out, i), out_sem.at[i]) for i in range(n)]
-    kv_heads, halves, _, chunk, _ = dkv_in.shape
-    rows = lambda ref, half: ref.at[pl.ds(half * chunk, chunk)]
-    kv_reads = [pltpu.make_async_copy(dkv_in.at[:, half], kv_buf.at[:, half], kv_sem.at[half]) for half in range(halves)]
-    for cpy in kv_reads + reads:
+    for cpy in reads:
         cpy.start()
     wq_out[...], wk_out[...] = w_in[0:1, :], w_in[1:2, :]
-    for half in range(halves):
-        kv_reads[half].wait()
-        for what, (ref, out) in enumerate(((k_buf, dk_out), (v_buf, dv_out))):
-            x = kv_buf[:, half, what].astype(F32)
-            ref[pl.ds(half * chunk, chunk)] = jnp.stack([x[h] for h in range(kv_heads)], axis=1).astype(BF16)
-            writes.append(pltpu.make_async_copy(rows(ref, half), rows(out, half), kv_sem.at[halves + 2 * half + what]))
+    kv_heads, halves, _, chunk, _ = dkv_in.shape
     for i in range(n):
         reads[i].wait()
         writes[i].start()
-    for cpy in writes[n:]:
-        cpy.start()
+        if i < 2 * halves:
+            ref, half, what = (dk_out, dv_out)[i & 1], i >> 1, i & 1
+            x = dkv_in[:, half, what].astype(F32)
+            ref[pl.ds(half * chunk, chunk)] = jnp.stack([x[h] for h in range(kv_heads)], axis=1).astype(BF16)
     for cpy in writes:
         cpy.wait()
 
@@ -647,18 +644,15 @@
     kv_heads = dkv.shape[0]
     n = 8
     any_spec, vmem = pl.BlockSpec(memory_space=pl.ANY), pl.BlockSpec(memory_space=pltpu.VMEM)
-    kv_shape = (tok, kv_heads, hd)
-    hbm = lambda a: pltpu.with_memory_space_constraint(a, pltpu.HBM)
-    dma = pltpu.SemaphoreType.DMA
     return pl.pallas_call(
         functools.partial(emit_kernel, n),
-        in_specs=[any_spec, any_spec, vmem],
-        out_specs=[any_spec] * 3 + [vmem] * 2,
-        out_shape=[jax.ShapeDtypeStruct(dq.shape, BF16)] + [jax.ShapeDtypeStruct(kv_shape, BF16)] * 2
+        in_specs=[any_spec, vmem, vmem],
+        out_specs=[any_spec] + [vmem] * 4,
+        out_shape=[jax.ShapeDtypeStruct(dq.shape, BF16)] + [jax.ShapeDtypeStruct((tok, kv_heads, hd), BF16)] * 2
         + [jax.ShapeDtypeStruct((1, hd), F32)] * 2,
-        scratch_shapes=[*[pltpu.VMEM(shape, BF16) for shape in (dq.shape, dkv.shape, kv_shape, kv_shape)], dma((n,)), *[dma((n,))] * 2],
+        scratch_shapes=[pltpu.VMEM(dq.shape, BF16), *[pltpu.SemaphoreType.DMA((n,))] * 2],
         name='emit',
-    )(hbm(dq), hbm(dkv), weights)
+    )(pltpu.with_memory_space_constraint(dq, pltpu.HBM), dkv, weights)
 
 
 def solution(mesh):

time: 143 us -> 144 us (level)
    pallas_call x1, Pallas kernels: 136 us -> 138 us  [mega(): pl.pallas_call(functools.partial(mega_kernel, nz, chunk, per_kv, kv_heads...]
where the time goes in v6:
time: 144 us
  Pallas kernels  143 us (99%)
    pallas_call x1, Pallas kernels, mega(): pl.pallas_call(functools.partial(mega_kernel, nz, chunk, per_kv, kv_heads...  138 us
    pallas_call x1, Pallas kernels, emit(): pl.pallas_call(functools.partial(emit_kernel, n), in_specs=[any_spec, vme...  5.41 us

profile of v6, /device:TPU:21, one launch (start us, length us, event | category | flops | bytes accessed | tf_op | source)
XLA Modules:
  0.0 143.8 jit_solution(14340929861411025593)
XLA Ops:
  0.6 137.8 %attn_bwd.1 = (bf16[256,64,128]{2,1,0:T(8,128)(2,1)}, bf16[4,2,2,128,128]{4,3,2,1,0:T(8,128)(2,1)}, f32[8,128]{1,0:T(8,128)}) custom-call(bf16[256,64,128]{2,1,0:T(8,128)(2,1)} %q_hbm.1, bf16[256,64,128]{2,1,0:T(8,128)(2,1)} %do_hbm.1, bf16[256,64,128]{2,1,0:T(8,128)(2,1)} %out_hbm.1, f32[64,256]{1,0:T(8,128)} %bitcast.9, bf16[1024,128]{1,0:T(8,128)(2,1)} %bitcast.7, ...), custom_call_target="tpu_custom_call" | custom-call | tf_op jit(solution)/shard_map/attn_bwd/pallas_call | solution.py:602
  138.4 5.4 %emit.1 = (bf16[256,64,128]{2,1,0:T(8,128)(2,1)}, bf16[256,4,128]{2,1,0:T(4,128)(2,1)}, bf16[256,4,128]{2,1,0:T(4,128)(2,1)}, f32[1,128]{1,0:T(1,128)}, f32[1,128]{1,0:T(1,128)}) custom-call(bf16[256,64,128]{2,1,0:T(8,128)(2,1)} %get-tuple-element.13.dq_in, bf16[4,2,2,128,128]{4,3,2,1,0:T(8,128)(2,1)} %get-tuple-element.14.dkv_in, ...), custom_call_target="tpu_custom_call" | custom-call | tf_op jit(solution)/shard_map/emit/pallas_call | solution.py:647

commit v7 on v6

--- a/solution.py
+++ b/solution.py
@@ -17,15 +17,16 @@
 MESH = pl.DeviceIdType.MESH
 PAIR = range(2)
 
-ORDER = (43215687, 78135264)
-GATHER = (260003560000600070, 1994019300138201092, 2376023180228002184, 2706027940257202468, 3020030520296002894,
-    3348032380318203112, 3736038240362603478, 4268039200392203954, 4858045260446804470, 485604784)
-REDUCE = (1354013000104600968, 1991019390180901861, 2422023180218902066, 2826026970244702420, 3393031850308302931,
-    3591035900343903333, 4010038800394703693, 4227042910422504201, 5093047110464604389, 6369061150604905287, 6435)
-GATHER_RIGHT = (55554445, 22333322, 4444, 22)
-GATHER_LEFT = (22223332, 55444455, 1233333, 1234555)
-REDUCE_RIGHT = (55555555, 22222222, 1234555, 1222222)
-REDUCE_LEFT = (22222222, 55555555, 22, 55555)
+ORDER = (45681723, 82716354)
+GATHER = (966006440013400068, 2184020220167401736, 2506024680231802380, 2766026400257202532, 2982028560279402706,
+    3282031760302802966, 3436033100324403216, 3824036260363203482, 4342041480408403826, 5042047920472804398, 5114)
+REDUCE = (1168011060104200774, 1550016140161501356, 1865018020167701551, 2354021850225101931, 2759026740256702416,
+    2990029910286002885, 3626035670336903309, 3817037170362703649, 4197040750400603877, 5377050950505904135, 6307063050624105507,
+    6499)
+GATHER_RIGHT = (33333333, 22554322, 54555, 322)
+GATHER_LEFT = (44444444, 55223455, 1223222, 1234455)
+REDUCE_RIGHT = (44444444, 33333333, 1233444, 1234333)
+REDUCE_LEFT = (33333333, 44444444, 4333, 444)
 PREP_TOKENS = 32
 
 
@@ -525,12 +526,10 @@
                 cpy.start()
         return dwk
 
-    assert all(at < n_steps for at, (_, h, d, _, _) in zip(REDUCE_AT, r_seq) if h == 0 and d == 0)
     for el in PAIR:
         send_queries(0, el)
     for side in PAIR:
         unpack_keys(0, side)
-    dwk = key_gradients(0, jnp.zeros((8, HEAD_DIM), F32))
 
     def drain_gather(a, carry):
         direction, h, s, el, _ = split(packed(a, GATHER_CODE, 7), 1, 1, 3, 1, 1)
@@ -548,9 +547,17 @@
         for _, rem in row:
             rem.wait_send()
 
-    for el in PAIR:
-        done = lax.fori_loop(el * n_pieces // 2, (el + 1) * n_pieces // 2, last, done)
-        send_queries(1, el)
+    complete = 1 + max(at for at, (_, h, d, _, _) in zip(REDUCE_AT, r_seq) if h == 0 and d == 0) - n_steps
+    assert complete <= n_pieces
+    complete, begin = max(complete, 0), 0
+    for end in sorted({complete, n_pieces // 2, n_pieces}):
+        if end > begin:
+            done = lax.fori_loop(begin, end, last, done)
+        if end in (n_pieces // 2, n_pieces):
+            send_queries(1, 2 * end // n_pieces - 1)
+        if end == complete:
+            dwk = key_gradients(0, jnp.zeros((8, HEAD_DIM), F32))
+        begin = end
     run_actions(reduce_step, done[1], len(R_SEQ) - done[1])
     dwk = key_gradients(1, dwk)
     top = lax.broadcasted_iota(jnp.int32, (8, HEAD_DIM), 0)

time: 144 us -> 141 us (0.979)
  Pallas kernels: 143 us -> 140 us
    pallas_call x1, Pallas kernels: 138 us -> 134 us  [mega(): pl.pallas_call(functools.partial(mega_kernel, nz, chunk, per_kv, kv_heads...]
where the time goes in v7:
time: 141 us; the launch traced here: 140 us
  Pallas kernels  140 us (99%)
    pallas_call x1, Pallas kernels, mega(): pl.pallas_call(functools.partial(mega_kernel, nz, chunk, per_kv, kv_heads...  134 us
    pallas_call x1, Pallas kernels, emit(): pl.pallas_call(functools.partial(emit_kernel, n), in_specs=[any_spec, vme...  5.41 us

profile of v7, /device:TPU:21, one launch (start us, length us, event | category | flops | bytes accessed | tf_op | source)
XLA Modules:
  0.0 140.4 jit_solution(13246455343476403147)
XLA Ops:
  0.6 134.4 %attn_bwd.1 = (bf16[256,64,128]{2,1,0:T(8,128)(2,1)}, bf16[4,2,2,128,128]{4,3,2,1,0:T(8,128)(2,1)}, f32[8,128]{1,0:T(8,128)}) custom-call(bf16[256,64,128]{2,1,0:T(8,128)(2,1)} %q_hbm.1, bf16[256,64,128]{2,1,0:T(8,128)(2,1)} %do_hbm.1, bf16[256,64,128]{2,1,0:T(8,128)(2,1)} %out_hbm.1, f32[64,256]{1,0:T(8,128)} %bitcast.9, bf16[1024,128]{1,0:T(8,128)(2,1)} %bitcast.7, ...), custom_call_target="tpu_custom_call" | custom-call | tf_op jit(solution)/shard_map/attn_bwd/pallas_call | solution.py:609
  135.0 5.4 %emit.1 = (bf16[256,64,128]{2,1,0:T(8,128)(2,1)}, bf16[256,4,128]{2,1,0:T(4,128)(2,1)}, bf16[256,4,128]{2,1,0:T(4,128)(2,1)}, f32[1,128]{1,0:T(1,128)}, f32[1,128]{1,0:T(1,128)}) custom-call(bf16[256,64,128]{2,1,0:T(8,128)(2,1)} %get-tuple-element.13.dq_in, bf16[4,2,2,128,128]{4,3,2,1,0:T(8,128)(2,1)} %get-tuple-element.14.dkv_in, ...), custom_call_target="tpu_custom_call" | custom-call | tf_op jit(solution)/shard_map/emit/pallas_call | solution.py:654

commit v8 on v7

--- a/solution.py
+++ b/solution.py
@@ -17,16 +17,16 @@
 MESH = pl.DeviceIdType.MESH
 PAIR = range(2)
 
-ORDER = (45681723, 82716354)
-GATHER = (966006440013400068, 2184020220167401736, 2506024680231802380, 2766026400257202532, 2982028560279402706,
-    3282031760302802966, 3436033100324403216, 3824036260363203482, 4342041480408403826, 5042047920472804398, 5114)
-REDUCE = (1168011060104200774, 1550016140161501356, 1865018020167701551, 2354021850225101931, 2759026740256702416,
-    2990029910286002885, 3626035670336903309, 3817037170362703649, 4197040750400603877, 5377050950505904135, 6307063050624105507,
-    6499)
-GATHER_RIGHT = (33333333, 22554322, 54555, 322)
-GATHER_LEFT = (44444444, 55223455, 1223222, 1234455)
-REDUCE_RIGHT = (44444444, 33333333, 1233444, 1234333)
-REDUCE_LEFT = (33333333, 44444444, 4333, 444)
+ORDER = (56817243, 87136254)
+GATHER = (774003240013200070, 2120018280154401482, 2186022520206002126, 2472023200238602278, 2646025740253202512,
+    2792027260279402580, 3114030540290602732, 3636033080324803096, 4146040820395203630, 4858043420434004152, 4856)
+REDUCE = (720006580065600262, 1165011640110000974, 1423014830135701294, 1931018650180201545, 2354024180241602119,
+    2695026040250102309, 3311031190305302862, 3689035210349803369, 3947038770358703627, 4839041350419704006, 6433059850582705121,
+    649906435)
+GATHER_RIGHT = (54555555, 22554322, 22, 322)
+GATHER_LEFT = (23222222, 55223455, 1234555, 1234455)
+REDUCE_RIGHT = (43333443, 33333333, 1234444, 1234333)
+REDUCE_LEFT = (34444334, 44444444, 333, 444)
 PREP_TOKENS = 32
 
 
@@ -50,7 +50,7 @@
 G_SEQ, R_SEQ = unpacked(GATHER), unpacked(REDUCE)
 GATHER_AT, GATHER_CODE = [n >> 7 for n in G_SEQ], [n & 127 for n in G_SEQ]
 REDUCE_AT, REDUCE_CODE = [n >> 7 for n in R_SEQ], [n & 127 for n in R_SEQ]
-MAX_HOP = max(map(max, GATHER_REACH + REDUCE_REACH))
+GATHER_HOPS, REDUCE_HOPS = max(map(max, GATHER_REACH)), max(map(max, REDUCE_REACH))
 SLOTS = [[4 * int(d) + j for d in str(order) for j in range(3 if d == '4' else 2)] for order in ORDER]
 
 
@@ -618,7 +618,7 @@
             scr((2, 2) + k_rows.shape, BF16), scr((2,) + lse.shape, F32), scr((2, 2 * tok, 1, hd), F32),
             *[scr((2 * tok, 1, hd), F32)] * 2, *[scr((2 * tok, hd), F32)] * 2,
             scr((2, 2, 2, tok, hd), BF16), *[scr((8, hd), F32)] * 2, scr((2 * nz, 8, hd), F32),
-            *[dma((3,))] * 3, *[dma((2, 2, 3))] * 3, dma((4,)), *[dma((2, 2, MAX_HOP, 2))] * 2, *[dma((2, MAX_HOP, 2, 2))] * 2,
+            *[dma((3,))] * 3, *[dma((2, 2, 3))] * 3, dma((4,)), *[dma((2, 2, GATHER_HOPS, 2))] * 2, *[dma((2, REDUCE_HOPS, 2, 2))] * 2,
             *[dma((2, 2))] * 6, *[dma((2 * nz,))] * 2,
         ],
         name='attn_bwd',

time: 141 us -> 141 us (level)
  no operation moved by 1% of the time
where the time goes in v8:
time: 141 us; the launch traced here: 140 us
  Pallas kernels  140 us (99%)
    pallas_call x1, Pallas kernels, mega(): pl.pallas_call(functools.partial(mega_kernel, nz, chunk, per_kv, kv_heads...  134 us
    pallas_call x1, Pallas kernels, emit(): pl.pallas_call(functools.partial(emit_kernel, n), in_specs=[any_spec, vme...  5.41 us

profile of v8, /device:TPU:21, one launch (start us, length us, event | category | flops | bytes accessed | tf_op | source)
XLA Modules:
  0.0 140.4 jit_solution(13665442582739487972)
XLA Ops:
  0.6 134.3 %attn_bwd.1 = (bf16[256,64,128]{2,1,0:T(8,128)(2,1)}, bf16[4,2,2,128,128]{4,3,2,1,0:T(8,128)(2,1)}, f32[8,128]{1,0:T(8,128)}) custom-call(bf16[256,64,128]{2,1,0:T(8,128)(2,1)} %q_hbm.1, bf16[256,64,128]{2,1,0:T(8,128)(2,1)} %do_hbm.1, bf16[256,64,128]{2,1,0:T(8,128)(2,1)} %out_hbm.1, f32[64,256]{1,0:T(8,128)} %bitcast.9, bf16[1024,128]{1,0:T(8,128)(2,1)} %bitcast.7, ...), custom_call_target="tpu_custom_call" | custom-call | tf_op jit(solution)/shard_map/attn_bwd/pallas_call | solution.py:609
  134.9 5.4 %emit.1 = (bf16[256,64,128]{2,1,0:T(8,128)(2,1)}, bf16[256,4,128]{2,1,0:T(4,128)(2,1)}, bf16[256,4,128]{2,1,0:T(4,128)(2,1)}, f32[1,128]{1,0:T(1,128)}, f32[1,128]{1,0:T(1,128)}) custom-call(bf16[256,64,128]{2,1,0:T(8,128)(2,1)} %get-tuple-element.13.dq_in, bf16[4,2,2,128,128]{4,3,2,1,0:T(8,128)(2,1)} %get-tuple-element.14.dkv_in, ...), custom_call_target="tpu_custom_call" | custom-call | tf_op jit(solution)/shard_map/emit/pallas_call | solution.py:654
